TPU v7x, 256 devices: a whole 4x4x8 slice. The times are simulated.
256 devices in a mesh: row: 8 (over y, core), col: 4 (over x), layer: 8 (over z).
Axes of the slice: x: 4, y: 4, z: 8, core: 2. Of those that a mesh axis runs over, the one named last changes fastest.
Arguments:
- hamiltonian: bfloat16 [5120, 5120], P(('row', 'layer'), 'col'), may hold values from -1.2 to 1.2, as said below
- tile_pattern: int32 [40, 40], replicated, may hold values from 0 to 1, as said below
- n_occ: int32 [1], replicated, may hold values from 1024 to 4095
- mu: float32 [1], replicated, may hold values from -0.2 to 0.2
- gamma: float32 [1], replicated, may hold values from 0.25 to 0.4
Outputs:
- density: float32 [5120, 5120], P(('row', 'layer'), 'col')
Inputs may be any that keep to these rules, and one draw needn't show every extreme that they name: `tile_pattern`: Symmetric, 0 or 1, with ones on the diagonal and next to it. `hamiltonian`: Symmetric; its eigenvalues lie within -1.8 and 1.8.
All inputs are finite; a program needn't handle non-finite values.
Results may differ from a plain program's by a relative error of at most 0.0055.
Values may be sent and summed in bfloat16 or wider, within the bound.
No kernel may reach another device: no remote copies, remote signals or barrier semaphores. Data moves between devices by JAX's collectives and lax.ppermute only.
A program may use at most 64 MiB of HBM per device.

v0:
```python
import functools
import math

import jax
import jax.numpy as jnp
from jax import lax
from jax.experimental import pallas as pl
from jax.experimental.pallas import tpu as pltpu
from jax.sharding import PartitionSpec as P

TILE = 128
STEPS = 2
SUB = 16

SHARE = 80
ROWS = 2 * SHARE
NY, NX, NZ = 4, 4, 8
ROW_BLOCK = SHARE * NZ
BAND_TILES = 10
HALF_TILES = BAND_TILES // 2
WIDTH = HALF_TILES * TILE
TILES = 40
ORDER = TILES * TILE
NSUB = SHARE // SUB
ALL_SLOTS = NY * 2 * NSUB * HALF_TILES
Z_ORDER = (0, -1, 1, -2, 2, -3, 3, 4)
SLOTS = 256
UNROLL = 8
CAPACITY = 96
SPLIT = 48
EXTRA = 16
ROUNDS = -(-(ALL_SLOTS - CAPACITY) // EXTRA)
DEPTH = 4 * TILE

SMEM = pl.BlockSpec(memory_space=pltpu.SMEM)
VMEM = pl.BlockSpec(memory_space=pltpu.VMEM)
ANY = pl.BlockSpec(memory_space=pl.ANY)
PARAMS = pltpu.CompilerParams(vmem_limit_bytes=14 * 1024 * 1024)


def row_of(y, half, z, sub):
    return (2 * y + half) * ROW_BLOCK + SHARE * z + SUB * sub


def col_tile(x, core, t):
    return BAND_TILES * x + 2 * t + core


def where_am_i(pos):
    return pos[0], pos[1], pos[2], pos[3]


def split_kernel(pos, whole, keep, send):
    y, core, x, z = where_am_i(pos)
    for t in range(HALF_TILES):
        at = slice(t * TILE, (t + 1) * TILE)
        mine = pl.multiple_of((2 * t + core) * TILE, TILE)
        other = pl.multiple_of((2 * t + 1 - core) * TILE, TILE)
        keep[:, at] = whole[:, pl.ds(mine, TILE)]
        send[:, at] = whole[:, pl.ds(other, TILE)]


def merge_kernel(pos, result, theirs, whole):
    y, core, x, z = where_am_i(pos)
    rows = pl.ds(pl.multiple_of(core * SHARE, SHARE), SHARE)
    for t in range(HALF_TILES):
        at = slice(t * TILE, (t + 1) * TILE)
        mine = pl.multiple_of((2 * t + core) * TILE, TILE)
        other = pl.multiple_of((2 * t + 1 - core) * TILE, TILE)
        whole[:, pl.ds(mine, TILE)] = result[rows, at]
        whole[:, pl.ds(other, TILE)] = theirs[:, at]


def start_kernel(pos, pat, n_occ, mu, gamma, keep, recv, out):
    y, core, x, z = where_am_i(pos)
    filling = jnp.full((SUB, TILE), n_occ[0].astype(jnp.float32)) / ORDER
    apart = lax.broadcasted_iota(jnp.int32, (SUB, TILE), 1) - lax.broadcasted_iota(
        jnp.int32, (SUB, TILE), 0
    )
    for side, ref in ((0, keep), (1, recv)):
        half = core if side == 0 else 1 - core

        def strip(s, _):
            g = row_of(y, half, z, s)
            i = g // TILE
            near = apart == g % TILE
            frm = pl.multiple_of(s * SUB, SUB)
            to = pl.multiple_of(half * SHARE + s * SUB, SUB)
            for t in range(HALF_TILES):
                j = col_tile(x, core, t)
                cols = slice(t * TILE, (t + 1) * TILE)
                identity = jnp.where(near, (i == j).astype(jnp.float32), 0.0)
                h = ref[pl.ds(frm, SUB), cols].astype(jnp.float32)
                value = filling * identity + gamma[0] * (mu[0] * identity - h)
                value = value * pat[i, j].astype(jnp.float32)
                out[pl.ds(to, SUB), cols] = value.astype(jnp.bfloat16)
            return 0

        lax.fori_loop(0, NSUB, strip, 0)


def table_kernel(pos, pat, table, most):
    y, core, x, z = where_am_i(pos)
    f32 = jnp.float32
    pattern = pat[...].astype(f32)
    n = NY * 2 * NSUB

    def iota(shape, dim):
        return lax.broadcasted_iota(jnp.int32, shape, dim)

    rows = iota((NZ * n, TILES), 0)
    rz, rn = rows // n, rows % n
    rk = (row_of(rn // (2 * NSUB), rn // NSUB % 2, rz, rn % NSUB)) // TILE
    picked = jnp.dot((rk == iota((NZ * n, TILES), 1)).astype(f32), pattern)
    total = jnp.dot(
        (iota((NZ, NZ * n), 0) == iota((NZ, NZ * n), 1) // n).astype(f32), picked
    )
    k, group = iota((TILES, 2 * NX), 0), iota((TILES, 2 * NX), 1)
    group = ((k // BAND_TILES) * 2 + k % 2 == group).astype(f32)
    most[0] = jnp.max(jnp.dot(total, group)).astype(jnp.int32)

    cols = (iota((TILES, TILE), 0) == col_tile(x, core, iota((TILES, TILE), 1))) & (
        iota((TILES, TILE), 1) < HALF_TILES
    )
    mine = jnp.dot(pattern, cols.astype(f32))
    before = (iota((TILE, TILE), 0) < iota((TILE, TILE), 1)).astype(f32)
    below = (iota((n, n), 1) < iota((n, n), 0)).astype(f32)
    slots = iota((n, SLOTS), 1)
    for m, rel in enumerate(Z_ORDER):
        zz = (z + rel) % NZ

        def first_row(shape, dim):
            r = iota(shape, dim)
            return row_of((y + r // (2 * NSUB)) % NY, r // NSUB % 2, zz, r % NSUB)

        pick = (first_row((n, TILES), 0) // TILE == iota((n, TILES), 1)).astype(f32)
        p = jnp.dot(pick, mine)
        count = jnp.sum(p, axis=1, keepdims=True)
        ahead = jnp.sum(below * jnp.reshape(jnp.dot(pick, mine).sum(axis=1), (1, n)), axis=1, keepdims=True)
        slot = (ahead + jnp.dot(p, before)).astype(jnp.int32)
        g = first_row((n, 1), 0)
        kk = g // TILE
        kx, kt = kk // BAND_TILES, kk % BAND_TILES
        place = ((kt + core) % 2 * NX + (kx + NX - x) % NX) * HALF_TILES + kt // 2
        to = (place * TILE + g % TILE) * 8
        r = iota((n, 1), 0)
        frm = (r // NSUB * SHARE + r % NSUB * SUB) * 8
        codes = jnp.zeros((n, SLOTS), jnp.int32)
        sources = jnp.zeros((n, SLOTS), jnp.int32)
        for t in range(HALF_TILES):
            here = (slots == slot[:, t : t + 1]) & (p[:, t : t + 1] > 0)
            codes += jnp.where(here, to + t, 0)
            if m == 0:
                sources += jnp.where(here, frm + t, 0)
        number = jnp.sum(count).astype(jnp.int32)
        at = iota((1, SLOTS), 1)
        line = jnp.sum(codes, axis=0, keepdims=True)
        line = jnp.where(at < number, line, ORDER * 8)
        table[m : m + 1, :] = jnp.where(at == SLOTS - 1, number, line)
        if m == 0:
            table[NZ : NZ + 1, :] = jnp.sum(sources, axis=0, keepdims=True)


def pack_kernel(count, base, table, own, one, two, three, out, block):
    for d, ref in enumerate((own, one, two, three)):
        block[d * ROWS : (d + 1) * ROWS, :] = ref[...]

    def some(i, _):
        for u in range(UNROLL):
            slot = i * UNROLL + u
            code = table[NZ, base[0] + slot]
            row = pl.multiple_of(code // 8, SUB)
            col = pl.multiple_of(code % 8 * TILE, TILE)
            to = pl.multiple_of(slot * SUB, SUB)
            out[pl.ds(to, SUB), :] = block[pl.ds(row, SUB), pl.ds(col, TILE)]
        return 0

    lax.fori_loop(0, count // UNROLL, some, 0)


def place(table, m, source, panel, first, last):
    def some(i, _):
        for u in range(UNROLL):
            slot = first + i * UNROLL + u
            code = table[m, slot]
            row = pl.multiple_of(code // 8, SUB)
            col = pl.multiple_of(code % 8 * TILE, TILE)
            frm = pl.multiple_of((i * UNROLL + u) * SUB, SUB)
            panel[pl.ds(row, SUB), pl.ds(col, TILE)] = source[pl.ds(frm, SUB), :]
        return 0

    number = jnp.clip(table[m, SLOTS - 1] - first, 0, last - first)
    lax.fori_loop(0, (number + UNROLL - 1) // UNROLL, some, 0)


def product(left, panel, rows, total):
    for m, ref in enumerate(left):
        for t in range(HALF_TILES):
            at = (m * HALF_TILES + t) * TILE
            rows[at // DEPTH, :, at % DEPTH : at % DEPTH + TILE] = ref[:, t * TILE : (t + 1) * TILE]
    total[...] = jnp.zeros_like(total)

    def some(m, _):
        at = pl.multiple_of(m * DEPTH, DEPTH)
        total[...] += jnp.dot(
            rows[m], panel[pl.ds(at, DEPTH), :], preferred_element_type=jnp.float32
        )
        return 0

    lax.fori_loop(0, ORDER // DEPTH, some, 0)


def each_tile(pos, pat, use):
    y, core, x, z = where_am_i(pos)

    def strip(q, _):
        i = row_of(y, q // NSUB, z, q % NSUB) // TILE
        at = pl.multiple_of(q // NSUB * SHARE + q % NSUB * SUB, SUB)
        for t in range(HALF_TILES):
            where = (pl.ds(at, SUB), slice(t * TILE, (t + 1) * TILE))
            use(where, pat[i, col_tile(x, core, t)].astype(jnp.float32))
        return 0

    lax.fori_loop(0, 2 * NSUB, strip, 0)


def square_kernel(pos, pat, table, *refs):
    packed, left, spill = refs[:9], refs[9:17], refs[17]
    (square, square_half, panel), (rows, total, more) = refs[18:21], refs[21:]
    panel[...] = jnp.zeros_like(panel)
    for m in range(NZ - 1):
        place(table, m, packed[m], panel, 0, CAPACITY)
    place(table, NZ - 1, packed[NZ - 1], panel, 0, SPLIT)
    place(table, NZ - 1, packed[NZ], panel, SPLIT, CAPACITY)
    for m in range(NZ):

        @pl.when(table[m, SLOTS - 1] > CAPACITY)
        def _():
            pltpu.sync_copy(spill.at[m], more)
            place(table, m, more, panel, CAPACITY, CAPACITY + ROUNDS * EXTRA)

    product(left, panel, rows, total)

    def use(where, mask):
        value = total[where] * mask
        square[where] = value
        square_half[where] = value.astype(jnp.bfloat16)

    each_tile(pos, pat, use)


def cube_kernel(pos, pat, square, panel, *refs):
    left, (out, out_half), (rows, total) = refs[:8], refs[8:10], refs[10:]
    product(left, panel, rows, total)

    def use(where, mask):
        value = 3.0 * square[where] - 2.0 * (total[where] * mask)
        out[where] = value
        out_half[where] = value.astype(jnp.bfloat16)

    each_tile(pos, pat, use)


def ring(axis, shift, size, stride=1):
    return [(i, (i + shift * stride) % size) for i in range(size)]


def along_x(value, shift):
    return lax.ppermute(value, "col", ring("col", shift, NX))


def along_y(value, shift):
    return lax.ppermute(value, "row", ring("row", shift, 2 * NY, 2))


def along_z(value, shift):
    return lax.ppermute(value, "layer", ring("layer", shift, NZ))


def other_core(value):
    return lax.ppermute(value, "row", [(i, i ^ 1) for i in range(2 * NY)])


def whole_rows(half_rows):
    pieces = [half_rows, along_x(half_rows, -1), along_x(half_rows, 2), along_x(half_rows, 1)]
    return pieces + [other_core(piece) for piece in pieces]


def call(kernel, outs, n_smem, *args, scratch=(), n_any=0, flops=0):
    single = not isinstance(outs, (tuple, list))
    arrays = [*args, outs] if single else [*args, *outs]
    touched = sum(math.prod(a.shape) * jnp.dtype(a.dtype).itemsize for a in arrays)
    return pl.pallas_call(
        kernel,
        out_shape=outs,
        in_specs=[SMEM] * n_smem + [VMEM] * (len(args) - n_smem - n_any) + [ANY] * n_any,
        out_specs=VMEM if single else [VMEM] * len(outs),
        scratch_shapes=scratch,
        compiler_params=PARAMS,
        cost_estimate=pl.CostEstimate(flops=flops, bytes_accessed=touched, transcendentals=0),
    )(*args)


def pack(count, base, table, blocks):
    return call(
        functools.partial(pack_kernel, count),
        jax.ShapeDtypeStruct((count * SUB, TILE), jnp.bfloat16),
        2,
        *(jnp.asarray(base, jnp.int32).reshape(1), table, *blocks),
        scratch=(pltpu.VMEM((NY * ROWS, WIDTH), jnp.bfloat16),),
    )


def nothing_kernel(out):
    pass


def spilled(most, table, blocks):
    rounds = (most[0] - CAPACITY + EXTRA - 1) // EXTRA
    shape = (NZ, ROUNDS * EXTRA * SUB, TILE)
    empty = pl.pallas_call(
        nothing_kernel, out_shape=jax.ShapeDtypeStruct(shape, jnp.bfloat16), out_specs=ANY
    )()

    def one_round(carry):
        turn, spill = carry
        mine = pack(EXTRA, CAPACITY + turn * EXTRA, table, blocks)
        got = [mine] + [along_z(mine, -rel) for rel in Z_ORDER[1:]]
        at = (0, turn * EXTRA * SUB, 0)
        return turn + 1, lax.dynamic_update_slice(spill, jnp.stack(got), at)

    return lax.while_loop(lambda carry: carry[0] < rounds, one_round, (jnp.int32(0), empty))[1]


def steps(pos, pat, current, table, most):
    f32 = jax.ShapeDtypeStruct((ROWS, WIDTH), jnp.float32)
    bf16 = jax.ShapeDtypeStruct((ROWS, WIDTH), jnp.bfloat16)
    panel_shape = jax.ShapeDtypeStruct((ORDER + SUB, WIDTH), jnp.bfloat16)
    work = (
        pltpu.VMEM((ORDER // DEPTH, ROWS, DEPTH), jnp.bfloat16),
        pltpu.VMEM((ROWS, WIDTH), jnp.float32),
    )
    more = (pltpu.VMEM((ROUNDS * EXTRA * SUB, TILE), jnp.bfloat16),)
    split = SPLIT * SUB

    def step(carry):
        turn, current = carry[:2]
        blocks = (current, along_y(current, -1), along_y(current, 2), along_y(current, 1))
        packed = pack(CAPACITY, 0, table, blocks)
        turn, current, packed = lax.optimization_barrier((turn + 1, current, packed))
        down, up = along_z(packed, 1), along_z(packed, -1)
        down2, up2 = along_z(down, 1), along_z(up, -1)
        down3, up3 = along_z(down2, 1), along_z(up2, -1)
        far_a, far_b = along_z(down3[:split], 1), along_z(up3[split:], -1)
        left = whole_rows(current)
        spill = spilled(most, table, blocks)
        square, square_half, panel = call(
            square_kernel,
            (f32, bf16, panel_shape),
            3,
            *(pos, pat, table, packed, down, up, down2, up2, down3, up3, far_a, far_b),
            *left,
            spill,
            scratch=work + more,
            n_any=1,
            flops=10**9,
        )
        left = whole_rows(square_half)
        result, following = call(
            cube_kernel, (f32, bf16), 2, pos, pat, square, panel, *left, scratch=work, flops=10**9
        )
        return turn, following, result

    first = (jnp.int32(0), current, jnp.zeros((ROWS, WIDTH), jnp.float32))
    return lax.while_loop(lambda carry: carry[0] < STEPS, step, first)[2]


def shards(hamiltonian, tile_pattern, n_occ, mu, gamma):
    row, x, z = lax.axis_index("row"), lax.axis_index("col"), lax.axis_index("layer")
    y, core = row // 2, row % 2
    pos = jnp.stack([y, core, x, z]).astype(jnp.int32)
    share = jax.ShapeDtypeStruct((SHARE, WIDTH), jnp.bfloat16)
    keep, send = call(split_kernel, (share, share), 1, pos, hamiltonian)
    recv = other_core(send)
    bf16 = jax.ShapeDtypeStruct((ROWS, WIDTH), jnp.bfloat16)
    current = call(start_kernel, bf16, 5, pos, tile_pattern, n_occ, mu, gamma, keep, recv)
    table, most = pl.pallas_call(
        table_kernel,
        out_shape=(
            jax.ShapeDtypeStruct((NZ + 1, SLOTS), jnp.int32),
            jax.ShapeDtypeStruct((1,), jnp.int32),
        ),
        in_specs=[SMEM, VMEM],
        out_specs=[VMEM, SMEM],
        compiler_params=PARAMS,
    )(pos, tile_pattern)
    result = steps(pos, tile_pattern, current, table, most)
    theirs = other_core(jnp.where(core == 0, result[SHARE:], result[:SHARE]))
    whole = jax.ShapeDtypeStruct((SHARE, 2 * WIDTH), jnp.float32)
    return call(merge_kernel, whole, 1, pos, result, theirs)


def solution(mesh):
    placed = (P(("row", "layer"), "col"), P(), P(), P(), P())
    return jax.shard_map(
        shards, mesh=mesh, in_specs=placed, out_specs=P(("row", "layer"), "col"), check_vma=False
    )
```

profile of v0, /device:TPU:1, one launch (start us, length us, event | category | flops | bytes accessed | tf_op | source)
XLA Modules:
  0.0 200.0 jit_solution(4515429672307967259)
XLA Ops:
  1.6 3.3 %collective-permute-start.32 = (bf16[80,640]{1,0:T(8,128)(2,1)S(1)}, bf16[80,640]{1,0:T(8,128)(2,1)S(1)}, u32[]{:S(2)}, u32[]{:S(2)}) collective-permute-start(bf16[80,640]{1,0:T(8,128)(2,1)S(1)} %get-tuple-element.316), channel_id=1, source_target_pairs={{0,32},{32,0},{64,96},{96,64},{128,160},{160,128},{192,224},{224,1... | collective-permute-start | bytes 307208 | tf_op jit(solution)/shard_map/ppermute | solution.py:281
  4.9 3.1 %shard_map.57 = (s32[9,256]{1,0:T(8,128)S(1)}, s32[1]{0:T(128)}) custom-call(s32[4]{0:T(128)S(1)} %pad_add_fusion.pos, s32[40,40]{1,0:T(8,128)} %pat.3), custom_call_target="tpu_custom_call" | custom-call | tf_op jit(solution)/shard_map/pallas_call | solution.py:387
  12.8 182.8 %while.33 = (s32[]{:T(128)}, bf16[160,640]{1,0:T(8,128)(2,1)S(1)}, f32[160,640]{1,0:T(8,128)}, s32[9,256]{1,0:T(8,128)S(1)}, s32[]{:T(128)}, /*index=5*/s32[4]{0...) while((s32[]{:T(128)}, bf16[160,640]{1,0:T(8,128)(2,1)S(1)}, ...), condition=%wide.region_3.4_spmd, body=%wide.region_0.3_spmd.sunk | while | flops 2000000000 | bytes 56699176 | solution.py:375
  16.1 5.0 %collective-permute-done.9.three = bf16[160,640]{1,0:T(8,128)(2,1)S(1)} collective-permute-done((bf16[160,640]{1,0:T(8,128)(2,1)S(1)}, bf16[160,640]{1,0:T(8,128)(2,1)S(1)}, u32[]{:S(2)}, u32[]{:S(2)}) %collective-permute-start.9) | collective-permute-done | bytes 204832 | tf_op jit(solution)/shard_map/while/body/ppermute | solution.py:273
  21.1 3.5 %collective-permute-done.8.two = bf16[160,640]{1,0:T(8,128)(2,1)S(1)} collective-permute-done((bf16[160,640]{1,0:T(8,128)(2,1)S(1)}, bf16[160,640]{1,0:T(8,128)(2,1)S(1)}, u32[]{:S(2)}, u32[]{:S(2)}) %collective-permute-start.8) | collective-permute-done | bytes 204832 | tf_op jit(solution)/shard_map/while/body/ppermute | solution.py:273
  27.2 4.8 %collective-permute-start.11 = (bf16[1536,128]{1,0:T(8,128)(2,1)S(1)}, bf16[1536,128]{1,0:T(8,128)(2,1)S(1)}, u32[]{:S(2)}, u32[]{:S(2)}) collective-permute-start(bf16[1536,128]{1,0:T(8,128)(2,1)S(1)} %body.24.refs_0_), channel_id=1, source_target_pairs={{0,7},{1,0},{2,1},{3,2},{4,3},{5,4},{6,5},{7,6},{8,15},{9,8},{10,9... | collective-permute-start | bytes 1179656 | tf_op jit(solution)/shard_map/while/body/ppermute | solution.py:277
  32.1 7.6 %collective-permute-done.11.refs_2_ = bf16[1536,128]{1,0:T(8,128)(2,1)S(1)} collective-permute-done((bf16[1536,128]{1,0:T(8,128)(2,1)S(1)}, bf16[1536,128]{1,0:T(8,128)(2,1)S(1)}, u32[]{:S(2)}, u32[]{:S(2)}) %collective-permute-start.11) | collective-permute-done | bytes 393248 | tf_op jit(solution)/shard_map/while/body/ppermute | solution.py:277
  39.7 3.4 %collective-permute-start.13 = (bf16[1536,128]{1,0:T(8,128)(2,1)S(1)}, bf16[1536,128]{1,0:T(8,128)(2,1)S(1)}, u32[]{:S(2)}, u32[]{:S(2)}) collective-permute-start(bf16[1536,128]{1,0:T(8,128)(2,1)S(1)} %collective-permute-done.11.refs_2_), channel_id=1, source_target_pairs={{0,7},{1,0},{2,1},{3,2},{4,3},{5,4},{6,5},{7,6},{8,15},{9,8},{10,9... | collective-permute-start | bytes 1179656 | tf_op jit(solution)/shard_map/while/body/ppermute | solution.py:277
  44.3 5.5 %collective-permute-done.13.refs_4_ = bf16[1536,128]{1,0:T(8,128)(2,1)S(1)} collective-permute-done((bf16[1536,128]{1,0:T(8,128)(2,1)S(1)}, bf16[1536,128]{1,0:T(8,128)(2,1)S(1)}, u32[]{:S(2)}, u32[]{:S(2)}) %collective-permute-start.13) | collective-permute-done | bytes 393248 | tf_op jit(solution)/shard_map/while/body/ppermute | solution.py:277
  49.8 3.4 %collective-permute-start.15 = (bf16[1536,128]{1,0:T(8,128)(2,1)S(1)}, bf16[1536,128]{1,0:T(8,128)(2,1)S(1)}, u32[]{:S(2)}, u32[]{:S(2)}) collective-permute-start(bf16[1536,128]{1,0:T(8,128)(2,1)S(1)} %collective-permute-done.13.refs_4_), channel_id=1, source_target_pairs={{0,7},{1,0},{2,1},{3,2},{4,3},{5,4},{6,5},{7,6},{8,15},{9,8},{10,9... | collective-permute-start | bytes 1179656 | tf_op jit(solution)/shard_map/while/body/ppermute | solution.py:277
  56.9 3.4 %collective-permute-start.21 = (bf16[160,640]{1,0:T(8,128)(2,1)S(1)}, bf16[160,640]{1,0:T(8,128)(2,1)S(1)}, u32[]{:S(2)}, u32[]{:S(2)}) collective-permute-start(bf16[160,640]{1,0:T(8,128)(2,1)S(1)} %get-tuple-element.617), channel_id=1, source_target_pairs={{0,32},{32,0},{64,96},{96,64},{128,160},{160,128},{192,224},{224,1... | collective-permute-start | bytes 614408 | tf_op jit(solution)/shard_map/while/body/ppermute | solution.py:281
  60.3 3.1 %collective-permute-start.24 = (bf16[160,640]{1,0:T(8,128)(2,1)S(1)}, bf16[160,640]{1,0:T(8,128)(2,1)S(1)}, u32[]{:S(2)}, u32[]{:S(2)}) collective-permute-start(bf16[160,640]{1,0:T(8,128)(2,1)S(1)} %collective-permute-done.20.refs_12_), channel_id=1, source_target_pairs={{0,32},{32,0},{64,96},{96,64},{128,160},{160,128},{192,224},{224,1... | collective-permute-start | bytes 614408 | tf_op jit(solution)/shard_map/while/body/ppermute | solution.py:281
  63.5 3.2 %collective-permute-start.23 = (bf16[160,640]{1,0:T(8,128)(2,1)S(1)}, bf16[160,640]{1,0:T(8,128)(2,1)S(1)}, u32[]{:S(2)}, u32[]{:S(2)}) collective-permute-start(bf16[160,640]{1,0:T(8,128)(2,1)S(1)} %collective-permute-done.19.refs_11_), channel_id=1, source_target_pairs={{0,32},{32,0},{64,96},{96,64},{128,160},{160,128},{192,224},{224,1... | collective-permute-start | bytes 614408 | tf_op jit(solution)/shard_map/while/body/ppermute | solution.py:281
  66.8 2.8 %collective-permute-start.17 = (bf16[768,128]{1,0:T(8,128)(2,1)S(1)}, bf16[768,128]{1,0:T(8,128)(2,1)S(1)}, u32[]{:S(2)}, u32[]{:S(2)}) collective-permute-start(bf16[768,128]{1,0:T(8,128)(2,1)S(1)} %slice.29), channel_id=1, source_target_pairs={{0,7},{1,0},{2,1},{3,2},{4,3},{5,4},{6,5},{7,6},{8,15},{9,8},{10,9... | collective-permute-start | bytes 589832 | tf_op jit(solution)/shard_map/while/body/ppermute | solution.py:277
  69.6 3.7 %collective-permute-done.17.refs_8_ = bf16[768,128]{1,0:T(8,128)(2,1)S(1)} collective-permute-done((bf16[768,128]{1,0:T(8,128)(2,1)S(1)}, bf16[768,128]{1,0:T(8,128)(2,1)S(1)}, u32[]{:S(2)}, u32[]{:S(2)}) %collective-permute-start.17) | collective-permute-done | bytes 196640 | tf_op jit(solution)/shard_map/while/body/ppermute | solution.py:277
  73.3 3.1 %collective-permute-done.16.refs_7_ = bf16[768,128]{1,0:T(8,128)(2,1)S(1)} collective-permute-done((bf16[768,128]{1,0:T(8,128)(2,1)S(1)}, bf16[768,128]{1,0:T(8,128)(2,1)S(1)}, u32[]{:S(2)}, u32[]{:S(2)}) %collective-permute-start.16) | collective-permute-done | bytes 196640 | tf_op jit(solution)/shard_map/while/body/ppermute | solution.py:277
  76.5 8.6 %body.26 = (f32[160,640]{1,0:T(8,128)S(1)}, bf16[160,640]{1,0:T(8,128)(2,1)S(1)}, bf16[5136,640]{1,0:T(8,128)(2,1)S(1)}) custom-call(s32[4]{0:T(128)S(1)} %get-tuple-element.555.pos, s32[40,40]{1,0:T(8,128)S(1)} %copy-done.1, s32[9,256]{1,0:T(8,128)S(1)} %get-tuple-element.632, bf16[1536,128]{1,0:T(8,128)(2,1)S(1)} %body.24.refs_0_, ...), custom_call_target="tpu_custom_call" | custom-call | flops 1000000000 | bytes 15658256 | tf_op jit(solution)/shard_map/while/body/pallas_call | solution.py:293
  86.9 2.9 %collective-permute-start.26 = (bf16[160,640]{1,0:T(8,128)(2,1)S(1)}, bf16[160,640]{1,0:T(8,128)(2,1)S(1)}, u32[]{:S(2)}, u32[]{:S(2)}) collective-permute-start(bf16[160,640]{1,0:T(8,128)(2,1)S(1)} %get-tuple-element.464.refs_0_), channel_id=1, source_target_pairs={{0,16},{8,24},{16,0},{24,8},{1,17},{9,25},{17,1},{25,9},{2,18},{10... | collective-permute-start | bytes 614408 | tf_op jit(solution)/shard_map/while/body/ppermute | solution.py:269
  92.6 3.0 %collective-permute-start.31 = (bf16[160,640]{1,0:T(8,128)(2,1)S(1)}, bf16[160,640]{1,0:T(8,128)(2,1)S(1)}, u32[]{:S(2)}, u32[]{:S(2)}) collective-permute-start(bf16[160,640]{1,0:T(8,128)(2,1)S(1)} %collective-permute-done.27.refs_3_), channel_id=1, source_target_pairs={{0,32},{32,0},{64,96},{96,64},{128,160},{160,128},{192,224},{224,1... | collective-permute-start | bytes 614408 | tf_op jit(solution)/shard_map/while/body/ppermute | solution.py:281
  101.7 5.2 %body.27 = (f32[160,640]{1,0:T(8,128)}, bf16[160,640]{1,0:T(8,128)(2,1)S(1)}) custom-call(s32[4]{0:T(128)S(1)} %get-tuple-element.555.pos, s32[40,40]{1,0:T(8,128)S(1)} %copy-done.1, f32[160,640]{1,0:T(8,128)S(1)} %get-tuple-element.462.square, bf16[5136,640]{1,0:T(8,128)(2,1)S(1)} %get-tuple-element.463.panel, ...), custom_call_target="tpu_custom_call" | custom-call | flops 1000000000 | bytes 9242896 | tf_op jit(solution)/shard_map/while/body/pallas_call | solution.py:293
  106.9 4.1 %collective-permute-start.8 = (bf16[160,640]{1,0:T(8,128)(2,1)S(1)}, bf16[160,640]{1,0:T(8,128)(2,1)S(1)}, u32[]{:S(2)}, u32[]{:S(2)}) collective-permute-start(bf16[160,640]{1,0:T(8,128)(2,1)S(1)} %get-tuple-element.460.own.refs_9_), channel_id=1, source_target_pairs={{0,128},{32,160},{64,192},{96,224},{128,0},{160,32},{192,64},{224,... | collective-permute-start | bytes 614408 | tf_op jit(solution)/shard_map/while/body/ppermute | solution.py:273
  111.0 4.0 %collective-permute-done.9.three = bf16[160,640]{1,0:T(8,128)(2,1)S(1)} collective-permute-done((bf16[160,640]{1,0:T(8,128)(2,1)S(1)}, bf16[160,640]{1,0:T(8,128)(2,1)S(1)}, u32[]{:S(2)}, u32[]{:S(2)}) %collective-permute-start.9) | collective-permute-done | bytes 204832 | tf_op jit(solution)/shard_map/while/body/ppermute | solution.py:273
  115.0 5.3 %collective-permute-done.8.two = bf16[160,640]{1,0:T(8,128)(2,1)S(1)} collective-permute-done((bf16[160,640]{1,0:T(8,128)(2,1)S(1)}, bf16[160,640]{1,0:T(8,128)(2,1)S(1)}, u32[]{:S(2)}, u32[]{:S(2)}) %collective-permute-start.8) | collective-permute-done | bytes 204832 | tf_op jit(solution)/shard_map/while/body/ppermute | solution.py:273
  123.8 8.1 %collective-permute-done.11.refs_2_ = bf16[1536,128]{1,0:T(8,128)(2,1)S(1)} collective-permute-done((bf16[1536,128]{1,0:T(8,128)(2,1)S(1)}, bf16[1536,128]{1,0:T(8,128)(2,1)S(1)}, u32[]{:S(2)}, u32[]{:S(2)}) %collective-permute-start.11) | collective-permute-done | bytes 393248 | tf_op jit(solution)/shard_map/while/body/ppermute | solution.py:277
  133.7 6.7 %collective-permute-done.13.refs_4_ = bf16[1536,128]{1,0:T(8,128)(2,1)S(1)} collective-permute-done((bf16[1536,128]{1,0:T(8,128)(2,1)S(1)}, bf16[1536,128]{1,0:T(8,128)(2,1)S(1)}, u32[]{:S(2)}, u32[]{:S(2)}) %collective-permute-start.13) | collective-permute-done | bytes 393248 | tf_op jit(solution)/shard_map/while/body/ppermute | solution.py:277
  145.9 3.8 %collective-permute-start.21 = (bf16[160,640]{1,0:T(8,128)(2,1)S(1)}, bf16[160,640]{1,0:T(8,128)(2,1)S(1)}, u32[]{:S(2)}, u32[]{:S(2)}) collective-permute-start(bf16[160,640]{1,0:T(8,128)(2,1)S(1)} %get-tuple-element.617), channel_id=1, source_target_pairs={{0,32},{32,0},{64,96},{96,64},{128,160},{160,128},{192,224},{224,1... | collective-permute-start | bytes 614408 | tf_op jit(solution)/shard_map/while/body/ppermute | solution.py:281
  149.7 3.9 %collective-permute-start.24 = (bf16[160,640]{1,0:T(8,128)(2,1)S(1)}, bf16[160,640]{1,0:T(8,128)(2,1)S(1)}, u32[]{:S(2)}, u32[]{:S(2)}) collective-permute-start(bf16[160,640]{1,0:T(8,128)(2,1)S(1)} %collective-permute-done.20.refs_12_), channel_id=1, source_target_pairs={{0,32},{32,0},{64,96},{96,64},{128,160},{160,128},{192,224},{224,1... | collective-permute-start | bytes 614408 | tf_op jit(solution)/shard_map/while/body/ppermute | solution.py:281
  158.3 3.7 %collective-permute-done.17.refs_8_ = bf16[768,128]{1,0:T(8,128)(2,1)S(1)} collective-permute-done((bf16[768,128]{1,0:T(8,128)(2,1)S(1)}, bf16[768,128]{1,0:T(8,128)(2,1)S(1)}, u32[]{:S(2)}, u32[]{:S(2)}) %collective-permute-start.17) | collective-permute-done | bytes 196640 | tf_op jit(solution)/shard_map/while/body/ppermute | solution.py:277
  162.0 3.1 %collective-permute-done.16.refs_7_ = bf16[768,128]{1,0:T(8,128)(2,1)S(1)} collective-permute-done((bf16[768,128]{1,0:T(8,128)(2,1)S(1)}, bf16[768,128]{1,0:T(8,128)(2,1)S(1)}, u32[]{:S(2)}, u32[]{:S(2)}) %collective-permute-start.16) | collective-permute-done | bytes 196640 | tf_op jit(solution)/shard_map/while/body/ppermute | solution.py:277
  165.1 8.6 %body.26 = (f32[160,640]{1,0:T(8,128)S(1)}, bf16[160,640]{1,0:T(8,128)(2,1)S(1)}, bf16[5136,640]{1,0:T(8,128)(2,1)S(1)}) custom-call(s32[4]{0:T(128)S(1)} %get-tuple-element.555.pos, s32[40,40]{1,0:T(8,128)S(1)} %copy-done.1, s32[9,256]{1,0:T(8,128)S(1)} %get-tuple-element.632, bf16[1536,128]{1,0:T(8,128)(2,1)S(1)} %body.24.refs_0_, ...), custom_call_target="tpu_custom_call" | custom-call | flops 1000000000 | bytes 15658256 | tf_op jit(solution)/shard_map/while/body/pallas_call | solution.py:293
  181.4 2.8 %collective-permute-start.31 = (bf16[160,640]{1,0:T(8,128)(2,1)S(1)}, bf16[160,640]{1,0:T(8,128)(2,1)S(1)}, u32[]{:S(2)}, u32[]{:S(2)}) collective-permute-start(bf16[160,640]{1,0:T(8,128)(2,1)S(1)} %collective-permute-done.27.refs_3_), channel_id=1, source_target_pairs={{0,32},{32,0},{64,96},{96,64},{128,160},{160,128},{192,224},{224,1... | collective-permute-start | bytes 614408 | tf_op jit(solution)/shard_map/while/body/ppermute | solution.py:281
  190.4 5.2 %body.27 = (f32[160,640]{1,0:T(8,128)}, bf16[160,640]{1,0:T(8,128)(2,1)S(1)}) custom-call(s32[4]{0:T(128)S(1)} %get-tuple-element.555.pos, s32[40,40]{1,0:T(8,128)S(1)} %copy-done.1, f32[160,640]{1,0:T(8,128)S(1)} %get-tuple-element.462.square, bf16[5136,640]{1,0:T(8,128)(2,1)S(1)} %get-tuple-element.463.panel, ...), custom_call_target="tpu_custom_call" | custom-call | flops 1000000000 | bytes 9242896 | tf_op jit(solution)/shard_map/while/body/pallas_call | solution.py:293
  (100 shorter events, 59.0 us)
Async XLA Ops:
  1.6 9.0 %collective-permute-start.32 = (bf16[80,640]{1,0:T(8,128)(2,1)S(1)}, bf16[80,640]{1,0:T(8,128)(2,1)S(1)}, u32[]{:S(2)}, u32[]{:S(2)}) collective-permute-start(bf16[80,640]{1,0:T(8,128)(2,1)S(1)} %get-tuple-element.316), channel_id=1, source_target_pairs={{0,32},{32,0},{64,96},{96,64},{128,160},{160,128},{192,224},{224,1... | collective-permute-start | bytes 307208 | tf_op jit(solution)/shard_map/ppermute | solution.py:281
  12.8 8.3 %collective-permute-start.9 = (bf16[160,640]{1,0:T(8,128)(2,1)S(1)}, bf16[160,640]{1,0:T(8,128)(2,1)S(1)}, u32[]{:S(2)}, u32[]{:S(2)}) collective-permute-start(bf16[160,640]{1,0:T(8,128)(2,1)S(1)} %get-tuple-element.460.own.refs_9_), channel_id=1, source_target_pairs={{0,64},{32,96},{64,128},{96,160},{128,192},{160,224},{192,0},{224,... | collective-permute-start | bytes 614408 | tf_op jit(solution)/shard_map/while/body/ppermute | solution.py:273
  12.8 11.8 %collective-permute-start.8 = (bf16[160,640]{1,0:T(8,128)(2,1)S(1)}, bf16[160,640]{1,0:T(8,128)(2,1)S(1)}, u32[]{:S(2)}, u32[]{:S(2)}) collective-permute-start(bf16[160,640]{1,0:T(8,128)(2,1)S(1)} %get-tuple-element.460.own.refs_9_), channel_id=1, source_target_pairs={{0,128},{32,160},{64,192},{96,224},{128,0},{160,32},{192,64},{224,... | collective-permute-start | bytes 614408 | tf_op jit(solution)/shard_map/while/body/ppermute | solution.py:273
  15.0 10.3 %collective-permute-start.7 = (bf16[160,640]{1,0:T(8,128)(2,1)S(1)}, bf16[160,640]{1,0:T(8,128)(2,1)S(1)}, u32[]{:S(2)}, u32[]{:S(2)}) collective-permute-start(bf16[160,640]{1,0:T(8,128)(2,1)S(1)} %get-tuple-element.460.own.refs_9_), channel_id=1, source_target_pairs={{0,192},{32,224},{64,0},{96,32},{128,64},{160,96},{192,128},{224,1... | collective-permute-start | bytes 614408 | tf_op jit(solution)/shard_map/while/body/ppermute | solution.py:273
  27.2 12.4 %collective-permute-start.11 = (bf16[1536,128]{1,0:T(8,128)(2,1)S(1)}, bf16[1536,128]{1,0:T(8,128)(2,1)S(1)}, u32[]{:S(2)}, u32[]{:S(2)}) collective-permute-start(bf16[1536,128]{1,0:T(8,128)(2,1)S(1)} %body.24.refs_0_), channel_id=1, source_target_pairs={{0,7},{1,0},{2,1},{3,2},{4,3},{5,4},{6,5},{7,6},{8,15},{9,8},{10,9... | collective-permute-start | bytes 1179656 | tf_op jit(solution)/shard_map/while/body/ppermute | solution.py:277
  32.1 11.0 %collective-permute-start.10 = (bf16[1536,128]{1,0:T(8,128)(2,1)S(1)}, bf16[1536,128]{1,0:T(8,128)(2,1)S(1)}, u32[]{:S(2)}, u32[]{:S(2)}) collective-permute-start(bf16[1536,128]{1,0:T(8,128)(2,1)S(1)} %body.24.refs_0_), channel_id=1, source_target_pairs={{0,1},{1,2},{2,3},{3,4},{4,5},{5,6},{6,7},{7,0},{8,9},{9,10},{10,1... | collective-permute-start | bytes 1179656 | tf_op jit(solution)/shard_map/while/body/ppermute | solution.py:277
  39.7 10.2 %collective-permute-start.13 = (bf16[1536,128]{1,0:T(8,128)(2,1)S(1)}, bf16[1536,128]{1,0:T(8,128)(2,1)S(1)}, u32[]{:S(2)}, u32[]{:S(2)}) collective-permute-start(bf16[1536,128]{1,0:T(8,128)(2,1)S(1)} %collective-permute-done.11.refs_2_), channel_id=1, source_target_pairs={{0,7},{1,0},{2,1},{3,2},{4,3},{5,4},{6,5},{7,6},{8,15},{9,8},{10,9... | collective-permute-start | bytes 1179656 | tf_op jit(solution)/shard_map/while/body/ppermute | solution.py:277
  43.1 10.2 %collective-permute-start.12 = (bf16[1536,128]{1,0:T(8,128)(2,1)S(1)}, bf16[1536,128]{1,0:T(8,128)(2,1)S(1)}, u32[]{:S(2)}, u32[]{:S(2)}) collective-permute-start(bf16[1536,128]{1,0:T(8,128)(2,1)S(1)} %collective-permute-done.10.refs_1_), channel_id=1, source_target_pairs={{0,1},{1,2},{2,3},{3,4},{4,5},{5,6},{6,7},{7,0},{8,9},{9,10},{10,1... | collective-permute-start | bytes 1179656 | tf_op jit(solution)/shard_map/while/body/ppermute | solution.py:277
  43.1 13.8 %collective-permute-start.20 = (bf16[160,640]{1,0:T(8,128)(2,1)S(1)}, bf16[160,640]{1,0:T(8,128)(2,1)S(1)}, u32[]{:S(2)}, u32[]{:S(2)}) collective-permute-start(bf16[160,640]{1,0:T(8,128)(2,1)S(1)} %get-tuple-element.617), channel_id=1, source_target_pairs={{0,8},{8,16},{16,24},{24,0},{1,9},{9,17},{17,25},{25,1},{2,10},{10... | collective-permute-start | bytes 614408 | tf_op jit(solution)/shard_map/while/body/ppermute | solution.py:269
  49.8 16.9 %collective-permute-start.15 = (bf16[1536,128]{1,0:T(8,128)(2,1)S(1)}, bf16[1536,128]{1,0:T(8,128)(2,1)S(1)}, u32[]{:S(2)}, u32[]{:S(2)}) collective-permute-start(bf16[1536,128]{1,0:T(8,128)(2,1)S(1)} %collective-permute-done.13.refs_4_), channel_id=1, source_target_pairs={{0,7},{1,0},{2,1},{3,2},{4,3},{5,4},{6,5},{7,6},{8,15},{9,8},{10,9... | collective-permute-start | bytes 1179656 | tf_op jit(solution)/shard_map/while/body/ppermute | solution.py:277
  53.3 13.5 %collective-permute-start.14 = (bf16[1536,128]{1,0:T(8,128)(2,1)S(1)}, bf16[1536,128]{1,0:T(8,128)(2,1)S(1)}, u32[]{:S(2)}, u32[]{:S(2)}) collective-permute-start(bf16[1536,128]{1,0:T(8,128)(2,1)S(1)} %collective-permute-done.12.refs_3_), channel_id=1, source_target_pairs={{0,1},{1,2},{2,3},{3,4},{4,5},{5,6},{6,7},{7,0},{8,9},{9,10},{10,1... | collective-permute-start | bytes 1179656 | tf_op jit(solution)/shard_map/while/body/ppermute | solution.py:277
  56.9 12.7 %collective-permute-start.21 = (bf16[160,640]{1,0:T(8,128)(2,1)S(1)}, bf16[160,640]{1,0:T(8,128)(2,1)S(1)}, u32[]{:S(2)}, u32[]{:S(2)}) collective-permute-start(bf16[160,640]{1,0:T(8,128)(2,1)S(1)} %get-tuple-element.617), channel_id=1, source_target_pairs={{0,32},{32,0},{64,96},{96,64},{128,160},{160,128},{192,224},{224,1... | collective-permute-start | bytes 614408 | tf_op jit(solution)/shard_map/while/body/ppermute | solution.py:281
  60.3 9.3 %collective-permute-start.24 = (bf16[160,640]{1,0:T(8,128)(2,1)S(1)}, bf16[160,640]{1,0:T(8,128)(2,1)S(1)}, u32[]{:S(2)}, u32[]{:S(2)}) collective-permute-start(bf16[160,640]{1,0:T(8,128)(2,1)S(1)} %collective-permute-done.20.refs_12_), channel_id=1, source_target_pairs={{0,32},{32,0},{64,96},{96,64},{128,160},{160,128},{192,224},{224,1... | collective-permute-start | bytes 614408 | tf_op jit(solution)/shard_map/while/body/ppermute | solution.py:281
  86.9 10.9 %collective-permute-start.26 = (bf16[160,640]{1,0:T(8,128)(2,1)S(1)}, bf16[160,640]{1,0:T(8,128)(2,1)S(1)}, u32[]{:S(2)}, u32[]{:S(2)}) collective-permute-start(bf16[160,640]{1,0:T(8,128)(2,1)S(1)} %get-tuple-element.464.refs_0_), channel_id=1, source_target_pairs={{0,16},{8,24},{16,0},{24,8},{1,17},{9,25},{17,1},{25,9},{2,18},{10... | collective-permute-start | bytes 614408 | tf_op jit(solution)/shard_map/while/body/ppermute | solution.py:269
  89.9 10.4 %collective-permute-start.25 = (bf16[160,640]{1,0:T(8,128)(2,1)S(1)}, bf16[160,640]{1,0:T(8,128)(2,1)S(1)}, u32[]{:S(2)}, u32[]{:S(2)}) collective-permute-start(bf16[160,640]{1,0:T(8,128)(2,1)S(1)} %get-tuple-element.464.refs_0_), channel_id=1, source_target_pairs={{0,24},{8,0},{16,8},{24,16},{1,25},{9,1},{17,9},{25,17},{2,26},{10... | collective-permute-start | bytes 614408 | tf_op jit(solution)/shard_map/while/body/ppermute | solution.py:269
  90.3 10.0 %collective-permute-start.28 = (bf16[160,640]{1,0:T(8,128)(2,1)S(1)}, bf16[160,640]{1,0:T(8,128)(2,1)S(1)}, u32[]{:S(2)}, u32[]{:S(2)}) collective-permute-start(bf16[160,640]{1,0:T(8,128)(2,1)S(1)} %get-tuple-element.464.refs_0_), channel_id=1, source_target_pairs={{0,32},{32,0},{64,96},{96,64},{128,160},{160,128},{192,224},{224,1... | collective-permute-start | bytes 614408 | tf_op jit(solution)/shard_map/while/body/ppermute | solution.py:281
  106.9 8.1 %collective-permute-start.9 = (bf16[160,640]{1,0:T(8,128)(2,1)S(1)}, bf16[160,640]{1,0:T(8,128)(2,1)S(1)}, u32[]{:S(2)}, u32[]{:S(2)}) collective-permute-start(bf16[160,640]{1,0:T(8,128)(2,1)S(1)} %get-tuple-element.460.own.refs_9_), channel_id=1, source_target_pairs={{0,64},{32,96},{64,128},{96,160},{128,192},{160,224},{192,0},{224,... | collective-permute-start | bytes 614408 | tf_op jit(solution)/shard_map/while/body/ppermute | solution.py:273
  106.9 13.4 %collective-permute-start.8 = (bf16[160,640]{1,0:T(8,128)(2,1)S(1)}, bf16[160,640]{1,0:T(8,128)(2,1)S(1)}, u32[]{:S(2)}, u32[]{:S(2)}) collective-permute-start(bf16[160,640]{1,0:T(8,128)(2,1)S(1)} %get-tuple-element.460.own.refs_9_), channel_id=1, source_target_pairs={{0,128},{32,160},{64,192},{96,224},{128,0},{160,32},{192,64},{224,... | collective-permute-start | bytes 614408 | tf_op jit(solution)/shard_map/while/body/ppermute | solution.py:273
  111.0 9.3 %collective-permute-start.7 = (bf16[160,640]{1,0:T(8,128)(2,1)S(1)}, bf16[160,640]{1,0:T(8,128)(2,1)S(1)}, u32[]{:S(2)}, u32[]{:S(2)}) collective-permute-start(bf16[160,640]{1,0:T(8,128)(2,1)S(1)} %get-tuple-element.460.own.refs_9_), channel_id=1, source_target_pairs={{0,192},{32,224},{64,0},{96,32},{128,64},{160,96},{192,128},{224,1... | collective-permute-start | bytes 614408 | tf_op jit(solution)/shard_map/while/body/ppermute | solution.py:273
  122.2 9.6 %collective-permute-start.11 = (bf16[1536,128]{1,0:T(8,128)(2,1)S(1)}, bf16[1536,128]{1,0:T(8,128)(2,1)S(1)}, u32[]{:S(2)}, u32[]{:S(2)}) collective-permute-start(bf16[1536,128]{1,0:T(8,128)(2,1)S(1)} %body.24.refs_0_), channel_id=1, source_target_pairs={{0,7},{1,0},{2,1},{3,2},{4,3},{5,4},{6,5},{7,6},{8,15},{9,8},{10,9... | collective-permute-start | bytes 1179656 | tf_op jit(solution)/shard_map/while/body/ppermute | solution.py:277
  122.5 10.7 %collective-permute-start.10 = (bf16[1536,128]{1,0:T(8,128)(2,1)S(1)}, bf16[1536,128]{1,0:T(8,128)(2,1)S(1)}, u32[]{:S(2)}, u32[]{:S(2)}) collective-permute-start(bf16[1536,128]{1,0:T(8,128)(2,1)S(1)} %body.24.refs_0_), channel_id=1, source_target_pairs={{0,1},{1,2},{2,3},{3,4},{4,5},{5,6},{6,7},{7,0},{8,9},{9,10},{10,1... | collective-permute-start | bytes 1179656 | tf_op jit(solution)/shard_map/while/body/ppermute | solution.py:277
  131.8 8.7 %collective-permute-start.13 = (bf16[1536,128]{1,0:T(8,128)(2,1)S(1)}, bf16[1536,128]{1,0:T(8,128)(2,1)S(1)}, u32[]{:S(2)}, u32[]{:S(2)}) collective-permute-start(bf16[1536,128]{1,0:T(8,128)(2,1)S(1)} %collective-permute-done.11.refs_2_), channel_id=1, source_target_pairs={{0,7},{1,0},{2,1},{3,2},{4,3},{5,4},{6,5},{7,6},{8,15},{9,8},{10,9... | collective-permute-start | bytes 1179656 | tf_op jit(solution)/shard_map/while/body/ppermute | solution.py:277
  133.3 9.9 %collective-permute-start.12 = (bf16[1536,128]{1,0:T(8,128)(2,1)S(1)}, bf16[1536,128]{1,0:T(8,128)(2,1)S(1)}, u32[]{:S(2)}, u32[]{:S(2)}) collective-permute-start(bf16[1536,128]{1,0:T(8,128)(2,1)S(1)} %collective-permute-done.10.refs_1_), channel_id=1, source_target_pairs={{0,1},{1,2},{2,3},{3,4},{4,5},{5,6},{6,7},{7,0},{8,9},{9,10},{10,1... | collective-permute-start | bytes 1179656 | tf_op jit(solution)/shard_map/while/body/ppermute | solution.py:277
  133.3 12.6 %collective-permute-start.20 = (bf16[160,640]{1,0:T(8,128)(2,1)S(1)}, bf16[160,640]{1,0:T(8,128)(2,1)S(1)}, u32[]{:S(2)}, u32[]{:S(2)}) collective-permute-start(bf16[160,640]{1,0:T(8,128)(2,1)S(1)} %get-tuple-element.617), channel_id=1, source_target_pairs={{0,8},{8,16},{16,24},{24,0},{1,9},{9,17},{17,25},{25,1},{2,10},{10... | collective-permute-start | bytes 614408 | tf_op jit(solution)/shard_map/while/body/ppermute | solution.py:269
  140.5 14.9 %collective-permute-start.15 = (bf16[1536,128]{1,0:T(8,128)(2,1)S(1)}, bf16[1536,128]{1,0:T(8,128)(2,1)S(1)}, u32[]{:S(2)}, u32[]{:S(2)}) collective-permute-start(bf16[1536,128]{1,0:T(8,128)(2,1)S(1)} %collective-permute-done.13.refs_4_), channel_id=1, source_target_pairs={{0,7},{1,0},{2,1},{3,2},{4,3},{5,4},{6,5},{7,6},{8,15},{9,8},{10,9... | collective-permute-start | bytes 1179656 | tf_op jit(solution)/shard_map/while/body/ppermute | solution.py:277
  143.2 12.3 %collective-permute-start.14 = (bf16[1536,128]{1,0:T(8,128)(2,1)S(1)}, bf16[1536,128]{1,0:T(8,128)(2,1)S(1)}, u32[]{:S(2)}, u32[]{:S(2)}) collective-permute-start(bf16[1536,128]{1,0:T(8,128)(2,1)S(1)} %collective-permute-done.12.refs_3_), channel_id=1, source_target_pairs={{0,1},{1,2},{2,3},{3,4},{4,5},{5,6},{6,7},{7,0},{8,9},{9,10},{10,1... | collective-permute-start | bytes 1179656 | tf_op jit(solution)/shard_map/while/body/ppermute | solution.py:277
  144.2 9.4 %collective-permute-start.18 = (bf16[160,640]{1,0:T(8,128)(2,1)S(1)}, bf16[160,640]{1,0:T(8,128)(2,1)S(1)}, u32[]{:S(2)}, u32[]{:S(2)}) collective-permute-start(bf16[160,640]{1,0:T(8,128)(2,1)S(1)} %get-tuple-element.617), channel_id=1, source_target_pairs={{0,24},{8,0},{16,8},{24,16},{1,25},{9,1},{17,9},{25,17},{2,26},{10... | collective-permute-start | bytes 614408 | tf_op jit(solution)/shard_map/while/body/ppermute | solution.py:269
  145.9 12.3 %collective-permute-start.21 = (bf16[160,640]{1,0:T(8,128)(2,1)S(1)}, bf16[160,640]{1,0:T(8,128)(2,1)S(1)}, u32[]{:S(2)}, u32[]{:S(2)}) collective-permute-start(bf16[160,640]{1,0:T(8,128)(2,1)S(1)} %get-tuple-element.617), channel_id=1, source_target_pairs={{0,32},{32,0},{64,96},{96,64},{128,160},{160,128},{192,224},{224,1... | collective-permute-start | bytes 614408 | tf_op jit(solution)/shard_map/while/body/ppermute | solution.py:281
  149.7 8.5 %collective-permute-start.24 = (bf16[160,640]{1,0:T(8,128)(2,1)S(1)}, bf16[160,640]{1,0:T(8,128)(2,1)S(1)}, u32[]{:S(2)}, u32[]{:S(2)}) collective-permute-start(bf16[160,640]{1,0:T(8,128)(2,1)S(1)} %collective-permute-done.20.refs_12_), channel_id=1, source_target_pairs={{0,32},{32,0},{64,96},{96,64},{128,160},{160,128},{192,224},{224,1... | collective-permute-start | bytes 614408 | tf_op jit(solution)/shard_map/while/body/ppermute | solution.py:281
  176.0 10.6 %collective-permute-start.26 = (bf16[160,640]{1,0:T(8,128)(2,1)S(1)}, bf16[160,640]{1,0:T(8,128)(2,1)S(1)}, u32[]{:S(2)}, u32[]{:S(2)}) collective-permute-start(bf16[160,640]{1,0:T(8,128)(2,1)S(1)} %get-tuple-element.464.refs_0_), channel_id=1, source_target_pairs={{0,16},{8,24},{16,0},{24,8},{1,17},{9,25},{17,1},{25,9},{2,18},{10... | collective-permute-start | bytes 614408 | tf_op jit(solution)/shard_map/while/body/ppermute | solution.py:269
  178.6 10.4 %collective-permute-start.25 = (bf16[160,640]{1,0:T(8,128)(2,1)S(1)}, bf16[160,640]{1,0:T(8,128)(2,1)S(1)}, u32[]{:S(2)}, u32[]{:S(2)}) collective-permute-start(bf16[160,640]{1,0:T(8,128)(2,1)S(1)} %get-tuple-element.464.refs_0_), channel_id=1, source_target_pairs={{0,24},{8,0},{16,8},{24,16},{1,25},{9,1},{17,9},{25,17},{2,26},{10... | collective-permute-start | bytes 614408 | tf_op jit(solution)/shard_map/while/body/ppermute | solution.py:269
  179.3 9.6 %collective-permute-start.28 = (bf16[160,640]{1,0:T(8,128)(2,1)S(1)}, bf16[160,640]{1,0:T(8,128)(2,1)S(1)}, u32[]{:S(2)}, u32[]{:S(2)}) collective-permute-start(bf16[160,640]{1,0:T(8,128)(2,1)S(1)} %get-tuple-element.464.refs_0_), channel_id=1, source_target_pairs={{0,32},{32,0},{64,96},{96,64},{128,160},{160,128},{192,224},{224,1... | collective-permute-start | bytes 614408 | tf_op jit(solution)/shard_map/while/body/ppermute | solution.py:281
  (23 other events, 199.4 us)
where the time goes:
time: 201 us; the launch traced here: 200 us
  starting transfers between devices  86.8 us (43%)
  waiting for transfers between devices  69.2 us (34%)
  Pallas kernels  38.2 us (19%)
  between operations  2.64 us (1%)
    ppermute x16, waiting for transfers between devices, along_z(): return lax.ppermute(value, 'layer', ring('layer', shift, NZ))  41.6 us
    ppermute x18, starting transfers between devices, other_core(): return lax.ppermute(value, 'row', [(i, i ^ 1) for i in range(2 * NY)])  37.8 us
    pallas_call x9, Pallas kernels, call(): pl.pallas_call(kernel, out_shape=outs, in_specs=[SMEM] * n_smem + [VMEM]...  35.1 us
    ppermute x16, starting transfers between devices, along_z(): return lax.ppermute(value, 'layer', ring('layer', shift, NZ))  22.9 us
    ppermute x12, starting transfers between devices, along_x(): return lax.ppermute(value, 'col', ring('col', shift, NX))  18.7 us
    ppermute x6, waiting for transfers between devices, along_y(): return lax.ppermute(value, 'row', ring('row', shift, 2 * NY, 2))  18.5 us
    ppermute x6, starting transfers between devices, along_y(): return lax.ppermute(value, 'row', ring('row', shift, 2 * NY, 2))  7.41 us
    ppermute x12, waiting for transfers between devices, along_x(): return lax.ppermute(value, 'col', ring('col', shift, NX))  4.93 us
  transfers between devices with their start and end apart: 52, of which 22 were waited for; matrix products, arithmetic and copies ran while one was open for 0% of the time, Pallas kernels for 2%

commit v1 on v0

v1 whole, which is shorter than its diff:
```python
import functools

import jax
import jax.numpy as jnp
from jax import lax
from jax.experimental import pallas as pl
from jax.experimental.pallas import tpu as pltpu
from jax.sharding import PartitionSpec as P

TILE = 128
STEPS = 2
SUB = 16

SHARE = 80
NY, NX, NZ = 4, 4, 8
ROW_BLOCK = SHARE * NZ
BAND_TILES = 10
WIDTH = BAND_TILES * TILE
TILES = 40
ORDER = TILES * TILE
NSUB = SHARE // SUB
ALL_SLOTS = 2 * NY * NSUB * BAND_TILES
Z_ORDER = (0, -1, 1, -2, 2, -3, 3, 4)
SLOTS = 512
UNROLL = 8
CAPACITY = 88
SPLIT = 48
EXTRA = 16
ROUNDS = -(-(ALL_SLOTS // 2 - CAPACITY) // EXTRA)

SMEM = pl.BlockSpec(memory_space=pltpu.SMEM)
VMEM = pl.BlockSpec(memory_space=pltpu.VMEM)
HBM = pl.BlockSpec(memory_space=pltpu.HBM)
PARAMS = pltpu.CompilerParams(vmem_limit_bytes=20 * 1024 * 1024)


def row_of(block, z, sub):
    return block * ROW_BLOCK + SHARE * z + SUB * sub


def where_am_i(pos):
    return pos[0], pos[1], pos[2], pos[3]


def start_kernel(pos, pat, n_occ, mu, gamma, hamiltonian, out):
    y, core, x, z = where_am_i(pos)
    filling = jnp.full((SUB, TILE), n_occ[0].astype(jnp.float32)) / ORDER
    apart = lax.broadcasted_iota(jnp.int32, (SUB, TILE), 1) - lax.broadcasted_iota(
        jnp.int32, (SUB, TILE), 0
    )

    def strip(s, _):
        g = row_of(2 * y + core, z, s)
        i = g // TILE
        near = apart == g % TILE
        rows = pl.ds(pl.multiple_of(s * SUB, SUB), SUB)
        for t in range(BAND_TILES):
            j = BAND_TILES * x + t
            cols = slice(t * TILE, (t + 1) * TILE)
            identity = jnp.where(near, (i == j).astype(jnp.float32), 0.0)
            h = hamiltonian[rows, cols].astype(jnp.float32)
            value = filling * identity + gamma[0] * (mu[0] * identity - h)
            out[rows, cols] = (value * pat[i, j].astype(jnp.float32)).astype(jnp.bfloat16)
        return 0

    lax.fori_loop(0, NSUB, strip, 0)


def table_kernel(pos, pat, table, most):
    y, core, x, z = where_am_i(pos)
    f32 = jnp.float32
    pattern = pat[...].astype(f32)
    n = 8 * NSUB

    def iota(shape, dim):
        return lax.broadcasted_iota(jnp.int32, shape, dim)

    rows = iota((NZ * n, TILES), 0)
    rz, rn = rows // n, rows % n
    rk = row_of(rn // NSUB, rz, rn % NSUB) // TILE
    picked = jnp.dot((rk == iota((NZ * n, TILES), 1)).astype(f32), pattern)
    total = jnp.dot(
        (iota((NZ, NZ * n), 0) == iota((NZ, NZ * n), 1) // n).astype(f32), picked
    )
    k, band = iota((TILES, NX), 0), iota((TILES, NX), 1)
    group = (k // BAND_TILES == band).astype(f32)
    most[0] = jnp.max(jnp.dot(total, group)).astype(jnp.int32)

    cols = (iota((TILES, TILE), 0) == BAND_TILES * x + iota((TILES, TILE), 1)) & (
        iota((TILES, TILE), 1) < BAND_TILES
    )
    mine = jnp.dot(pattern, cols.astype(f32))
    before = (iota((TILE, TILE), 0) < iota((TILE, TILE), 1)).astype(f32)
    below = (iota((n, n), 1) < iota((n, n), 0)).astype(f32)
    slots = iota((n, SLOTS), 1)
    for m, rel in enumerate(Z_ORDER):
        zz = (z + rel) % NZ

        def first_row(shape, dim):
            r = iota(shape, dim)
            return row_of((2 * y + r // NSUB) % (2 * NY), zz, r % NSUB)

        pick = (first_row((n, TILES), 0) // TILE == iota((n, TILES), 1)).astype(f32)
        p = jnp.dot(pick, mine)
        count = jnp.sum(p, axis=1, keepdims=True)
        ahead = jnp.sum(below * jnp.reshape(jnp.dot(pick, mine).sum(axis=1), (1, n)), axis=1, keepdims=True)
        slot = (ahead + jnp.dot(p, before)).astype(jnp.int32)
        g = first_row((n, 1), 0)
        kk = g // TILE
        kx, kt = kk // BAND_TILES, kk % BAND_TILES
        place = (kx + NX - x) % NX * BAND_TILES + kt
        to = (place * TILE + g % TILE) * 16
        r = iota((n, 1), 0)
        frm = (r // NSUB * SHARE + r % NSUB * SUB) * 16
        codes = jnp.zeros((n, SLOTS), jnp.int32)
        sources = jnp.zeros((n, SLOTS), jnp.int32)
        for t in range(BAND_TILES):
            here = (slots == slot[:, t : t + 1]) & (p[:, t : t + 1] > 0)
            codes += jnp.where(here, to + t, 0)
            if m == 0:
                sources += jnp.where(here, frm + t, 0)
        number = jnp.sum(count).astype(jnp.int32)
        at = iota((1, SLOTS), 1)
        line = jnp.sum(codes, axis=0, keepdims=True)
        line = jnp.where(at < number, line, ORDER * 16)
        table[m : m + 1, :] = jnp.where(at == SLOTS - 1, number, line)
        if m == 0:
            table[NZ : NZ + 1, :] = jnp.sum(sources, axis=0, keepdims=True)


def pack_kernel(count, pos, base, table, *refs):
    blocks, (out, block) = refs[:8], refs[8:]
    core = pos[1]
    for d, ref in enumerate(blocks):
        at = d % NY * 2 + (core if d < NY else 1 - core)
        block[pl.ds(pl.multiple_of(at * SHARE, SHARE), SHARE), :] = ref[...]

    def some(i, _):
        for u in range(UNROLL):
            slot = i * UNROLL + u
            code = table[NZ, 2 * (base[0] + slot) + core]
            row = pl.multiple_of(code // 16, SUB)
            col = pl.multiple_of(code % 16 * TILE, TILE)
            to = pl.multiple_of(slot * SUB, SUB)
            out[pl.ds(to, SUB), :] = block[pl.ds(row, SUB), pl.ds(col, TILE)]
        return 0

    lax.fori_loop(0, count // UNROLL, some, 0)


def place(table, m, core, source, panel, first, last):
    def some(i, _):
        for u in range(UNROLL):
            slot = first + i * UNROLL + u
            code = table[m, 2 * slot + core]
            row = pl.multiple_of(code // 16, SUB)
            col = pl.multiple_of(code % 16 * TILE, TILE)
            frm = pl.multiple_of((i * UNROLL + u) * SUB, SUB)
            panel[pl.ds(row, SUB), pl.ds(col, TILE)] = source[pl.ds(frm, SUB), :]
        return 0

    number = jnp.clip((table[m, SLOTS - 1] + 1 - core) // 2 - first, 0, last - first)
    lax.fori_loop(0, (number + UNROLL - 1) // UNROLL, some, 0)


def product(left, panel):
    total = None
    for m, ref in enumerate(left):
        at = slice(m * WIDTH, (m + 1) * WIDTH)
        one = jnp.dot(ref[...], panel[at, :], preferred_element_type=jnp.float32)
        total = one if total is None else total + one
    return total


def each_tile(pos, pat, use):
    y, core, x, z = where_am_i(pos)

    def strip(s, _):
        i = row_of(2 * y + core, z, s) // TILE
        rows = pl.ds(pl.multiple_of(s * SUB, SUB), SUB)
        for t in range(BAND_TILES):
            where = (rows, slice(t * TILE, (t + 1) * TILE))
            use(where, pat[i, BAND_TILES * x + t].astype(jnp.float32))
        return 0

    lax.fori_loop(0, NSUB, strip, 0)


def parts_kernel(down, up, first, last):
    first[...] = down[: SPLIT * SUB, :]
    last[...] = up[SPLIT * SUB :, :]


def near_kernel(pos, table, *refs):
    packed, panel = refs[:-1], refs[-1]
    panel[...] = jnp.zeros_like(panel)
    for q, ref in enumerate(packed):
        core = pos[1] if q % 2 == 0 else 1 - pos[1]
        place(table, q // 2, core, ref, panel, 0, CAPACITY)


def square_kernel(pos, pat, table, *refs):
    packed, left, spill = refs[:8], refs[9:13], refs[13]
    (square, square_half, panel), (total, more) = refs[14:17], refs[17:]
    for q, ref in enumerate(packed):
        core = pos[1] if q % 2 == 0 else 1 - pos[1]
        m = (5, 6, 7, 7)[q // 2]
        first, last = ((0, CAPACITY), (0, CAPACITY), (0, SPLIT), (SPLIT, CAPACITY))[q // 2]
        place(table, m, core, ref, panel, first, last)
    for m in range(NZ):

        @pl.when(table[m, SLOTS - 1] > 2 * CAPACITY)
        def _():
            for side in range(2):
                core = pos[1] if side == 0 else 1 - pos[1]
                pltpu.sync_copy(spill.at[side, (pos[3] + Z_ORDER[m] + NZ) % NZ], more)
                place(table, m, core, more, panel, CAPACITY, CAPACITY + ROUNDS * EXTRA)

    total[...] = product(left, panel)

    def use(where, mask):
        value = total[where] * mask
        square[where] = value
        square_half[where] = value.astype(jnp.bfloat16)

    each_tile(pos, pat, use)


def cube_kernel(pos, pat, square, panel, *refs):
    left, (out, out_half), total = refs[:4], refs[4:6], refs[6]
    total[...] = product(left, panel)

    def use(where, mask):
        value = 3.0 * square[where] - 2.0 * (total[where] * mask)
        out[where] = value
        out_half[where] = value.astype(jnp.bfloat16)

    each_tile(pos, pat, use)


def ring(axis, shift, size, stride=1):
    return [(i, (i + shift * stride) % size) for i in range(size)]


def along_x(value, shift):
    return lax.ppermute(value, "col", ring("col", shift, NX))


def along_y(value, shift):
    return lax.ppermute(value, "row", ring("row", shift, 2 * NY, 2))


def along_z(value, shift):
    return lax.ppermute(value, "layer", ring("layer", shift, NZ))


def other_core(value):
    return lax.ppermute(value, "row", [(i, i ^ 1) for i in range(2 * NY)])


def whole_rows(mine):
    return [mine, along_x(mine, -1), along_x(mine, 2), along_x(mine, 1)]


def call(kernel, outs, n_smem, *args, scratch=(), n_hbm=0, flops=0, aliases=None):
    single = not isinstance(outs, (tuple, list))
    return pl.pallas_call(
        kernel,
        out_shape=outs,
        in_specs=[SMEM] * n_smem + [VMEM] * (len(args) - n_smem - n_hbm) + [HBM] * n_hbm,
        out_specs=VMEM if single else [VMEM] * len(outs),
        scratch_shapes=scratch,
        input_output_aliases=aliases or {},
        compiler_params=PARAMS,
        cost_estimate=pl.CostEstimate(flops=flops, bytes_accessed=0, transcendentals=0),
    )(*args)


def pack(count, pos, base, table, blocks):
    return call(
        functools.partial(pack_kernel, count),
        jax.ShapeDtypeStruct((count * SUB, TILE), jnp.bfloat16),
        3,
        *(pos, jnp.asarray(base, jnp.int32).reshape(1), table, *blocks),
        scratch=(pltpu.VMEM((ROW_BLOCK, WIDTH), jnp.bfloat16),),
    )


def nothing_kernel(out):
    pass


def spilled(pos, most, table, blocks):
    rounds = (most[0] - 2 * CAPACITY + 2 * EXTRA - 1) // (2 * EXTRA)
    shape = (2, NZ, ROUNDS * EXTRA * SUB, TILE)
    empty = pl.pallas_call(
        nothing_kernel, out_shape=jax.ShapeDtypeStruct(shape, jnp.bfloat16), out_specs=HBM
    )()

    def one_round(carry):
        turn, spill = carry
        mine = pack(EXTRA, pos, CAPACITY + turn * EXTRA, table, blocks)
        got = lax.all_gather(mine, "layer")
        got = jnp.stack([got, other_core(got)])
        return turn + 1, lax.dynamic_update_slice(spill, got, (0, 0, turn * EXTRA * SUB, 0))

    return lax.while_loop(lambda carry: carry[0] < rounds, one_round, (jnp.int32(0), empty))[1]


def steps(pos, pat, current, table, most):
    f32 = jax.ShapeDtypeStruct((SHARE, WIDTH), jnp.float32)
    bf16 = jax.ShapeDtypeStruct((SHARE, WIDTH), jnp.bfloat16)
    panel_shape = jax.ShapeDtypeStruct((ORDER + SUB, WIDTH), jnp.bfloat16)
    total = pltpu.VMEM((SHARE, WIDTH), jnp.float32)
    more = pltpu.VMEM((ROUNDS * EXTRA * SUB, TILE), jnp.bfloat16)
    split = SPLIT * SUB

    def step(carry):
        turn, current = carry[:2]
        blocks = [current, along_y(current, -1), along_y(current, 2), along_y(current, 1)]
        blocks += map(other_core, blocks[:4])
        packed = pack(CAPACITY, pos, 0, table, blocks)
        spill = spilled(pos, most, table, blocks)
        turn, current, packed, spill = lax.optimization_barrier((turn + 1, current, packed, spill))
        left = whole_rows(current)
        down, up = along_z(packed, 1), along_z(packed, -1)
        down2, up2 = along_z(down, 1), along_z(up, -1)
        down2, up2, *left = lax.optimization_barrier((down2, up2, *left))
        down3, up3 = along_z(down2, 1), along_z(up2, -1)
        near = [both for one in (packed, down, up, down2, up2) for both in (one, other_core(one))]
        panel = call(near_kernel, panel_shape, 2, pos, table, *near, flops=10**9)
        down3, up3, panel = lax.optimization_barrier((down3, up3, panel))
        first_part = jax.ShapeDtypeStruct((split, TILE), jnp.bfloat16)
        last_part = jax.ShapeDtypeStruct((CAPACITY * SUB - split, TILE), jnp.bfloat16)
        part_a, part_b = call(parts_kernel, (first_part, last_part), 0, down3, up3)
        far_a, far_b = along_z(part_a, 1), along_z(part_b, -1)
        far = [both for one in (down3, up3, far_a, far_b) for both in (one, other_core(one))]
        square, square_half, panel = call(
            square_kernel,
            (f32, bf16, panel_shape),
            3,
            *(pos, pat, table, *far, panel, *left, spill),
            scratch=(total, more),
            n_hbm=1,
            aliases={11: 2},
            flops=10**9,
        )
        left = whole_rows(square_half)
        result, following = call(
            cube_kernel,
            (f32, bf16),
            2,
            *(pos, pat, square, panel, *left),
            scratch=(total,),
            flops=10**9,
        )
        return turn, following, result

    first = (jnp.int32(0), current, jnp.zeros((SHARE, WIDTH), jnp.float32))
    return lax.while_loop(lambda carry: carry[0] < STEPS, step, first)[2]


def shards(hamiltonian, tile_pattern, n_occ, mu, gamma):
    row, x, z = lax.axis_index("row"), lax.axis_index("col"), lax.axis_index("layer")
    pos = jnp.stack([row // 2, row % 2, x, z]).astype(jnp.int32)
    share = jax.ShapeDtypeStruct((SHARE, WIDTH), jnp.bfloat16)
    current = call(start_kernel, share, 5, pos, tile_pattern, n_occ, mu, gamma, hamiltonian)
    table, most = pl.pallas_call(
        table_kernel,
        out_shape=(
            jax.ShapeDtypeStruct((NZ + 1, SLOTS), jnp.int32),
            jax.ShapeDtypeStruct((1,), jnp.int32),
        ),
        in_specs=[SMEM, VMEM],
        out_specs=[VMEM, SMEM],
        compiler_params=PARAMS,
    )(pos, tile_pattern)
    return steps(pos, tile_pattern, current, table, most)


def solution(mesh):
    placed = (P(("row", "layer"), "col"), P(), P(), P(), P())
    return jax.shard_map(
        shards, mesh=mesh, in_specs=placed, out_specs=P(("row", "layer"), "col"), check_vma=False
    )
```

time: 201 us -> 194 us (0.965)
  waiting for transfers between devices: 69.2 us -> 50.4 us
  starting transfers between devices: 86.8 us -> 93.9 us
  Pallas kernels: 38.2 us -> 42.8 us
    ppermute x16, waiting for transfers between devices: 41.6 us -> 16.2 us  [along_z(): return lax.ppermute(value, 'layer', ring('layer', shift, NZ))]
    ppermute x12, waiting for transfers between devices: 4.93 us -> 25.2 us  [along_x(): return lax.ppermute(value, 'col', ring('col', shift, NX))]
    ppermute x6, waiting for transfers between devices: 18.5 us -> 3.88 us  [along_y(): return lax.ppermute(value, 'row', ring('row', shift, 2 * NY, 2))]
    ppermute x12, starting transfers between devices: 18.7 us -> 24.2 us  [along_x(): return lax.ppermute(value, 'col', ring('col', shift, NX))]
    ppermute x18 -> x26, starting transfers between devices: 37.8 us -> 33.4 us  [other_core(): return lax.ppermute(value, 'row', [(i, i ^ 1) for i in range(2 * NY)])]
    pallas_call x9 -> x11, Pallas kernels: 35.1 us -> 38.8 us  [call(): pl.pallas_call(kernel, out_shape=outs, in_specs=[SMEM] * n_smem + [VMEM]...]
    ppermute x16, starting transfers between devices: 22.9 us -> 26.6 us  [along_z(): return lax.ppermute(value, 'layer', ring('layer', shift, NZ))]
    ppermute x6, starting transfers between devices: 7.41 us -> 9.71 us  [along_y(): return lax.ppermute(value, 'row', ring('row', shift, 2 * NY, 2))]
  transfers between devices with their start and end apart: 52 -> 60, of which waited for: 22 -> 25; matrix products, arithmetic and copies ran while one was open for 0% -> 0% of each run, Pallas kernels for 2% -> 6%
where the time goes in v1:
time: 194 us; the launch traced here: 192 us
  starting transfers between devices  93.9 us (48%)
  waiting for transfers between devices  50.4 us (26%)
  Pallas kernels  42.8 us (22%)
  between operations  2.64 us (1%)
    pallas_call x11, Pallas kernels, call(): pl.pallas_call(kernel, out_shape=outs, in_specs=[SMEM] * n_smem + [VMEM]...  38.8 us
    ppermute x26, starting transfers between devices, other_core(): return lax.ppermute(value, 'row', [(i, i ^ 1) for i in range(2 * NY)])  33.4 us
    ppermute x16, starting transfers between devices, along_z(): return lax.ppermute(value, 'layer', ring('layer', shift, NZ))  26.6 us
    ppermute x12, waiting for transfers between devices, along_x(): return lax.ppermute(value, 'col', ring('col', shift, NX))  25.2 us
    ppermute x12, starting transfers between devices, along_x(): return lax.ppermute(value, 'col', ring('col', shift, NX))  24.2 us
    ppermute x16, waiting for transfers between devices, along_z(): return lax.ppermute(value, 'layer', ring('layer', shift, NZ))  16.2 us
    ppermute x6, starting transfers between devices, along_y(): return lax.ppermute(value, 'row', ring('row', shift, 2 * NY, 2))  9.71 us
    ppermute x26, waiting for transfers between devices, other_core(): return lax.ppermute(value, 'row', [(i, i ^ 1) for i in range(2 * NY)])  5.01 us
  transfers between devices with their start and end apart: 60, of which 25 were waited for; matrix products, arithmetic and copies ran while one was open for 0% of the time, Pallas kernels for 6%

profile of v1, /device:TPU:1, one launch (start us, length us, event | category | flops | bytes accessed | tf_op | source)
XLA Modules:
  0.0 191.8 jit_solution(14408157066104879988)
XLA Ops:
  2.0 4.0 %shard_map.56 = (s32[9,512]{1,0:T(8,128)S(1)}, s32[1]{0:T(128)}) custom-call(s32[4]{0:T(128)S(1)} %pad_add_fusion.pos, s32[40,40]{1,0:T(8,128)} %pat.3), custom_call_target="tpu_custom_call" | custom-call | tf_op jit(solution)/shard_map/pallas_call | solution.py:368
  9.7 182.2 %while.37 = (s32[]{:T(128)}, bf16[80,1280]{1,0:T(8,128)(2,1)S(1)}, f32[80,1280]{1,0:T(8,128)}, s32[4]{0:T(128)S(1)}, s32[9,512]{1,0:T(8,128)S(1)}, /*index=5*/s3...) while((s32[]{:T(128)}, bf16[80,1280]{1,0:T(8,128)(2,1)S(1)}, ...), condition=%wide.region_3.4_spmd, body=%wide.region_0.3_spmd.sunk | while | flops 3002097152 | bytes 59108184 | solution.py:360
  11.8 2.6 %collective-permute-start.2 = (bf16[80,1280]{1,0:T(8,128)(2,1)S(1)}, bf16[80,1280]{1,0:T(8,128)(2,1)S(1)}, u32[]{:S(2)}, u32[]{:S(2)}) collective-permute-start(bf16[80,1280]{1,0:T(8,128)(2,1)S(1)} %get-tuple-element.599.refs_0_.refs_9_), channel_id=1, source_target_pairs={{0,128},{32,160},{64,192},{96,224},{128,0},{160,32},{192,64},{224,... | collective-permute-start | bytes 614408 | tf_op jit(solution)/shard_map/while/body/ppermute | solution.py:250
  17.0 3.4 %collective-permute-start.7 = (bf16[80,1280]{1,0:T(8,128)(2,1)S(1)}, bf16[80,1280]{1,0:T(8,128)(2,1)S(1)}, u32[]{:S(2)}, u32[]{:S(2)}) collective-permute-start(bf16[80,1280]{1,0:T(8,128)(2,1)S(1)} %collective-permute-done.3.refs_3_), channel_id=1, source_target_pairs={{0,32},{32,0},{64,96},{96,64},{128,160},{160,128},{192,224},{224,1... | collective-permute-start | bytes 614408 | tf_op jit(solution)/shard_map/while/body/ppermute | solution.py:258
  20.4 2.9 %collective-permute-done.2.refs_2_ = bf16[80,1280]{1,0:T(8,128)(2,1)S(1)} collective-permute-done((bf16[80,1280]{1,0:T(8,128)(2,1)S(1)}, bf16[80,1280]{1,0:T(8,128)(2,1)S(1)}, u32[]{:S(2)}, u32[]{:S(2)}) %collective-permute-start.2) | collective-permute-done | bytes 204832 | tf_op jit(solution)/shard_map/while/body/ppermute | solution.py:250
  28.5 5.7 %collective-permute-start.10 = (bf16[1408,128]{1,0:T(8,128)(2,1)S(1)}, bf16[1408,128]{1,0:T(8,128)(2,1)S(1)}, u32[]{:S(2)}, u32[]{:S(2)}) collective-permute-start(bf16[1408,128]{1,0:T(8,128)(2,1)S(1)} %body.34.refs_0_), channel_id=1, source_target_pairs={{0,7},{1,0},{2,1},{3,2},{4,3},{5,4},{6,5},{7,6},{8,15},{9,8},{10,9... | collective-permute-start | bytes 1081352 | tf_op jit(solution)/shard_map/while/body/ppermute | solution.py:254
  35.4 2.5 %collective-permute-start.13 = (bf16[80,1280]{1,0:T(8,128)(2,1)S(1)}, bf16[80,1280]{1,0:T(8,128)(2,1)S(1)}, u32[]{:S(2)}, u32[]{:S(2)}) collective-permute-start(bf16[80,1280]{1,0:T(8,128)(2,1)S(1)} %get-tuple-element.777), channel_id=1, source_target_pairs={{0,16},{8,24},{16,0},{24,8},{1,17},{9,25},{17,1},{25,9},{2,18},{10... | collective-permute-start | bytes 614408 | tf_op jit(solution)/shard_map/while/body/ppermute | solution.py:246
  37.8 3.8 %collective-permute-done.10.refs_4_ = bf16[1408,128]{1,0:T(8,128)(2,1)S(1)} collective-permute-done((bf16[1408,128]{1,0:T(8,128)(2,1)S(1)}, bf16[1408,128]{1,0:T(8,128)(2,1)S(1)}, u32[]{:S(2)}, u32[]{:S(2)}) %collective-permute-start.10) | collective-permute-done | bytes 360480 | tf_op jit(solution)/shard_map/while/body/ppermute | solution.py:254
  41.6 3.4 %collective-permute-start.11 = (bf16[1408,128]{1,0:T(8,128)(2,1)S(1)}, bf16[1408,128]{1,0:T(8,128)(2,1)S(1)}, u32[]{:S(2)}, u32[]{:S(2)}) collective-permute-start(bf16[1408,128]{1,0:T(8,128)(2,1)S(1)} %collective-permute-done.10.refs_4_), channel_id=1, source_target_pairs={{0,7},{1,0},{2,1},{3,2},{4,3},{5,4},{6,5},{7,6},{8,15},{9,8},{10,9... | collective-permute-start | bytes 1081352 | tf_op jit(solution)/shard_map/while/body/ppermute | solution.py:254
  49.1 4.0 %collective-permute-done.12.refs_10_ = bf16[80,1280]{1,0:T(8,128)(2,1)S(1)} collective-permute-done((bf16[80,1280]{1,0:T(8,128)(2,1)S(1)}, bf16[80,1280]{1,0:T(8,128)(2,1)S(1)}, u32[]{:S(2)}, u32[]{:S(2)}) %collective-permute-start.12) | collective-permute-done | bytes 204832 | tf_op jit(solution)/shard_map/while/body/ppermute | solution.py:246
  57.1 2.7 %collective-permute-start.16 = (bf16[1408,128]{1,0:T(8,128)(2,1)S(1)}, bf16[1408,128]{1,0:T(8,128)(2,1)S(1)}, u32[]{:S(2)}, u32[]{:S(2)}) collective-permute-start(bf16[1408,128]{1,0:T(8,128)(2,1)S(1)} %collective-permute-done.11.refs_8_), channel_id=1, source_target_pairs={{0,7},{1,0},{2,1},{3,2},{4,3},{5,4},{6,5},{7,6},{8,15},{9,8},{10,9... | collective-permute-start | bytes 1081352 | tf_op jit(solution)/shard_map/while/body/ppermute | solution.py:254
  59.8 6.0 %body.36.refs_8_ = bf16[5136,1280]{1,0:T(8,128)(2,1)S(1)} custom-call(s32[4]{0:T(128)S(1)} %get-tuple-element.792, s32[9,512]{1,0:T(8,128)S(1)} %get-tuple-element.791, bf16[1408,128]{1,0:T(8,128)(2,1)S(1)} %body.34.refs_0_, bf16[1408,128]{1,0:T(8,128)(2,1)S(1)} %collective-permute-done.17.refs_1_, bf16[1408,128]{1,0:T(8,128)(2,1)S(1)} %collective-permute-done.8.refs_2_, ...), custom_call_target="tpu_custom_call" | custom-call | flops 1000000000 | tf_op jit(solution)/shard_map/while/body/pallas_call | solution.py:267
  69.4 2.8 %collective-permute-start.26 = (bf16[640,128]{1,0:T(8,128)(2,1)S(1)}, bf16[640,128]{1,0:T(8,128)(2,1)S(1)}, u32[]{:S(2)}, u32[]{:S(2)}) collective-permute-start(bf16[640,128]{1,0:T(8,128)(2,1)S(1)} %get-tuple-element.597), channel_id=1, source_target_pairs={{0,7},{1,0},{2,1},{3,2},{4,3},{5,4},{6,5},{7,6},{8,15},{9,8},{10,9... | collective-permute-start | bytes 491528 | tf_op jit(solution)/shard_map/while/body/ppermute | solution.py:254
  77.8 6.4 %body.38 = (f32[80,1280]{1,0:T(8,128)S(1)}, bf16[80,1280]{1,0:T(8,128)(2,1)S(1)}, bf16[5136,1280]{1,0:T(8,128)(2,1)S(1)}) custom-call(s32[4]{0:T(128)S(1)} %get-tuple-element.792, s32[40,40]{1,0:T(8,128)S(1)} %copy-done.1, s32[9,512]{1,0:T(8,128)S(1)} %get-tuple-element.791, ...), custom_call_target="tpu_custom_call", output_to_operand_aliasing={{2}: (11, {})} | custom-call | flops 1000000000 | tf_op jit(solution)/shard_map/while/body/pallas_call | solution.py:267
  86.5 2.9 %collective-permute-start.29 = (bf16[80,1280]{1,0:T(8,128)(2,1)S(1)}, bf16[80,1280]{1,0:T(8,128)(2,1)S(1)}, u32[]{:S(2)}, u32[]{:S(2)}) collective-permute-start(bf16[80,1280]{1,0:T(8,128)(2,1)S(1)} %get-tuple-element.606.refs_0_), channel_id=1, source_target_pairs={{0,16},{8,24},{16,0},{24,8},{1,17},{9,25},{17,1},{25,9},{2,18},{10... | collective-permute-start | bytes 614408 | tf_op jit(solution)/shard_map/while/body/ppermute | solution.py:246
  90.7 2.7 %collective-permute-done.30.refs_3_ = bf16[80,1280]{1,0:T(8,128)(2,1)S(1)} collective-permute-done((bf16[80,1280]{1,0:T(8,128)(2,1)S(1)}, bf16[80,1280]{1,0:T(8,128)(2,1)S(1)}, u32[]{:S(2)}, u32[]{:S(2)}) %collective-permute-start.30) | collective-permute-done | bytes 204832 | tf_op jit(solution)/shard_map/while/body/ppermute | solution.py:246
  93.4 5.3 %collective-permute-done.29.refs_2_ = bf16[80,1280]{1,0:T(8,128)(2,1)S(1)} collective-permute-done((bf16[80,1280]{1,0:T(8,128)(2,1)S(1)}, bf16[80,1280]{1,0:T(8,128)(2,1)S(1)}, u32[]{:S(2)}, u32[]{:S(2)}) %collective-permute-start.29) | collective-permute-done | bytes 204832 | tf_op jit(solution)/shard_map/while/body/ppermute | solution.py:246
  98.6 4.2 %body.39 = (f32[80,1280]{1,0:T(8,128)}, bf16[80,1280]{1,0:T(8,128)(2,1)S(1)}) custom-call(s32[4]{0:T(128)S(1)} %get-tuple-element.792, s32[40,40]{1,0:T(8,128)S(1)} %copy-done.1, f32[80,1280]{1,0:T(8,128)S(1)} %get-tuple-element.604.square, bf16[5136,1280]{1,0:T(8,128)(2,1)S(1)} %get-tuple-element.605.panel, ...), custom_call_target="tpu_custom_call" | custom-call | flops 1000000000 | tf_op jit(solution)/shard_map/while/body/pallas_call | solution.py:267
  109.7 6.2 %collective-permute-start.7 = (bf16[80,1280]{1,0:T(8,128)(2,1)S(1)}, bf16[80,1280]{1,0:T(8,128)(2,1)S(1)}, u32[]{:S(2)}, u32[]{:S(2)}) collective-permute-start(bf16[80,1280]{1,0:T(8,128)(2,1)S(1)} %collective-permute-done.3.refs_3_), channel_id=1, source_target_pairs={{0,32},{32,0},{64,96},{96,64},{128,160},{160,128},{192,224},{224,1... | collective-permute-start | bytes 614408 | tf_op jit(solution)/shard_map/while/body/ppermute | solution.py:258
  119.9 3.1 %collective-permute-start.10 = (bf16[1408,128]{1,0:T(8,128)(2,1)S(1)}, bf16[1408,128]{1,0:T(8,128)(2,1)S(1)}, u32[]{:S(2)}, u32[]{:S(2)}) collective-permute-start(bf16[1408,128]{1,0:T(8,128)(2,1)S(1)} %body.34.refs_0_), channel_id=1, source_target_pairs={{0,7},{1,0},{2,1},{3,2},{4,3},{5,4},{6,5},{7,6},{8,15},{9,8},{10,9... | collective-permute-start | bytes 1081352 | tf_op jit(solution)/shard_map/while/body/ppermute | solution.py:254
  123.9 2.9 %collective-permute-start.13 = (bf16[80,1280]{1,0:T(8,128)(2,1)S(1)}, bf16[80,1280]{1,0:T(8,128)(2,1)S(1)}, u32[]{:S(2)}, u32[]{:S(2)}) collective-permute-start(bf16[80,1280]{1,0:T(8,128)(2,1)S(1)} %get-tuple-element.777), channel_id=1, source_target_pairs={{0,16},{8,24},{16,0},{24,8},{1,17},{9,25},{17,1},{25,9},{2,18},{10... | collective-permute-start | bytes 614408 | tf_op jit(solution)/shard_map/while/body/ppermute | solution.py:246
  126.8 3.7 %collective-permute-done.10.refs_4_ = bf16[1408,128]{1,0:T(8,128)(2,1)S(1)} collective-permute-done((bf16[1408,128]{1,0:T(8,128)(2,1)S(1)}, bf16[1408,128]{1,0:T(8,128)(2,1)S(1)}, u32[]{:S(2)}, u32[]{:S(2)}) %collective-permute-start.10) | collective-permute-done | bytes 360480 | tf_op jit(solution)/shard_map/while/body/ppermute | solution.py:254
  130.5 3.4 %collective-permute-start.11 = (bf16[1408,128]{1,0:T(8,128)(2,1)S(1)}, bf16[1408,128]{1,0:T(8,128)(2,1)S(1)}, u32[]{:S(2)}, u32[]{:S(2)}) collective-permute-start(bf16[1408,128]{1,0:T(8,128)(2,1)S(1)} %collective-permute-done.10.refs_4_), channel_id=1, source_target_pairs={{0,7},{1,0},{2,1},{3,2},{4,3},{5,4},{6,5},{7,6},{8,15},{9,8},{10,9... | collective-permute-start | bytes 1081352 | tf_op jit(solution)/shard_map/while/body/ppermute | solution.py:254
  138.1 4.0 %collective-permute-done.12.refs_10_ = bf16[80,1280]{1,0:T(8,128)(2,1)S(1)} collective-permute-done((bf16[80,1280]{1,0:T(8,128)(2,1)S(1)}, bf16[80,1280]{1,0:T(8,128)(2,1)S(1)}, u32[]{:S(2)}, u32[]{:S(2)}) %collective-permute-start.12) | collective-permute-done | bytes 204832 | tf_op jit(solution)/shard_map/while/body/ppermute | solution.py:246
  146.0 2.7 %collective-permute-start.16 = (bf16[1408,128]{1,0:T(8,128)(2,1)S(1)}, bf16[1408,128]{1,0:T(8,128)(2,1)S(1)}, u32[]{:S(2)}, u32[]{:S(2)}) collective-permute-start(bf16[1408,128]{1,0:T(8,128)(2,1)S(1)} %collective-permute-done.11.refs_8_), channel_id=1, source_target_pairs={{0,7},{1,0},{2,1},{3,2},{4,3},{5,4},{6,5},{7,6},{8,15},{9,8},{10,9... | collective-permute-start | bytes 1081352 | tf_op jit(solution)/shard_map/while/body/ppermute | solution.py:254
  148.6 6.0 %body.36.refs_8_ = bf16[5136,1280]{1,0:T(8,128)(2,1)S(1)} custom-call(s32[4]{0:T(128)S(1)} %get-tuple-element.792, s32[9,512]{1,0:T(8,128)S(1)} %get-tuple-element.791, bf16[1408,128]{1,0:T(8,128)(2,1)S(1)} %body.34.refs_0_, bf16[1408,128]{1,0:T(8,128)(2,1)S(1)} %collective-permute-done.17.refs_1_, bf16[1408,128]{1,0:T(8,128)(2,1)S(1)} %collective-permute-done.8.refs_2_, ...), custom_call_target="tpu_custom_call" | custom-call | flops 1000000000 | tf_op jit(solution)/shard_map/while/body/pallas_call | solution.py:267
  158.3 2.8 %collective-permute-start.26 = (bf16[640,128]{1,0:T(8,128)(2,1)S(1)}, bf16[640,128]{1,0:T(8,128)(2,1)S(1)}, u32[]{:S(2)}, u32[]{:S(2)}) collective-permute-start(bf16[640,128]{1,0:T(8,128)(2,1)S(1)} %get-tuple-element.597), channel_id=1, source_target_pairs={{0,7},{1,0},{2,1},{3,2},{4,3},{5,4},{6,5},{7,6},{8,15},{9,8},{10,9... | collective-permute-start | bytes 491528 | tf_op jit(solution)/shard_map/while/body/ppermute | solution.py:254
  166.7 6.4 %body.38 = (f32[80,1280]{1,0:T(8,128)S(1)}, bf16[80,1280]{1,0:T(8,128)(2,1)S(1)}, bf16[5136,1280]{1,0:T(8,128)(2,1)S(1)}) custom-call(s32[4]{0:T(128)S(1)} %get-tuple-element.792, s32[40,40]{1,0:T(8,128)S(1)} %copy-done.1, s32[9,512]{1,0:T(8,128)S(1)} %get-tuple-element.791, ...), custom_call_target="tpu_custom_call", output_to_operand_aliasing={{2}: (11, {})} | custom-call | flops 1000000000 | tf_op jit(solution)/shard_map/while/body/pallas_call | solution.py:267
  175.1 3.3 %collective-permute-start.29 = (bf16[80,1280]{1,0:T(8,128)(2,1)S(1)}, bf16[80,1280]{1,0:T(8,128)(2,1)S(1)}, u32[]{:S(2)}, u32[]{:S(2)}) collective-permute-start(bf16[80,1280]{1,0:T(8,128)(2,1)S(1)} %get-tuple-element.606.refs_0_), channel_id=1, source_target_pairs={{0,16},{8,24},{16,0},{24,8},{1,17},{9,25},{17,1},{25,9},{2,18},{10... | collective-permute-start | bytes 614408 | tf_op jit(solution)/shard_map/while/body/ppermute | solution.py:246
  178.9 3.4 %collective-permute-done.30.refs_3_ = bf16[80,1280]{1,0:T(8,128)(2,1)S(1)} collective-permute-done((bf16[80,1280]{1,0:T(8,128)(2,1)S(1)}, bf16[80,1280]{1,0:T(8,128)(2,1)S(1)}, u32[]{:S(2)}, u32[]{:S(2)}) %collective-permute-start.30) | collective-permute-done | bytes 204832 | tf_op jit(solution)/shard_map/while/body/ppermute | solution.py:246
  182.3 5.3 %collective-permute-done.29.refs_2_ = bf16[80,1280]{1,0:T(8,128)(2,1)S(1)} collective-permute-done((bf16[80,1280]{1,0:T(8,128)(2,1)S(1)}, bf16[80,1280]{1,0:T(8,128)(2,1)S(1)}, u32[]{:S(2)}, u32[]{:S(2)}) %collective-permute-start.29) | collective-permute-done | bytes 204832 | tf_op jit(solution)/shard_map/while/body/ppermute | solution.py:246
  187.6 4.2 %body.39 = (f32[80,1280]{1,0:T(8,128)}, bf16[80,1280]{1,0:T(8,128)(2,1)S(1)}) custom-call(s32[4]{0:T(128)S(1)} %get-tuple-element.792, s32[40,40]{1,0:T(8,128)S(1)} %copy-done.1, f32[80,1280]{1,0:T(8,128)S(1)} %get-tuple-element.604.square, bf16[5136,1280]{1,0:T(8,128)(2,1)S(1)} %get-tuple-element.605.panel, ...), custom_call_target="tpu_custom_call" | custom-call | flops 1000000000 | tf_op jit(solution)/shard_map/while/body/pallas_call | solution.py:267
  (123 shorter events, 66.5 us)
Async XLA Ops:
  11.8 11.5 %collective-permute-start.2 = (bf16[80,1280]{1,0:T(8,128)(2,1)S(1)}, bf16[80,1280]{1,0:T(8,128)(2,1)S(1)}, u32[]{:S(2)}, u32[]{:S(2)}) collective-permute-start(bf16[80,1280]{1,0:T(8,128)(2,1)S(1)} %get-tuple-element.599.refs_0_.refs_9_), channel_id=1, source_target_pairs={{0,128},{32,160},{64,192},{96,224},{128,0},{160,32},{192,64},{224,... | collective-permute-start | bytes 614408 | tf_op jit(solution)/shard_map/while/body/ppermute | solution.py:250
  14.4 10.4 %collective-permute-start.1 = (bf16[80,1280]{1,0:T(8,128)(2,1)S(1)}, bf16[80,1280]{1,0:T(8,128)(2,1)S(1)}, u32[]{:S(2)}, u32[]{:S(2)}) collective-permute-start(bf16[80,1280]{1,0:T(8,128)(2,1)S(1)} %get-tuple-element.599.refs_0_.refs_9_), channel_id=1, source_target_pairs={{0,192},{32,224},{64,0},{96,32},{128,64},{160,96},{192,128},{224,1... | collective-permute-start | bytes 614408 | tf_op jit(solution)/shard_map/while/body/ppermute | solution.py:250
  15.5 9.4 %collective-permute-start.4 = (bf16[80,1280]{1,0:T(8,128)(2,1)S(1)}, bf16[80,1280]{1,0:T(8,128)(2,1)S(1)}, u32[]{:S(2)}, u32[]{:S(2)}) collective-permute-start(bf16[80,1280]{1,0:T(8,128)(2,1)S(1)} %get-tuple-element.599.refs_0_.refs_9_), channel_id=1, source_target_pairs={{0,32},{32,0},{64,96},{96,64},{128,160},{160,128},{192,224},{224,1... | collective-permute-start | bytes 614408 | tf_op jit(solution)/shard_map/while/body/ppermute | solution.py:258
  28.5 13.1 %collective-permute-start.10 = (bf16[1408,128]{1,0:T(8,128)(2,1)S(1)}, bf16[1408,128]{1,0:T(8,128)(2,1)S(1)}, u32[]{:S(2)}, u32[]{:S(2)}) collective-permute-start(bf16[1408,128]{1,0:T(8,128)(2,1)S(1)} %body.34.refs_0_), channel_id=1, source_target_pairs={{0,7},{1,0},{2,1},{3,2},{4,3},{5,4},{6,5},{7,6},{8,15},{9,8},{10,9... | collective-permute-start | bytes 1081352 | tf_op jit(solution)/shard_map/while/body/ppermute | solution.py:254
  34.1 10.9 %collective-permute-start.8 = (bf16[1408,128]{1,0:T(8,128)(2,1)S(1)}, bf16[1408,128]{1,0:T(8,128)(2,1)S(1)}, u32[]{:S(2)}, u32[]{:S(2)}) collective-permute-start(bf16[1408,128]{1,0:T(8,128)(2,1)S(1)} %body.34.refs_0_), channel_id=1, source_target_pairs={{0,1},{1,2},{2,3},{3,4},{4,5},{5,6},{6,7},{7,0},{8,9},{9,10},{10,1... | collective-permute-start | bytes 1081352 | tf_op jit(solution)/shard_map/while/body/ppermute | solution.py:254
  34.1 12.3 %collective-permute-start.14 = (bf16[80,1280]{1,0:T(8,128)(2,1)S(1)}, bf16[80,1280]{1,0:T(8,128)(2,1)S(1)}, u32[]{:S(2)}, u32[]{:S(2)}) collective-permute-start(bf16[80,1280]{1,0:T(8,128)(2,1)S(1)} %get-tuple-element.777), channel_id=1, source_target_pairs={{0,8},{8,16},{16,24},{24,0},{1,9},{9,17},{17,25},{25,1},{2,10},{10... | collective-permute-start | bytes 614408 | tf_op jit(solution)/shard_map/while/body/ppermute | solution.py:246
  35.4 11.4 %collective-permute-start.13 = (bf16[80,1280]{1,0:T(8,128)(2,1)S(1)}, bf16[80,1280]{1,0:T(8,128)(2,1)S(1)}, u32[]{:S(2)}, u32[]{:S(2)}) collective-permute-start(bf16[80,1280]{1,0:T(8,128)(2,1)S(1)} %get-tuple-element.777), channel_id=1, source_target_pairs={{0,16},{8,24},{16,0},{24,8},{1,17},{9,25},{17,1},{25,9},{2,18},{10... | collective-permute-start | bytes 614408 | tf_op jit(solution)/shard_map/while/body/ppermute | solution.py:246
  41.6 12.7 %collective-permute-start.11 = (bf16[1408,128]{1,0:T(8,128)(2,1)S(1)}, bf16[1408,128]{1,0:T(8,128)(2,1)S(1)}, u32[]{:S(2)}, u32[]{:S(2)}) collective-permute-start(bf16[1408,128]{1,0:T(8,128)(2,1)S(1)} %collective-permute-done.10.refs_4_), channel_id=1, source_target_pairs={{0,7},{1,0},{2,1},{3,2},{4,3},{5,4},{6,5},{7,6},{8,15},{9,8},{10,9... | collective-permute-start | bytes 1081352 | tf_op jit(solution)/shard_map/while/body/ppermute | solution.py:254
  45.0 9.8 %collective-permute-start.9 = (bf16[1408,128]{1,0:T(8,128)(2,1)S(1)}, bf16[1408,128]{1,0:T(8,128)(2,1)S(1)}, u32[]{:S(2)}, u32[]{:S(2)}) collective-permute-start(bf16[1408,128]{1,0:T(8,128)(2,1)S(1)} %collective-permute-done.8.refs_2_), channel_id=1, source_target_pairs={{0,1},{1,2},{2,3},{3,4},{4,5},{5,6},{6,7},{7,0},{8,9},{9,10},{10,1... | collective-permute-start | bytes 1081352 | tf_op jit(solution)/shard_map/while/body/ppermute | solution.py:254
  45.0 12.0 %collective-permute-start.17 = (bf16[1408,128]{1,0:T(8,128)(2,1)S(1)}, bf16[1408,128]{1,0:T(8,128)(2,1)S(1)}, u32[]{:S(2)}, u32[]{:S(2)}) collective-permute-start(bf16[1408,128]{1,0:T(8,128)(2,1)S(1)} %body.34.refs_0_), channel_id=1, source_target_pairs={{0,32},{32,0},{64,96},{96,64},{128,160},{160,128},{192,224},{224,1... | collective-permute-start | bytes 1081352 | tf_op jit(solution)/shard_map/while/body/ppermute | solution.py:258
  46.5 10.6 %collective-permute-start.19 = (bf16[1408,128]{1,0:T(8,128)(2,1)S(1)}, bf16[1408,128]{1,0:T(8,128)(2,1)S(1)}, u32[]{:S(2)}, u32[]{:S(2)}) collective-permute-start(bf16[1408,128]{1,0:T(8,128)(2,1)S(1)} %collective-permute-done.10.refs_4_), channel_id=1, source_target_pairs={{0,32},{32,0},{64,96},{96,64},{128,160},{160,128},{192,224},{224,1... | collective-permute-start | bytes 1081352 | tf_op jit(solution)/shard_map/while/body/ppermute | solution.py:258
  57.1 10.7 %collective-permute-start.15 = (bf16[1408,128]{1,0:T(8,128)(2,1)S(1)}, bf16[1408,128]{1,0:T(8,128)(2,1)S(1)}, u32[]{:S(2)}, u32[]{:S(2)}) collective-permute-start(bf16[1408,128]{1,0:T(8,128)(2,1)S(1)} %collective-permute-done.9.refs_6_), channel_id=1, source_target_pairs={{0,1},{1,2},{2,3},{3,4},{4,5},{5,6},{6,7},{7,0},{8,9},{9,10},{10,1... | collective-permute-start | bytes 1081352 | tf_op jit(solution)/shard_map/while/body/ppermute | solution.py:254
  57.1 10.7 %collective-permute-start.16 = (bf16[1408,128]{1,0:T(8,128)(2,1)S(1)}, bf16[1408,128]{1,0:T(8,128)(2,1)S(1)}, u32[]{:S(2)}, u32[]{:S(2)}) collective-permute-start(bf16[1408,128]{1,0:T(8,128)(2,1)S(1)} %collective-permute-done.11.refs_8_), channel_id=1, source_target_pairs={{0,7},{1,0},{2,1},{3,2},{4,3},{5,4},{6,5},{7,6},{8,15},{9,8},{10,9... | collective-permute-start | bytes 1081352 | tf_op jit(solution)/shard_map/while/body/ppermute | solution.py:254
  67.9 9.9 %collective-permute-start.22 = (bf16[1408,128]{1,0:T(8,128)(2,1)S(1)}, bf16[1408,128]{1,0:T(8,128)(2,1)S(1)}, u32[]{:S(2)}, u32[]{:S(2)}) collective-permute-start(bf16[1408,128]{1,0:T(8,128)(2,1)S(1)} %collective-permute-done.15.down.refs_0_), channel_id=1, source_target_pairs={{0,32},{32,0},{64,96},{96,64},{128,160},{160,128},{192,224},{224,1... | collective-permute-start | bytes 1081352 | tf_op jit(solution)/shard_map/while/body/ppermute | solution.py:258
  86.5 12.1 %collective-permute-start.29 = (bf16[80,1280]{1,0:T(8,128)(2,1)S(1)}, bf16[80,1280]{1,0:T(8,128)(2,1)S(1)}, u32[]{:S(2)}, u32[]{:S(2)}) collective-permute-start(bf16[80,1280]{1,0:T(8,128)(2,1)S(1)} %get-tuple-element.606.refs_0_), channel_id=1, source_target_pairs={{0,16},{8,24},{16,0},{24,8},{1,17},{9,25},{17,1},{25,9},{2,18},{10... | collective-permute-start | bytes 614408 | tf_op jit(solution)/shard_map/while/body/ppermute | solution.py:246
  89.4 9.3 %collective-permute-start.28 = (bf16[80,1280]{1,0:T(8,128)(2,1)S(1)}, bf16[80,1280]{1,0:T(8,128)(2,1)S(1)}, u32[]{:S(2)}, u32[]{:S(2)}) collective-permute-start(bf16[80,1280]{1,0:T(8,128)(2,1)S(1)} %get-tuple-element.606.refs_0_), channel_id=1, source_target_pairs={{0,24},{8,0},{16,8},{24,16},{1,25},{9,1},{17,9},{25,17},{2,26},{10... | collective-permute-start | bytes 614408 | tf_op jit(solution)/shard_map/while/body/ppermute | solution.py:246
  103.3 12.7 %collective-permute-start.2 = (bf16[80,1280]{1,0:T(8,128)(2,1)S(1)}, bf16[80,1280]{1,0:T(8,128)(2,1)S(1)}, u32[]{:S(2)}, u32[]{:S(2)}) collective-permute-start(bf16[80,1280]{1,0:T(8,128)(2,1)S(1)} %get-tuple-element.599.refs_0_.refs_9_), channel_id=1, source_target_pairs={{0,128},{32,160},{64,192},{96,224},{128,0},{160,32},{192,64},{224,... | collective-permute-start | bytes 614408 | tf_op jit(solution)/shard_map/while/body/ppermute | solution.py:250
  105.4 10.6 %collective-permute-start.1 = (bf16[80,1280]{1,0:T(8,128)(2,1)S(1)}, bf16[80,1280]{1,0:T(8,128)(2,1)S(1)}, u32[]{:S(2)}, u32[]{:S(2)}) collective-permute-start(bf16[80,1280]{1,0:T(8,128)(2,1)S(1)} %get-tuple-element.599.refs_0_.refs_9_), channel_id=1, source_target_pairs={{0,192},{32,224},{64,0},{96,32},{128,64},{160,96},{192,128},{224,1... | collective-permute-start | bytes 614408 | tf_op jit(solution)/shard_map/while/body/ppermute | solution.py:250
  106.8 9.8 %collective-permute-start.4 = (bf16[80,1280]{1,0:T(8,128)(2,1)S(1)}, bf16[80,1280]{1,0:T(8,128)(2,1)S(1)}, u32[]{:S(2)}, u32[]{:S(2)}) collective-permute-start(bf16[80,1280]{1,0:T(8,128)(2,1)S(1)} %get-tuple-element.599.refs_0_.refs_9_), channel_id=1, source_target_pairs={{0,32},{32,0},{64,96},{96,64},{128,160},{160,128},{192,224},{224,1... | collective-permute-start | bytes 614408 | tf_op jit(solution)/shard_map/while/body/ppermute | solution.py:258
  119.9 10.6 %collective-permute-start.10 = (bf16[1408,128]{1,0:T(8,128)(2,1)S(1)}, bf16[1408,128]{1,0:T(8,128)(2,1)S(1)}, u32[]{:S(2)}, u32[]{:S(2)}) collective-permute-start(bf16[1408,128]{1,0:T(8,128)(2,1)S(1)} %body.34.refs_0_), channel_id=1, source_target_pairs={{0,7},{1,0},{2,1},{3,2},{4,3},{5,4},{6,5},{7,6},{8,15},{9,8},{10,9... | collective-permute-start | bytes 1081352 | tf_op jit(solution)/shard_map/while/body/ppermute | solution.py:254
  123.0 10.9 %collective-permute-start.8 = (bf16[1408,128]{1,0:T(8,128)(2,1)S(1)}, bf16[1408,128]{1,0:T(8,128)(2,1)S(1)}, u32[]{:S(2)}, u32[]{:S(2)}) collective-permute-start(bf16[1408,128]{1,0:T(8,128)(2,1)S(1)} %body.34.refs_0_), channel_id=1, source_target_pairs={{0,1},{1,2},{2,3},{3,4},{4,5},{5,6},{6,7},{7,0},{8,9},{9,10},{10,1... | collective-permute-start | bytes 1081352 | tf_op jit(solution)/shard_map/while/body/ppermute | solution.py:254
  123.0 12.3 %collective-permute-start.14 = (bf16[80,1280]{1,0:T(8,128)(2,1)S(1)}, bf16[80,1280]{1,0:T(8,128)(2,1)S(1)}, u32[]{:S(2)}, u32[]{:S(2)}) collective-permute-start(bf16[80,1280]{1,0:T(8,128)(2,1)S(1)} %get-tuple-element.777), channel_id=1, source_target_pairs={{0,8},{8,16},{16,24},{24,0},{1,9},{9,17},{17,25},{25,1},{2,10},{10... | collective-permute-start | bytes 614408 | tf_op jit(solution)/shard_map/while/body/ppermute | solution.py:246
  123.9 11.8 %collective-permute-start.13 = (bf16[80,1280]{1,0:T(8,128)(2,1)S(1)}, bf16[80,1280]{1,0:T(8,128)(2,1)S(1)}, u32[]{:S(2)}, u32[]{:S(2)}) collective-permute-start(bf16[80,1280]{1,0:T(8,128)(2,1)S(1)} %get-tuple-element.777), channel_id=1, source_target_pairs={{0,16},{8,24},{16,0},{24,8},{1,17},{9,25},{17,1},{25,9},{2,18},{10... | collective-permute-start | bytes 614408 | tf_op jit(solution)/shard_map/while/body/ppermute | solution.py:246
  130.5 12.9 %collective-permute-start.11 = (bf16[1408,128]{1,0:T(8,128)(2,1)S(1)}, bf16[1408,128]{1,0:T(8,128)(2,1)S(1)}, u32[]{:S(2)}, u32[]{:S(2)}) collective-permute-start(bf16[1408,128]{1,0:T(8,128)(2,1)S(1)} %collective-permute-done.10.refs_4_), channel_id=1, source_target_pairs={{0,7},{1,0},{2,1},{3,2},{4,3},{5,4},{6,5},{7,6},{8,15},{9,8},{10,9... | collective-permute-start | bytes 1081352 | tf_op jit(solution)/shard_map/while/body/ppermute | solution.py:254
  133.9 9.8 %collective-permute-start.9 = (bf16[1408,128]{1,0:T(8,128)(2,1)S(1)}, bf16[1408,128]{1,0:T(8,128)(2,1)S(1)}, u32[]{:S(2)}, u32[]{:S(2)}) collective-permute-start(bf16[1408,128]{1,0:T(8,128)(2,1)S(1)} %collective-permute-done.8.refs_2_), channel_id=1, source_target_pairs={{0,1},{1,2},{2,3},{3,4},{4,5},{5,6},{6,7},{7,0},{8,9},{9,10},{10,1... | collective-permute-start | bytes 1081352 | tf_op jit(solution)/shard_map/while/body/ppermute | solution.py:254
  133.9 12.0 %collective-permute-start.17 = (bf16[1408,128]{1,0:T(8,128)(2,1)S(1)}, bf16[1408,128]{1,0:T(8,128)(2,1)S(1)}, u32[]{:S(2)}, u32[]{:S(2)}) collective-permute-start(bf16[1408,128]{1,0:T(8,128)(2,1)S(1)} %body.34.refs_0_), channel_id=1, source_target_pairs={{0,32},{32,0},{64,96},{96,64},{128,160},{160,128},{192,224},{224,1... | collective-permute-start | bytes 1081352 | tf_op jit(solution)/shard_map/while/body/ppermute | solution.py:258
  135.3 10.6 %collective-permute-start.19 = (bf16[1408,128]{1,0:T(8,128)(2,1)S(1)}, bf16[1408,128]{1,0:T(8,128)(2,1)S(1)}, u32[]{:S(2)}, u32[]{:S(2)}) collective-permute-start(bf16[1408,128]{1,0:T(8,128)(2,1)S(1)} %collective-permute-done.10.refs_4_), channel_id=1, source_target_pairs={{0,32},{32,0},{64,96},{96,64},{128,160},{160,128},{192,224},{224,1... | collective-permute-start | bytes 1081352 | tf_op jit(solution)/shard_map/while/body/ppermute | solution.py:258
  145.9 10.7 %collective-permute-start.15 = (bf16[1408,128]{1,0:T(8,128)(2,1)S(1)}, bf16[1408,128]{1,0:T(8,128)(2,1)S(1)}, u32[]{:S(2)}, u32[]{:S(2)}) collective-permute-start(bf16[1408,128]{1,0:T(8,128)(2,1)S(1)} %collective-permute-done.9.refs_6_), channel_id=1, source_target_pairs={{0,1},{1,2},{2,3},{3,4},{4,5},{5,6},{6,7},{7,0},{8,9},{9,10},{10,1... | collective-permute-start | bytes 1081352 | tf_op jit(solution)/shard_map/while/body/ppermute | solution.py:254
  146.0 10.7 %collective-permute-start.16 = (bf16[1408,128]{1,0:T(8,128)(2,1)S(1)}, bf16[1408,128]{1,0:T(8,128)(2,1)S(1)}, u32[]{:S(2)}, u32[]{:S(2)}) collective-permute-start(bf16[1408,128]{1,0:T(8,128)(2,1)S(1)} %collective-permute-done.11.refs_8_), channel_id=1, source_target_pairs={{0,7},{1,0},{2,1},{3,2},{4,3},{5,4},{6,5},{7,6},{8,15},{9,8},{10,9... | collective-permute-start | bytes 1081352 | tf_op jit(solution)/shard_map/while/body/ppermute | solution.py:254
  156.7 9.9 %collective-permute-start.22 = (bf16[1408,128]{1,0:T(8,128)(2,1)S(1)}, bf16[1408,128]{1,0:T(8,128)(2,1)S(1)}, u32[]{:S(2)}, u32[]{:S(2)}) collective-permute-start(bf16[1408,128]{1,0:T(8,128)(2,1)S(1)} %collective-permute-done.15.down.refs_0_), channel_id=1, source_target_pairs={{0,32},{32,0},{64,96},{96,64},{128,160},{160,128},{192,224},{224,1... | collective-permute-start | bytes 1081352 | tf_op jit(solution)/shard_map/while/body/ppermute | solution.py:258
  175.1 12.5 %collective-permute-start.29 = (bf16[80,1280]{1,0:T(8,128)(2,1)S(1)}, bf16[80,1280]{1,0:T(8,128)(2,1)S(1)}, u32[]{:S(2)}, u32[]{:S(2)}) collective-permute-start(bf16[80,1280]{1,0:T(8,128)(2,1)S(1)} %get-tuple-element.606.refs_0_), channel_id=1, source_target_pairs={{0,16},{8,24},{16,0},{24,8},{1,17},{9,25},{17,1},{25,9},{2,18},{10... | collective-permute-start | bytes 614408 | tf_op jit(solution)/shard_map/while/body/ppermute | solution.py:246
  178.3 9.3 %collective-permute-start.28 = (bf16[80,1280]{1,0:T(8,128)(2,1)S(1)}, bf16[80,1280]{1,0:T(8,128)(2,1)S(1)}, u32[]{:S(2)}, u32[]{:S(2)}) collective-permute-start(bf16[80,1280]{1,0:T(8,128)(2,1)S(1)} %get-tuple-element.606.refs_0_), channel_id=1, source_target_pairs={{0,24},{8,0},{16,8},{24,16},{1,25},{9,1},{17,9},{25,17},{2,26},{10... | collective-permute-start | bytes 614408 | tf_op jit(solution)/shard_map/while/body/ppermute | solution.py:246
  (35 other events, 439.1 us)

commit v2 on v1

--- a/solution.py
+++ b/solution.py
@@ -199,14 +199,20 @@
         place(table, q // 2, core, ref, panel, 0, CAPACITY)
 
 
-def square_kernel(pos, pat, table, *refs):
-    packed, left, spill = refs[:8], refs[9:13], refs[13]
-    (square, square_half, panel), (total, more) = refs[14:17], refs[17:]
+def third_kernel(pos, table, *refs):
+    packed, panel = refs[:4], refs[5]
     for q, ref in enumerate(packed):
         core = pos[1] if q % 2 == 0 else 1 - pos[1]
-        m = (5, 6, 7, 7)[q // 2]
-        first, last = ((0, CAPACITY), (0, CAPACITY), (0, SPLIT), (SPLIT, CAPACITY))[q // 2]
-        place(table, m, core, ref, panel, first, last)
+        place(table, 5 + q // 2, core, ref, panel, 0, CAPACITY)
+
+
+def square_kernel(pos, pat, table, *refs):
+    packed, left, spill = refs[:4], refs[5:9], refs[9]
+    (square, square_half, panel), (total, more) = refs[10:13], refs[13:]
+    for q, ref in enumerate(packed):
+        core = pos[1] if q % 2 == 0 else 1 - pos[1]
+        first, last = ((0, SPLIT), (SPLIT, CAPACITY))[q // 2]
+        place(table, NZ - 1, core, ref, panel, first, last)
     for m in range(NZ):
 
         @pl.when(table[m, SLOTS - 1] > 2 * CAPACITY)
@@ -290,12 +296,30 @@
     pass
 
 
+def tables(pos, pat):
+    return pl.pallas_call(
+        table_kernel,
+        out_shape=(
+            jax.ShapeDtypeStruct((NZ + 1, SLOTS), jnp.int32),
+            jax.ShapeDtypeStruct((1,), jnp.int32),
+        ),
+        in_specs=[SMEM, VMEM],
+        out_specs=[VMEM, SMEM],
+        compiler_params=PARAMS,
+        cost_estimate=pl.CostEstimate(flops=10**9, bytes_accessed=0, transcendentals=0),
+    )(pos, pat)
+
+
+def unset(shape, dtype):
+    return pl.pallas_call(
+        nothing_kernel, out_shape=jax.ShapeDtypeStruct(shape, dtype), out_specs=HBM
+    )()
+
+
 def spilled(pos, most, table, blocks):
     rounds = (most[0] - 2 * CAPACITY + 2 * EXTRA - 1) // (2 * EXTRA)
     shape = (2, NZ, ROUNDS * EXTRA * SUB, TILE)
-    empty = pl.pallas_call(
-        nothing_kernel, out_shape=jax.ShapeDtypeStruct(shape, jnp.bfloat16), out_specs=HBM
-    )()
+    empty = unset(shape, jnp.bfloat16)
 
     def one_round(carry):
         turn, spill = carry
@@ -307,7 +331,7 @@
     return lax.while_loop(lambda carry: carry[0] < rounds, one_round, (jnp.int32(0), empty))[1]
 
 
-def steps(pos, pat, current, table, most):
+def steps(pos, pat, current):
     f32 = jax.ShapeDtypeStruct((SHARE, WIDTH), jnp.float32)
     bf16 = jax.ShapeDtypeStruct((SHARE, WIDTH), jnp.bfloat16)
     panel_shape = jax.ShapeDtypeStruct((ORDER + SUB, WIDTH), jnp.bfloat16)
@@ -318,6 +342,8 @@
     def step(carry):
         turn, current = carry[:2]
         blocks = [current, along_y(current, -1), along_y(current, 2), along_y(current, 1)]
+        here, _ = lax.optimization_barrier((pos, current))
+        table, most, *blocks = lax.optimization_barrier((*tables(here, pat), *blocks))
         blocks += map(other_core, blocks[:4])
         packed = pack(CAPACITY, pos, 0, table, blocks)
         spill = spilled(pos, most, table, blocks)
@@ -334,7 +360,12 @@
         last_part = jax.ShapeDtypeStruct((CAPACITY * SUB - split, TILE), jnp.bfloat16)
         part_a, part_b = call(parts_kernel, (first_part, last_part), 0, down3, up3)
         far_a, far_b = along_z(part_a, 1), along_z(part_b, -1)
-        far = [both for one in (down3, up3, far_a, far_b) for both in (one, other_core(one))]
+        third = [both for one in (down3, up3) for both in (one, other_core(one))]
+        panel = call(
+            third_kernel, panel_shape, 2, pos, table, *third, panel, aliases={6: 0}, flops=10**9
+        )
+        far_a, far_b, panel = lax.optimization_barrier((far_a, far_b, panel))
+        far = [both for one in (far_a, far_b) for both in (one, other_core(one))]
         square, square_half, panel = call(
             square_kernel,
             (f32, bf16, panel_shape),
@@ -342,7 +373,7 @@
             *(pos, pat, table, *far, panel, *left, spill),
             scratch=(total, more),
             n_hbm=1,
-            aliases={11: 2},
+            aliases={7: 2},
             flops=10**9,
         )
         left = whole_rows(square_half)
@@ -356,7 +387,7 @@
         )
         return turn, following, result
 
-    first = (jnp.int32(0), current, jnp.zeros((SHARE, WIDTH), jnp.float32))
+    first = (jnp.int32(0), current, unset((SHARE, WIDTH), jnp.float32))
     return lax.while_loop(lambda carry: carry[0] < STEPS, step, first)[2]
 
 
@@ -365,17 +396,7 @@
     pos = jnp.stack([row // 2, row % 2, x, z]).astype(jnp.int32)
     share = jax.ShapeDtypeStruct((SHARE, WIDTH), jnp.bfloat16)
     current = call(start_kernel, share, 5, pos, tile_pattern, n_occ, mu, gamma, hamiltonian)
-    table, most = pl.pallas_call(
-        table_kernel,
-        out_shape=(
-            jax.ShapeDtypeStruct((NZ + 1, SLOTS), jnp.int32),
-            jax.ShapeDtypeStruct((1,), jnp.int32),
-        ),
-        in_specs=[SMEM, VMEM],
-        out_specs=[VMEM, SMEM],
-        compiler_params=PARAMS,
-    )(pos, tile_pattern)
-    return steps(pos, tile_pattern, current, table, most)
+    return steps(pos, tile_pattern, current)
 
 
 def solution(mesh):

time: 194 us -> 189 us (0.974); the launches traced: 192 us -> 189 us
  starting transfers between devices: 93.9 us -> 58 us
  waiting for transfers between devices: 50.4 us -> 77 us
  Pallas kernels: 42.8 us -> 49.3 us
    ppermute x26, starting transfers between devices: 33.4 us -> 15.7 us  [other_core(): return lax.ppermute(value, 'row', [(i, i ^ 1) for i in range(2 * NY)])]
    ppermute x12, starting transfers between devices: 24.2 us -> 10.5 us  [along_x(): return lax.ppermute(value, 'col', ring('col', shift, NX))]
    ppermute x12, waiting for transfers between devices: 25.2 us -> 37.9 us  [along_x(): return lax.ppermute(value, 'col', ring('col', shift, NX))]
    ppermute x6, waiting for transfers between devices: 3.88 us -> 15.6 us  [along_y(): return lax.ppermute(value, 'row', ring('row', shift, 2 * NY, 2))]
    pallas_call x3 -> x5, Pallas kernels: 3.98 us -> 7.96 us  [the longest x2 7.95 us: tables(): pl.pallas_call(table_kernel, out_shape=(jax.ShapeDtypeStruct((NZ + 1, SLO...]
    ppermute x6, starting transfers between devices: 9.71 us -> 6.14 us  [along_y(): return lax.ppermute(value, 'row', ring('row', shift, 2 * NY, 2))]
    ppermute x16, waiting for transfers between devices: 16.2 us -> 18.9 us  [along_z(): return lax.ppermute(value, 'layer', ring('layer', shift, NZ))]
    pallas_call x11 -> x13, Pallas kernels: 38.8 us -> 41.3 us  [call(): pl.pallas_call(kernel, out_shape=outs, in_specs=[SMEM] * n_smem + [VMEM]...]
  transfers between devices with their start and end apart: 60 -> 60, of which waited for: 25 -> 28; matrix products, arithmetic and copies ran while one was open for 0% -> 0% of each run, Pallas kernels for 6% -> 13%
where the time goes in v2:
time: 189 us
  waiting for transfers between devices  77 us (41%)
  starting transfers between devices  58 us (31%)
  Pallas kernels  49.3 us (26%)
  between operations  1.97 us (1%)
    pallas_call x13, Pallas kernels, call(): pl.pallas_call(kernel, out_shape=outs, in_specs=[SMEM] * n_smem + [VMEM]...  41.3 us
    ppermute x12, waiting for transfers between devices, along_x(): return lax.ppermute(value, 'col', ring('col', shift, NX))  37.9 us
    ppermute x16, starting transfers between devices, along_z(): return lax.ppermute(value, 'layer', ring('layer', shift, NZ))  25.6 us
    ppermute x16, waiting for transfers between devices, along_z(): return lax.ppermute(value, 'layer', ring('layer', shift, NZ))  18.9 us
    ppermute x26, starting transfers between devices, other_core(): return lax.ppermute(value, 'row', [(i, i ^ 1) for i in range(2 * NY)])  15.7 us
    ppermute x6, waiting for transfers between devices, along_y(): return lax.ppermute(value, 'row', ring('row', shift, 2 * NY, 2))  15.6 us
    ppermute x12, starting transfers between devices, along_x(): return lax.ppermute(value, 'col', ring('col', shift, NX))  10.5 us
    pallas_call x2, Pallas kernels, tables(): pl.pallas_call(table_kernel, out_shape=(jax.ShapeDtypeStruct((NZ + 1, SLO...  7.95 us
  transfers between devices with their start and end apart: 60, of which 28 were waited for; matrix products, arithmetic and copies ran while one was open for 0% of the time, Pallas kernels for 13%

profile of v2, /device:TPU:1, one launch (start us, length us, event | category | flops | bytes accessed | tf_op | source)
XLA Modules:
  0.0 188.9 jit_solution(17424307100742388482)
XLA Ops:
  4.2 184.7 %while.44 = (s32[]{:T(128)}, bf16[80,1280]{1,0:T(8,128)(2,1)S(1)}, f32[80,1280]{1,0:T(8,128)}, s32[4]{0:T(128)S(1)}, s32[40,40]{1,0:T(8,128)}, /*index=5*/s32[]{...) while((s32[]{:T(128)}, bf16[80,1280]{1,0:T(8,128)(2,1)S(1)}, ...), condition=%wide.region_3.4_spmd, body=%wide.region_0.3_spmd.sunk | while | flops 5002097152 | bytes 59108352 | solution.py:391
  4.2 3.6 %collective-permute-start.1 = (bf16[80,1280]{1,0:T(8,128)(2,1)S(1)}, bf16[80,1280]{1,0:T(8,128)(2,1)S(1)}, u32[]{:S(2)}, u32[]{:S(2)}) collective-permute-start(bf16[80,1280]{1,0:T(8,128)(2,1)S(1)} %get-tuple-element.569.refs_0_.refs_5_), channel_id=1, source_target_pairs={{0,192},{32,224},{64,0},{96,32},{128,64},{160,96},{192,128},{224,1... | collective-permute-start | bytes 614408 | tf_op jit(solution)/shard_map/while/body/ppermute | solution.py:256
  8.9 4.0 %body.67 = (s32[9,512]{1,0:T(8,128)S(1)}, s32[1]{0:T(128)}) custom-call(s32[4]{0:T(128)S(1)} %get-tuple-element.546.pos, s32[40,40]{1,0:T(8,128)} %get-tuple-element.690.pat), custom_call_target="tpu_custom_call" | custom-call | flops 1000000000 | tf_op jit(solution)/shard_map/while/body/pallas_call | solution.py:300
  12.9 3.3 %collective-permute-done.1.refs_1_ = bf16[80,1280]{1,0:T(8,128)(2,1)S(1)} collective-permute-done((bf16[80,1280]{1,0:T(8,128)(2,1)S(1)}, bf16[80,1280]{1,0:T(8,128)(2,1)S(1)}, u32[]{:S(2)}, u32[]{:S(2)}) %collective-permute-start.1) | collective-permute-done | bytes 204832 | tf_op jit(solution)/shard_map/while/body/ppermute | solution.py:256
  16.2 4.6 %collective-permute-done.3.refs_3_ = bf16[80,1280]{1,0:T(8,128)(2,1)S(1)} collective-permute-done((bf16[80,1280]{1,0:T(8,128)(2,1)S(1)}, bf16[80,1280]{1,0:T(8,128)(2,1)S(1)}, u32[]{:S(2)}, u32[]{:S(2)}) %collective-permute-start.3) | collective-permute-done | bytes 204832 | tf_op jit(solution)/shard_map/while/body/ppermute | solution.py:256
  25.5 5.7 %collective-permute-start.10 = (bf16[1408,128]{1,0:T(8,128)(2,1)S(1)}, bf16[1408,128]{1,0:T(8,128)(2,1)S(1)}, u32[]{:S(2)}, u32[]{:S(2)}) collective-permute-start(bf16[1408,128]{1,0:T(8,128)(2,1)S(1)} %body.68.refs_0_), channel_id=1, source_target_pairs={{0,7},{1,0},{2,1},{3,2},{4,3},{5,4},{6,5},{7,6},{8,15},{9,8},{10,9... | collective-permute-start | bytes 1081352 | tf_op jit(solution)/shard_map/while/body/ppermute | solution.py:260
  31.1 2.5 %collective-permute-start.12 = (bf16[80,1280]{1,0:T(8,128)(2,1)S(1)}, bf16[80,1280]{1,0:T(8,128)(2,1)S(1)}, u32[]{:S(2)}, u32[]{:S(2)}) collective-permute-start(bf16[80,1280]{1,0:T(8,128)(2,1)S(1)} %get-tuple-element.753), channel_id=1, source_target_pairs={{0,24},{8,0},{16,8},{24,16},{1,25},{9,1},{17,9},{25,17},{2,26},{10... | collective-permute-start | bytes 614408 | tf_op jit(solution)/shard_map/while/body/ppermute | solution.py:252
  34.1 4.5 %collective-permute-done.10.refs_4_ = bf16[1408,128]{1,0:T(8,128)(2,1)S(1)} collective-permute-done((bf16[1408,128]{1,0:T(8,128)(2,1)S(1)}, bf16[1408,128]{1,0:T(8,128)(2,1)S(1)}, u32[]{:S(2)}, u32[]{:S(2)}) %collective-permute-start.10) | collective-permute-done | bytes 360480 | tf_op jit(solution)/shard_map/while/body/ppermute | solution.py:260
  38.6 3.4 %collective-permute-start.11 = (bf16[1408,128]{1,0:T(8,128)(2,1)S(1)}, bf16[1408,128]{1,0:T(8,128)(2,1)S(1)}, u32[]{:S(2)}, u32[]{:S(2)}) collective-permute-start(bf16[1408,128]{1,0:T(8,128)(2,1)S(1)} %collective-permute-done.10.refs_4_), channel_id=1, source_target_pairs={{0,7},{1,0},{2,1},{3,2},{4,3},{5,4},{6,5},{7,6},{8,15},{9,8},{10,9... | collective-permute-start | bytes 1081352 | tf_op jit(solution)/shard_map/while/body/ppermute | solution.py:260
  44.8 7.2 %collective-permute-done.14.refs_8_ = bf16[80,1280]{1,0:T(8,128)(2,1)S(1)} collective-permute-done((bf16[80,1280]{1,0:T(8,128)(2,1)S(1)}, bf16[80,1280]{1,0:T(8,128)(2,1)S(1)}, u32[]{:S(2)}, u32[]{:S(2)}) %collective-permute-start.14) | collective-permute-done | bytes 204832 | tf_op jit(solution)/shard_map/while/body/ppermute | solution.py:252
  54.1 2.7 %collective-permute-start.16 = (bf16[1408,128]{1,0:T(8,128)(2,1)S(1)}, bf16[1408,128]{1,0:T(8,128)(2,1)S(1)}, u32[]{:S(2)}, u32[]{:S(2)}) collective-permute-start(bf16[1408,128]{1,0:T(8,128)(2,1)S(1)} %collective-permute-done.11.refs_8_), channel_id=1, source_target_pairs={{0,7},{1,0},{2,1},{3,2},{4,3},{5,4},{6,5},{7,6},{8,15},{9,8},{10,9... | collective-permute-start | bytes 1081352 | tf_op jit(solution)/shard_map/while/body/ppermute | solution.py:260
  56.8 6.0 %body.70.refs_4_ = bf16[5136,1280]{1,0:T(8,128)(2,1)S(1)} custom-call(s32[4]{0:T(128)S(1)} %get-tuple-element.768, s32[9,512]{1,0:T(8,128)S(1)} %get-tuple-element.767, bf16[1408,128]{1,0:T(8,128)(2,1)S(1)} %body.68.refs_0_, bf16[1408,128]{1,0:T(8,128)(2,1)S(1)} %collective-permute-done.17.refs_1_, bf16[1408,128]{1,0:T(8,128)(2,1)S(1)} %collective-permute-done.8.refs_2_, ...), custom_call_target="tpu_custom_call" | custom-call | flops 1000000000 | tf_op jit(solution)/shard_map/while/body/pallas_call | solution.py:273
  66.3 2.8 %collective-permute-start.23 = (bf16[640,128]{1,0:T(8,128)(2,1)S(1)}, bf16[640,128]{1,0:T(8,128)(2,1)S(1)}, u32[]{:S(2)}, u32[]{:S(2)}) collective-permute-start(bf16[640,128]{1,0:T(8,128)(2,1)S(1)} %get-tuple-element.564), channel_id=1, source_target_pairs={{0,7},{1,0},{2,1},{3,2},{4,3},{5,4},{6,5},{7,6},{8,15},{9,8},{10,9... | collective-permute-start | bytes 491528 | tf_op jit(solution)/shard_map/while/body/ppermute | solution.py:260
  69.0 2.7 %body.72.refs_4_ = bf16[5136,1280]{1,0:T(8,128)(2,1)S(1)} custom-call(s32[4]{0:T(128)S(1)} %get-tuple-element.768, s32[9,512]{1,0:T(8,128)S(1)} %get-tuple-element.767, bf16[1408,128]{1,0:T(8,128)(2,1)S(1)} %collective-permute-done.15.down.refs_0_, bf16[1408,128]{1,0:T(8,128)(2,1)S(1)} %collective-permute-done.24.refs_1_, ...), custom_call_target="tpu_custom_call", output_to_operand_aliasing={{}: (6, {})} | custom-call | flops 1000000000 | tf_op jit(solution)/shard_map/while/body/pallas_call | solution.py:273
  76.2 5.0 %body.73 = (f32[80,1280]{1,0:T(8,128)S(1)}, bf16[80,1280]{1,0:T(8,128)(2,1)S(1)}, bf16[5136,1280]{1,0:T(8,128)(2,1)S(1)}) custom-call(s32[4]{0:T(128)S(1)} %get-tuple-element.768, s32[40,40]{1,0:T(8,128)S(1)} %copy-done.1, s32[9,512]{1,0:T(8,128)S(1)} %get-tuple-element.767, ...), custom_call_target="tpu_custom_call", output_to_operand_aliasing={{2}: (7, {})} | custom-call | flops 1000000000 | tf_op jit(solution)/shard_map/while/body/pallas_call | solution.py:273
  81.2 3.2 %collective-permute-start.28 = (bf16[80,1280]{1,0:T(8,128)(2,1)S(1)}, bf16[80,1280]{1,0:T(8,128)(2,1)S(1)}, u32[]{:S(2)}, u32[]{:S(2)}) collective-permute-start(bf16[80,1280]{1,0:T(8,128)(2,1)S(1)} %get-tuple-element.576.refs_0_), channel_id=1, source_target_pairs={{0,24},{8,0},{16,8},{24,16},{1,25},{9,1},{17,9},{25,17},{2,26},{10... | collective-permute-start | bytes 614408 | tf_op jit(solution)/shard_map/while/body/ppermute | solution.py:252
  85.2 7.6 %collective-permute-done.28.refs_1_ = bf16[80,1280]{1,0:T(8,128)(2,1)S(1)} collective-permute-done((bf16[80,1280]{1,0:T(8,128)(2,1)S(1)}, bf16[80,1280]{1,0:T(8,128)(2,1)S(1)}, u32[]{:S(2)}, u32[]{:S(2)}) %collective-permute-start.28) | collective-permute-done | bytes 204832 | tf_op jit(solution)/shard_map/while/body/ppermute | solution.py:252
  92.8 4.0 %collective-permute-done.30.refs_3_ = bf16[80,1280]{1,0:T(8,128)(2,1)S(1)} collective-permute-done((bf16[80,1280]{1,0:T(8,128)(2,1)S(1)}, bf16[80,1280]{1,0:T(8,128)(2,1)S(1)}, u32[]{:S(2)}, u32[]{:S(2)}) %collective-permute-start.30) | collective-permute-done | bytes 204832 | tf_op jit(solution)/shard_map/while/body/ppermute | solution.py:252
  96.8 4.2 %body.74 = (f32[80,1280]{1,0:T(8,128)}, bf16[80,1280]{1,0:T(8,128)(2,1)S(1)}) custom-call(s32[4]{0:T(128)S(1)} %get-tuple-element.768, s32[40,40]{1,0:T(8,128)S(1)} %copy-done.1, f32[80,1280]{1,0:T(8,128)S(1)} %get-tuple-element.574.square, bf16[5136,1280]{1,0:T(8,128)(2,1)S(1)} %get-tuple-element.575.panel, ...), custom_call_target="tpu_custom_call" | custom-call | flops 1000000000 | tf_op jit(solution)/shard_map/while/body/pallas_call | solution.py:273
  102.5 4.0 %body.67 = (s32[9,512]{1,0:T(8,128)S(1)}, s32[1]{0:T(128)}) custom-call(s32[4]{0:T(128)S(1)} %get-tuple-element.546.pos, s32[40,40]{1,0:T(8,128)} %get-tuple-element.690.pat), custom_call_target="tpu_custom_call" | custom-call | flops 1000000000 | tf_op jit(solution)/shard_map/while/body/pallas_call | solution.py:300
  108.5 5.7 %collective-permute-done.3.refs_3_ = bf16[80,1280]{1,0:T(8,128)(2,1)S(1)} collective-permute-done((bf16[80,1280]{1,0:T(8,128)(2,1)S(1)}, bf16[80,1280]{1,0:T(8,128)(2,1)S(1)}, u32[]{:S(2)}, u32[]{:S(2)}) %collective-permute-start.3) | collective-permute-done | bytes 204832 | tf_op jit(solution)/shard_map/while/body/ppermute | solution.py:256
  121.7 7.0 %collective-permute-done.10.refs_4_ = bf16[1408,128]{1,0:T(8,128)(2,1)S(1)} collective-permute-done((bf16[1408,128]{1,0:T(8,128)(2,1)S(1)}, bf16[1408,128]{1,0:T(8,128)(2,1)S(1)}, u32[]{:S(2)}, u32[]{:S(2)}) %collective-permute-start.10) | collective-permute-done | bytes 360480 | tf_op jit(solution)/shard_map/while/body/ppermute | solution.py:260
  128.7 3.3 %collective-permute-start.11 = (bf16[1408,128]{1,0:T(8,128)(2,1)S(1)}, bf16[1408,128]{1,0:T(8,128)(2,1)S(1)}, u32[]{:S(2)}, u32[]{:S(2)}) collective-permute-start(bf16[1408,128]{1,0:T(8,128)(2,1)S(1)} %collective-permute-done.10.refs_4_), channel_id=1, source_target_pairs={{0,7},{1,0},{2,1},{3,2},{4,3},{5,4},{6,5},{7,6},{8,15},{9,8},{10,9... | collective-permute-start | bytes 1081352 | tf_op jit(solution)/shard_map/while/body/ppermute | solution.py:260
  133.6 7.4 %collective-permute-done.14.refs_8_ = bf16[80,1280]{1,0:T(8,128)(2,1)S(1)} collective-permute-done((bf16[80,1280]{1,0:T(8,128)(2,1)S(1)}, bf16[80,1280]{1,0:T(8,128)(2,1)S(1)}, u32[]{:S(2)}, u32[]{:S(2)}) %collective-permute-start.14) | collective-permute-done | bytes 204832 | tf_op jit(solution)/shard_map/while/body/ppermute | solution.py:252
  144.1 2.7 %collective-permute-start.16 = (bf16[1408,128]{1,0:T(8,128)(2,1)S(1)}, bf16[1408,128]{1,0:T(8,128)(2,1)S(1)}, u32[]{:S(2)}, u32[]{:S(2)}) collective-permute-start(bf16[1408,128]{1,0:T(8,128)(2,1)S(1)} %collective-permute-done.11.refs_8_), channel_id=1, source_target_pairs={{0,7},{1,0},{2,1},{3,2},{4,3},{5,4},{6,5},{7,6},{8,15},{9,8},{10,9... | collective-permute-start | bytes 1081352 | tf_op jit(solution)/shard_map/while/body/ppermute | solution.py:260
  146.8 6.0 %body.70.refs_4_ = bf16[5136,1280]{1,0:T(8,128)(2,1)S(1)} custom-call(s32[4]{0:T(128)S(1)} %get-tuple-element.768, s32[9,512]{1,0:T(8,128)S(1)} %get-tuple-element.767, bf16[1408,128]{1,0:T(8,128)(2,1)S(1)} %body.68.refs_0_, bf16[1408,128]{1,0:T(8,128)(2,1)S(1)} %collective-permute-done.17.refs_1_, bf16[1408,128]{1,0:T(8,128)(2,1)S(1)} %collective-permute-done.8.refs_2_, ...), custom_call_target="tpu_custom_call" | custom-call | flops 1000000000 | tf_op jit(solution)/shard_map/while/body/pallas_call | solution.py:273
  156.3 2.8 %collective-permute-start.23 = (bf16[640,128]{1,0:T(8,128)(2,1)S(1)}, bf16[640,128]{1,0:T(8,128)(2,1)S(1)}, u32[]{:S(2)}, u32[]{:S(2)}) collective-permute-start(bf16[640,128]{1,0:T(8,128)(2,1)S(1)} %get-tuple-element.564), channel_id=1, source_target_pairs={{0,7},{1,0},{2,1},{3,2},{4,3},{5,4},{6,5},{7,6},{8,15},{9,8},{10,9... | collective-permute-start | bytes 491528 | tf_op jit(solution)/shard_map/while/body/ppermute | solution.py:260
  159.0 2.7 %body.72.refs_4_ = bf16[5136,1280]{1,0:T(8,128)(2,1)S(1)} custom-call(s32[4]{0:T(128)S(1)} %get-tuple-element.768, s32[9,512]{1,0:T(8,128)S(1)} %get-tuple-element.767, bf16[1408,128]{1,0:T(8,128)(2,1)S(1)} %collective-permute-done.15.down.refs_0_, bf16[1408,128]{1,0:T(8,128)(2,1)S(1)} %collective-permute-done.24.refs_1_, ...), custom_call_target="tpu_custom_call", output_to_operand_aliasing={{}: (6, {})} | custom-call | flops 1000000000 | tf_op jit(solution)/shard_map/while/body/pallas_call | solution.py:273
  166.2 5.0 %body.73 = (f32[80,1280]{1,0:T(8,128)S(1)}, bf16[80,1280]{1,0:T(8,128)(2,1)S(1)}, bf16[5136,1280]{1,0:T(8,128)(2,1)S(1)}) custom-call(s32[4]{0:T(128)S(1)} %get-tuple-element.768, s32[40,40]{1,0:T(8,128)S(1)} %copy-done.1, s32[9,512]{1,0:T(8,128)S(1)} %get-tuple-element.767, ...), custom_call_target="tpu_custom_call", output_to_operand_aliasing={{2}: (7, {})} | custom-call | flops 1000000000 | tf_op jit(solution)/shard_map/while/body/pallas_call | solution.py:273
  173.0 4.6 %collective-permute-done.28.refs_1_ = bf16[80,1280]{1,0:T(8,128)(2,1)S(1)} collective-permute-done((bf16[80,1280]{1,0:T(8,128)(2,1)S(1)}, bf16[80,1280]{1,0:T(8,128)(2,1)S(1)}, u32[]{:S(2)}, u32[]{:S(2)}) %collective-permute-start.28) | collective-permute-done | bytes 204832 | tf_op jit(solution)/shard_map/while/body/ppermute | solution.py:252
  179.4 5.3 %collective-permute-done.30.refs_3_ = bf16[80,1280]{1,0:T(8,128)(2,1)S(1)} collective-permute-done((bf16[80,1280]{1,0:T(8,128)(2,1)S(1)}, bf16[80,1280]{1,0:T(8,128)(2,1)S(1)}, u32[]{:S(2)}, u32[]{:S(2)}) %collective-permute-start.30) | collective-permute-done | bytes 204832 | tf_op jit(solution)/shard_map/while/body/ppermute | solution.py:252
  184.7 4.2 %body.74 = (f32[80,1280]{1,0:T(8,128)}, bf16[80,1280]{1,0:T(8,128)(2,1)S(1)}) custom-call(s32[4]{0:T(128)S(1)} %get-tuple-element.768, s32[40,40]{1,0:T(8,128)S(1)} %copy-done.1, f32[80,1280]{1,0:T(8,128)S(1)} %get-tuple-element.574.square, bf16[5136,1280]{1,0:T(8,128)(2,1)S(1)} %get-tuple-element.575.panel, ...), custom_call_target="tpu_custom_call" | custom-call | flops 1000000000 | tf_op jit(solution)/shard_map/while/body/pallas_call | solution.py:273
  (126 shorter events, 48.0 us)
Async XLA Ops:
  4.2 11.9 %collective-permute-start.1 = (bf16[80,1280]{1,0:T(8,128)(2,1)S(1)}, bf16[80,1280]{1,0:T(8,128)(2,1)S(1)}, u32[]{:S(2)}, u32[]{:S(2)}) collective-permute-start(bf16[80,1280]{1,0:T(8,128)(2,1)S(1)} %get-tuple-element.569.refs_0_.refs_5_), channel_id=1, source_target_pairs={{0,192},{32,224},{64,0},{96,32},{128,64},{160,96},{192,128},{224,1... | collective-permute-start | bytes 614408 | tf_op jit(solution)/shard_map/while/body/ppermute | solution.py:256
  7.9 8.3 %collective-permute-start.2 = (bf16[80,1280]{1,0:T(8,128)(2,1)S(1)}, bf16[80,1280]{1,0:T(8,128)(2,1)S(1)}, u32[]{:S(2)}, u32[]{:S(2)}) collective-permute-start(bf16[80,1280]{1,0:T(8,128)(2,1)S(1)} %get-tuple-element.569.refs_0_.refs_5_), channel_id=1, source_target_pairs={{0,128},{32,160},{64,192},{96,224},{128,0},{160,32},{192,64},{224,... | collective-permute-start | bytes 614408 | tf_op jit(solution)/shard_map/while/body/ppermute | solution.py:256
  8.2 12.5 %collective-permute-start.3 = (bf16[80,1280]{1,0:T(8,128)(2,1)S(1)}, bf16[80,1280]{1,0:T(8,128)(2,1)S(1)}, u32[]{:S(2)}, u32[]{:S(2)}) collective-permute-start(bf16[80,1280]{1,0:T(8,128)(2,1)S(1)} %get-tuple-element.569.refs_0_.refs_5_), channel_id=1, source_target_pairs={{0,64},{32,96},{64,128},{96,160},{128,192},{160,224},{192,0},{224,... | collective-permute-start | bytes 614408 | tf_op jit(solution)/shard_map/while/body/ppermute | solution.py:256
  25.5 13.1 %collective-permute-start.10 = (bf16[1408,128]{1,0:T(8,128)(2,1)S(1)}, bf16[1408,128]{1,0:T(8,128)(2,1)S(1)}, u32[]{:S(2)}, u32[]{:S(2)}) collective-permute-start(bf16[1408,128]{1,0:T(8,128)(2,1)S(1)} %body.68.refs_0_), channel_id=1, source_target_pairs={{0,7},{1,0},{2,1},{3,2},{4,3},{5,4},{6,5},{7,6},{8,15},{9,8},{10,9... | collective-permute-start | bytes 1081352 | tf_op jit(solution)/shard_map/while/body/ppermute | solution.py:260
  31.1 10.9 %collective-permute-start.8 = (bf16[1408,128]{1,0:T(8,128)(2,1)S(1)}, bf16[1408,128]{1,0:T(8,128)(2,1)S(1)}, u32[]{:S(2)}, u32[]{:S(2)}) collective-permute-start(bf16[1408,128]{1,0:T(8,128)(2,1)S(1)} %body.68.refs_0_), channel_id=1, source_target_pairs={{0,1},{1,2},{2,3},{3,4},{4,5},{5,6},{6,7},{7,0},{8,9},{9,10},{10,1... | collective-permute-start | bytes 1081352 | tf_op jit(solution)/shard_map/while/body/ppermute | solution.py:260
  31.1 12.3 %collective-permute-start.12 = (bf16[80,1280]{1,0:T(8,128)(2,1)S(1)}, bf16[80,1280]{1,0:T(8,128)(2,1)S(1)}, u32[]{:S(2)}, u32[]{:S(2)}) collective-permute-start(bf16[80,1280]{1,0:T(8,128)(2,1)S(1)} %get-tuple-element.753), channel_id=1, source_target_pairs={{0,24},{8,0},{16,8},{24,16},{1,25},{9,1},{17,9},{25,17},{2,26},{10... | collective-permute-start | bytes 614408 | tf_op jit(solution)/shard_map/while/body/ppermute | solution.py:252
  33.6 10.0 %collective-permute-start.13 = (bf16[80,1280]{1,0:T(8,128)(2,1)S(1)}, bf16[80,1280]{1,0:T(8,128)(2,1)S(1)}, u32[]{:S(2)}, u32[]{:S(2)}) collective-permute-start(bf16[80,1280]{1,0:T(8,128)(2,1)S(1)} %get-tuple-element.753), channel_id=1, source_target_pairs={{0,16},{8,24},{16,0},{24,8},{1,17},{9,25},{17,1},{25,9},{2,18},{10... | collective-permute-start | bytes 614408 | tf_op jit(solution)/shard_map/while/body/ppermute | solution.py:252
  38.6 14.1 %collective-permute-start.11 = (bf16[1408,128]{1,0:T(8,128)(2,1)S(1)}, bf16[1408,128]{1,0:T(8,128)(2,1)S(1)}, u32[]{:S(2)}, u32[]{:S(2)}) collective-permute-start(bf16[1408,128]{1,0:T(8,128)(2,1)S(1)} %collective-permute-done.10.refs_4_), channel_id=1, source_target_pairs={{0,7},{1,0},{2,1},{3,2},{4,3},{5,4},{6,5},{7,6},{8,15},{9,8},{10,9... | collective-permute-start | bytes 1081352 | tf_op jit(solution)/shard_map/while/body/ppermute | solution.py:260
  42.0 10.7 %collective-permute-start.9 = (bf16[1408,128]{1,0:T(8,128)(2,1)S(1)}, bf16[1408,128]{1,0:T(8,128)(2,1)S(1)}, u32[]{:S(2)}, u32[]{:S(2)}) collective-permute-start(bf16[1408,128]{1,0:T(8,128)(2,1)S(1)} %collective-permute-done.8.refs_2_), channel_id=1, source_target_pairs={{0,1},{1,2},{2,3},{3,4},{4,5},{5,6},{6,7},{7,0},{8,9},{9,10},{10,1... | collective-permute-start | bytes 1081352 | tf_op jit(solution)/shard_map/while/body/ppermute | solution.py:260
  42.0 12.0 %collective-permute-start.17 = (bf16[1408,128]{1,0:T(8,128)(2,1)S(1)}, bf16[1408,128]{1,0:T(8,128)(2,1)S(1)}, u32[]{:S(2)}, u32[]{:S(2)}) collective-permute-start(bf16[1408,128]{1,0:T(8,128)(2,1)S(1)} %body.68.refs_0_), channel_id=1, source_target_pairs={{0,32},{32,0},{64,96},{96,64},{128,160},{160,128},{192,224},{224,1... | collective-permute-start | bytes 1081352 | tf_op jit(solution)/shard_map/while/body/ppermute | solution.py:264
  43.5 10.6 %collective-permute-start.18 = (bf16[1408,128]{1,0:T(8,128)(2,1)S(1)}, bf16[1408,128]{1,0:T(8,128)(2,1)S(1)}, u32[]{:S(2)}, u32[]{:S(2)}) collective-permute-start(bf16[1408,128]{1,0:T(8,128)(2,1)S(1)} %collective-permute-done.8.refs_2_), channel_id=1, source_target_pairs={{0,32},{32,0},{64,96},{96,64},{128,160},{160,128},{192,224},{224,1... | collective-permute-start | bytes 1081352 | tf_op jit(solution)/shard_map/while/body/ppermute | solution.py:264
  43.6 8.4 %collective-permute-start.14 = (bf16[80,1280]{1,0:T(8,128)(2,1)S(1)}, bf16[80,1280]{1,0:T(8,128)(2,1)S(1)}, u32[]{:S(2)}, u32[]{:S(2)}) collective-permute-start(bf16[80,1280]{1,0:T(8,128)(2,1)S(1)} %get-tuple-element.753), channel_id=1, source_target_pairs={{0,8},{8,16},{16,24},{24,0},{1,9},{9,17},{17,25},{25,1},{2,10},{10... | collective-permute-start | bytes 614408 | tf_op jit(solution)/shard_map/while/body/ppermute | solution.py:252
  54.1 10.7 %collective-permute-start.15 = (bf16[1408,128]{1,0:T(8,128)(2,1)S(1)}, bf16[1408,128]{1,0:T(8,128)(2,1)S(1)}, u32[]{:S(2)}, u32[]{:S(2)}) collective-permute-start(bf16[1408,128]{1,0:T(8,128)(2,1)S(1)} %collective-permute-done.9.refs_6_), channel_id=1, source_target_pairs={{0,1},{1,2},{2,3},{3,4},{4,5},{5,6},{6,7},{7,0},{8,9},{9,10},{10,1... | collective-permute-start | bytes 1081352 | tf_op jit(solution)/shard_map/while/body/ppermute | solution.py:260
  54.1 10.7 %collective-permute-start.16 = (bf16[1408,128]{1,0:T(8,128)(2,1)S(1)}, bf16[1408,128]{1,0:T(8,128)(2,1)S(1)}, u32[]{:S(2)}, u32[]{:S(2)}) collective-permute-start(bf16[1408,128]{1,0:T(8,128)(2,1)S(1)} %collective-permute-done.11.refs_8_), channel_id=1, source_target_pairs={{0,7},{1,0},{2,1},{3,2},{4,3},{5,4},{6,5},{7,6},{8,15},{9,8},{10,9... | collective-permute-start | bytes 1081352 | tf_op jit(solution)/shard_map/while/body/ppermute | solution.py:260
  66.2 7.2 %collective-permute-start.22 = (bf16[768,128]{1,0:T(8,128)(2,1)S(1)}, bf16[768,128]{1,0:T(8,128)(2,1)S(1)}, u32[]{:S(2)}, u32[]{:S(2)}) collective-permute-start(bf16[768,128]{1,0:T(8,128)(2,1)S(1)} %get-tuple-element.563), channel_id=1, source_target_pairs={{0,1},{1,2},{2,3},{3,4},{4,5},{5,6},{6,7},{7,0},{8,9},{9,10},{10,1... | collective-permute-start | bytes 589832 | tf_op jit(solution)/shard_map/while/body/ppermute | solution.py:260
  81.2 11.6 %collective-permute-start.28 = (bf16[80,1280]{1,0:T(8,128)(2,1)S(1)}, bf16[80,1280]{1,0:T(8,128)(2,1)S(1)}, u32[]{:S(2)}, u32[]{:S(2)}) collective-permute-start(bf16[80,1280]{1,0:T(8,128)(2,1)S(1)} %get-tuple-element.576.refs_0_), channel_id=1, source_target_pairs={{0,24},{8,0},{16,8},{24,16},{1,25},{9,1},{17,9},{25,17},{2,26},{10... | collective-permute-start | bytes 614408 | tf_op jit(solution)/shard_map/while/body/ppermute | solution.py:252
  84.4 8.4 %collective-permute-start.29 = (bf16[80,1280]{1,0:T(8,128)(2,1)S(1)}, bf16[80,1280]{1,0:T(8,128)(2,1)S(1)}, u32[]{:S(2)}, u32[]{:S(2)}) collective-permute-start(bf16[80,1280]{1,0:T(8,128)(2,1)S(1)} %get-tuple-element.576.refs_0_), channel_id=1, source_target_pairs={{0,16},{8,24},{16,0},{24,8},{1,17},{9,25},{17,1},{25,9},{2,18},{10... | collective-permute-start | bytes 614408 | tf_op jit(solution)/shard_map/while/body/ppermute | solution.py:252
  84.4 12.3 %collective-permute-start.30 = (bf16[80,1280]{1,0:T(8,128)(2,1)S(1)}, bf16[80,1280]{1,0:T(8,128)(2,1)S(1)}, u32[]{:S(2)}, u32[]{:S(2)}) collective-permute-start(bf16[80,1280]{1,0:T(8,128)(2,1)S(1)} %get-tuple-element.576.refs_0_), channel_id=1, source_target_pairs={{0,8},{8,16},{16,24},{24,0},{1,9},{9,17},{17,25},{25,1},{2,10},{10... | collective-permute-start | bytes 614408 | tf_op jit(solution)/shard_map/while/body/ppermute | solution.py:252
  101.7 12.5 %collective-permute-start.3 = (bf16[80,1280]{1,0:T(8,128)(2,1)S(1)}, bf16[80,1280]{1,0:T(8,128)(2,1)S(1)}, u32[]{:S(2)}, u32[]{:S(2)}) collective-permute-start(bf16[80,1280]{1,0:T(8,128)(2,1)S(1)} %get-tuple-element.569.refs_0_.refs_5_), channel_id=1, source_target_pairs={{0,64},{32,96},{64,128},{96,160},{128,192},{160,224},{192,0},{224,... | collective-permute-start | bytes 614408 | tf_op jit(solution)/shard_map/while/body/ppermute | solution.py:256
  118.9 9.8 %collective-permute-start.10 = (bf16[1408,128]{1,0:T(8,128)(2,1)S(1)}, bf16[1408,128]{1,0:T(8,128)(2,1)S(1)}, u32[]{:S(2)}, u32[]{:S(2)}) collective-permute-start(bf16[1408,128]{1,0:T(8,128)(2,1)S(1)} %body.68.refs_0_), channel_id=1, source_target_pairs={{0,7},{1,0},{2,1},{3,2},{4,3},{5,4},{6,5},{7,6},{8,15},{9,8},{10,9... | collective-permute-start | bytes 1081352 | tf_op jit(solution)/shard_map/while/body/ppermute | solution.py:260
  121.1 10.9 %collective-permute-start.8 = (bf16[1408,128]{1,0:T(8,128)(2,1)S(1)}, bf16[1408,128]{1,0:T(8,128)(2,1)S(1)}, u32[]{:S(2)}, u32[]{:S(2)}) collective-permute-start(bf16[1408,128]{1,0:T(8,128)(2,1)S(1)} %body.68.refs_0_), channel_id=1, source_target_pairs={{0,1},{1,2},{2,3},{3,4},{4,5},{5,6},{6,7},{7,0},{8,9},{9,10},{10,1... | collective-permute-start | bytes 1081352 | tf_op jit(solution)/shard_map/while/body/ppermute | solution.py:260
  121.2 12.3 %collective-permute-start.12 = (bf16[80,1280]{1,0:T(8,128)(2,1)S(1)}, bf16[80,1280]{1,0:T(8,128)(2,1)S(1)}, u32[]{:S(2)}, u32[]{:S(2)}) collective-permute-start(bf16[80,1280]{1,0:T(8,128)(2,1)S(1)} %get-tuple-element.753), channel_id=1, source_target_pairs={{0,24},{8,0},{16,8},{24,16},{1,25},{9,1},{17,9},{25,17},{2,26},{10... | collective-permute-start | bytes 614408 | tf_op jit(solution)/shard_map/while/body/ppermute | solution.py:252
  121.2 12.4 %collective-permute-start.13 = (bf16[80,1280]{1,0:T(8,128)(2,1)S(1)}, bf16[80,1280]{1,0:T(8,128)(2,1)S(1)}, u32[]{:S(2)}, u32[]{:S(2)}) collective-permute-start(bf16[80,1280]{1,0:T(8,128)(2,1)S(1)} %get-tuple-element.753), channel_id=1, source_target_pairs={{0,16},{8,24},{16,0},{24,8},{1,17},{9,25},{17,1},{25,9},{2,18},{10... | collective-permute-start | bytes 614408 | tf_op jit(solution)/shard_map/while/body/ppermute | solution.py:252
  128.7 13.6 %collective-permute-start.11 = (bf16[1408,128]{1,0:T(8,128)(2,1)S(1)}, bf16[1408,128]{1,0:T(8,128)(2,1)S(1)}, u32[]{:S(2)}, u32[]{:S(2)}) collective-permute-start(bf16[1408,128]{1,0:T(8,128)(2,1)S(1)} %collective-permute-done.10.refs_4_), channel_id=1, source_target_pairs={{0,7},{1,0},{2,1},{3,2},{4,3},{5,4},{6,5},{7,6},{8,15},{9,8},{10,9... | collective-permute-start | bytes 1081352 | tf_op jit(solution)/shard_map/while/body/ppermute | solution.py:260
  132.0 10.3 %collective-permute-start.9 = (bf16[1408,128]{1,0:T(8,128)(2,1)S(1)}, bf16[1408,128]{1,0:T(8,128)(2,1)S(1)}, u32[]{:S(2)}, u32[]{:S(2)}) collective-permute-start(bf16[1408,128]{1,0:T(8,128)(2,1)S(1)} %collective-permute-done.8.refs_2_), channel_id=1, source_target_pairs={{0,1},{1,2},{2,3},{3,4},{4,5},{5,6},{6,7},{7,0},{8,9},{9,10},{10,1... | collective-permute-start | bytes 1081352 | tf_op jit(solution)/shard_map/while/body/ppermute | solution.py:260
  132.0 12.0 %collective-permute-start.17 = (bf16[1408,128]{1,0:T(8,128)(2,1)S(1)}, bf16[1408,128]{1,0:T(8,128)(2,1)S(1)}, u32[]{:S(2)}, u32[]{:S(2)}) collective-permute-start(bf16[1408,128]{1,0:T(8,128)(2,1)S(1)} %body.68.refs_0_), channel_id=1, source_target_pairs={{0,32},{32,0},{64,96},{96,64},{128,160},{160,128},{192,224},{224,1... | collective-permute-start | bytes 1081352 | tf_op jit(solution)/shard_map/while/body/ppermute | solution.py:264
  133.5 10.6 %collective-permute-start.18 = (bf16[1408,128]{1,0:T(8,128)(2,1)S(1)}, bf16[1408,128]{1,0:T(8,128)(2,1)S(1)}, u32[]{:S(2)}, u32[]{:S(2)}) collective-permute-start(bf16[1408,128]{1,0:T(8,128)(2,1)S(1)} %collective-permute-done.8.refs_2_), channel_id=1, source_target_pairs={{0,32},{32,0},{64,96},{96,64},{128,160},{160,128},{192,224},{224,1... | collective-permute-start | bytes 1081352 | tf_op jit(solution)/shard_map/while/body/ppermute | solution.py:264
  133.6 7.4 %collective-permute-start.14 = (bf16[80,1280]{1,0:T(8,128)(2,1)S(1)}, bf16[80,1280]{1,0:T(8,128)(2,1)S(1)}, u32[]{:S(2)}, u32[]{:S(2)}) collective-permute-start(bf16[80,1280]{1,0:T(8,128)(2,1)S(1)} %get-tuple-element.753), channel_id=1, source_target_pairs={{0,8},{8,16},{16,24},{24,0},{1,9},{9,17},{17,25},{25,1},{2,10},{10... | collective-permute-start | bytes 614408 | tf_op jit(solution)/shard_map/while/body/ppermute | solution.py:252
  144.1 10.7 %collective-permute-start.15 = (bf16[1408,128]{1,0:T(8,128)(2,1)S(1)}, bf16[1408,128]{1,0:T(8,128)(2,1)S(1)}, u32[]{:S(2)}, u32[]{:S(2)}) collective-permute-start(bf16[1408,128]{1,0:T(8,128)(2,1)S(1)} %collective-permute-done.9.refs_6_), channel_id=1, source_target_pairs={{0,1},{1,2},{2,3},{3,4},{4,5},{5,6},{6,7},{7,0},{8,9},{9,10},{10,1... | collective-permute-start | bytes 1081352 | tf_op jit(solution)/shard_map/while/body/ppermute | solution.py:260
  144.1 10.7 %collective-permute-start.16 = (bf16[1408,128]{1,0:T(8,128)(2,1)S(1)}, bf16[1408,128]{1,0:T(8,128)(2,1)S(1)}, u32[]{:S(2)}, u32[]{:S(2)}) collective-permute-start(bf16[1408,128]{1,0:T(8,128)(2,1)S(1)} %collective-permute-done.11.refs_8_), channel_id=1, source_target_pairs={{0,7},{1,0},{2,1},{3,2},{4,3},{5,4},{6,5},{7,6},{8,15},{9,8},{10,9... | collective-permute-start | bytes 1081352 | tf_op jit(solution)/shard_map/while/body/ppermute | solution.py:260
  171.8 7.6 %collective-permute-start.29 = (bf16[80,1280]{1,0:T(8,128)(2,1)S(1)}, bf16[80,1280]{1,0:T(8,128)(2,1)S(1)}, u32[]{:S(2)}, u32[]{:S(2)}) collective-permute-start(bf16[80,1280]{1,0:T(8,128)(2,1)S(1)} %get-tuple-element.576.refs_0_), channel_id=1, source_target_pairs={{0,16},{8,24},{16,0},{24,8},{1,17},{9,25},{17,1},{25,9},{2,18},{10... | collective-permute-start | bytes 614408 | tf_op jit(solution)/shard_map/while/body/ppermute | solution.py:252
  172.2 12.5 %collective-permute-start.30 = (bf16[80,1280]{1,0:T(8,128)(2,1)S(1)}, bf16[80,1280]{1,0:T(8,128)(2,1)S(1)}, u32[]{:S(2)}, u32[]{:S(2)}) collective-permute-start(bf16[80,1280]{1,0:T(8,128)(2,1)S(1)} %get-tuple-element.576.refs_0_), channel_id=1, source_target_pairs={{0,8},{8,16},{16,24},{24,0},{1,9},{9,17},{17,25},{25,1},{2,10},{10... | collective-permute-start | bytes 614408 | tf_op jit(solution)/shard_map/while/body/ppermute | solution.py:252
  (35 other events, 158.3 us)

commit v3 on v2

--- a/solution.py
+++ b/solution.py
@@ -23,8 +23,8 @@
 Z_ORDER = (0, -1, 1, -2, 2, -3, 3, 4)
 SLOTS = 512
 UNROLL = 8
-CAPACITY = 88
-SPLIT = 48
+CAPACITY = 80
+SPLIT = 40
 EXTRA = 16
 ROUNDS = -(-(ALL_SLOTS // 2 - CAPACITY) // EXTRA)
 

time: 189 us -> 186 us (0.984)
  waiting for transfers between devices: 77 us -> 72.9 us
    ppermute x16, waiting for transfers between devices: 18.9 us -> 14 us  [along_z(): return lax.ppermute(value, 'layer', ring('layer', shift, NZ))]
  transfers between devices with their start and end apart: 60 -> 60, of which waited for: 28 -> 27; matrix products, arithmetic and copies ran while one was open for 0% -> 0% of each run, Pallas kernels for 13% -> 14%
where the time goes in v3:
time: 186 us
  waiting for transfers between devices  72.9 us (39%)
  starting transfers between devices  58.9 us (32%)
  Pallas kernels  50.1 us (27%)
  between operations  1.97 us (1%)
    pallas_call x13, Pallas kernels, call(): pl.pallas_call(kernel, out_shape=outs, in_specs=[SMEM] * n_smem + [VMEM]...  42.1 us
    ppermute x12, waiting for transfers between devices, along_x(): return lax.ppermute(value, 'col', ring('col', shift, NX))  38.8 us
    ppermute x16, starting transfers between devices, along_z(): return lax.ppermute(value, 'layer', ring('layer', shift, NZ))  26.3 us
    ppermute x6, waiting for transfers between devices, along_y(): return lax.ppermute(value, 'row', ring('row', shift, 2 * NY, 2))  15.6 us
    ppermute x26, starting transfers between devices, other_core(): return lax.ppermute(value, 'row', [(i, i ^ 1) for i in range(2 * NY)])  14 us
    ppermute x16, waiting for transfers between devices, along_z(): return lax.ppermute(value, 'layer', ring('layer', shift, NZ))  14 us
    ppermute x12, starting transfers between devices, along_x(): return lax.ppermute(value, 'col', ring('col', shift, NX))  12.4 us
    pallas_call x2, Pallas kernels, tables(): pl.pallas_call(table_kernel, out_shape=(jax.ShapeDtypeStruct((NZ + 1, SLO...  7.95 us
  transfers between devices with their start and end apart: 60, of which 27 were waited for; matrix products, arithmetic and copies ran while one was open for 0% of the time, Pallas kernels for 14%

profile of v3, /device:TPU:1, one launch (start us, length us, event | category | flops | bytes accessed | tf_op | source)
XLA Modules:
  0.0 186.5 jit_solution(14200082865042458394)
XLA Ops:
  4.2 182.3 %while.44 = (s32[]{:T(128)}, bf16[80,1280]{1,0:T(8,128)(2,1)S(1)}, f32[80,1280]{1,0:T(8,128)}, s32[4]{0:T(128)S(1)}, s32[40,40]{1,0:T(8,128)}, /*index=5*/s32[]{...) while((s32[]{:T(128)}, bf16[80,1280]{1,0:T(8,128)(2,1)S(1)}, ...), condition=%wide.region_3.4_spmd, body=%wide.region_0.3_spmd.sunk | while | flops 5002097152 | bytes 60288000 | solution.py:391
  4.2 3.6 %collective-permute-start.1 = (bf16[80,1280]{1,0:T(8,128)(2,1)S(1)}, bf16[80,1280]{1,0:T(8,128)(2,1)S(1)}, u32[]{:S(2)}, u32[]{:S(2)}) collective-permute-start(bf16[80,1280]{1,0:T(8,128)(2,1)S(1)} %get-tuple-element.569.refs_0_.refs_5_), channel_id=1, source_target_pairs={{0,192},{32,224},{64,0},{96,32},{128,64},{160,96},{192,128},{224,1... | collective-permute-start | bytes 614408 | tf_op jit(solution)/shard_map/while/body/ppermute | solution.py:256
  8.9 4.0 %body.67 = (s32[9,512]{1,0:T(8,128)S(1)}, s32[1]{0:T(128)}) custom-call(s32[4]{0:T(128)S(1)} %get-tuple-element.546.pos, s32[40,40]{1,0:T(8,128)} %get-tuple-element.690.pat), custom_call_target="tpu_custom_call" | custom-call | flops 1000000000 | tf_op jit(solution)/shard_map/while/body/pallas_call | solution.py:300
  12.9 3.3 %collective-permute-done.1.refs_1_ = bf16[80,1280]{1,0:T(8,128)(2,1)S(1)} collective-permute-done((bf16[80,1280]{1,0:T(8,128)(2,1)S(1)}, bf16[80,1280]{1,0:T(8,128)(2,1)S(1)}, u32[]{:S(2)}, u32[]{:S(2)}) %collective-permute-start.1) | collective-permute-done | bytes 204832 | tf_op jit(solution)/shard_map/while/body/ppermute | solution.py:256
  16.2 4.6 %collective-permute-done.3.refs_3_ = bf16[80,1280]{1,0:T(8,128)(2,1)S(1)} collective-permute-done((bf16[80,1280]{1,0:T(8,128)(2,1)S(1)}, bf16[80,1280]{1,0:T(8,128)(2,1)S(1)}, u32[]{:S(2)}, u32[]{:S(2)}) %collective-permute-start.3) | collective-permute-done | bytes 204832 | tf_op jit(solution)/shard_map/while/body/ppermute | solution.py:256
  25.4 5.7 %collective-permute-start.10 = (bf16[1280,128]{1,0:T(8,128)(2,1)S(1)}, bf16[1280,128]{1,0:T(8,128)(2,1)S(1)}, u32[]{:S(2)}, u32[]{:S(2)}) collective-permute-start(bf16[1280,128]{1,0:T(8,128)(2,1)S(1)} %body.68.refs_0_), channel_id=1, source_target_pairs={{0,7},{1,0},{2,1},{3,2},{4,3},{5,4},{6,5},{7,6},{8,15},{9,8},{10,9... | collective-permute-start | bytes 983048 | tf_op jit(solution)/shard_map/while/body/ppermute | solution.py:260
  34.1 3.8 %collective-permute-done.10.refs_4_ = bf16[1280,128]{1,0:T(8,128)(2,1)S(1)} collective-permute-done((bf16[1280,128]{1,0:T(8,128)(2,1)S(1)}, bf16[1280,128]{1,0:T(8,128)(2,1)S(1)}, u32[]{:S(2)}, u32[]{:S(2)}) %collective-permute-start.10) | collective-permute-done | bytes 327712 | tf_op jit(solution)/shard_map/while/body/ppermute | solution.py:260
  37.8 3.4 %collective-permute-start.11 = (bf16[1280,128]{1,0:T(8,128)(2,1)S(1)}, bf16[1280,128]{1,0:T(8,128)(2,1)S(1)}, u32[]{:S(2)}, u32[]{:S(2)}) collective-permute-start(bf16[1280,128]{1,0:T(8,128)(2,1)S(1)} %collective-permute-done.10.refs_4_), channel_id=1, source_target_pairs={{0,7},{1,0},{2,1},{3,2},{4,3},{5,4},{6,5},{7,6},{8,15},{9,8},{10,9... | collective-permute-start | bytes 983048 | tf_op jit(solution)/shard_map/while/body/ppermute | solution.py:260
  44.0 8.1 %collective-permute-done.14.refs_8_ = bf16[80,1280]{1,0:T(8,128)(2,1)S(1)} collective-permute-done((bf16[80,1280]{1,0:T(8,128)(2,1)S(1)}, bf16[80,1280]{1,0:T(8,128)(2,1)S(1)}, u32[]{:S(2)}, u32[]{:S(2)}) %collective-permute-start.14) | collective-permute-done | bytes 204832 | tf_op jit(solution)/shard_map/while/body/ppermute | solution.py:252
  53.2 2.8 %collective-permute-start.16 = (bf16[1280,128]{1,0:T(8,128)(2,1)S(1)}, bf16[1280,128]{1,0:T(8,128)(2,1)S(1)}, u32[]{:S(2)}, u32[]{:S(2)}) collective-permute-start(bf16[1280,128]{1,0:T(8,128)(2,1)S(1)} %collective-permute-done.11.refs_8_), channel_id=1, source_target_pairs={{0,7},{1,0},{2,1},{3,2},{4,3},{5,4},{6,5},{7,6},{8,15},{9,8},{10,9... | collective-permute-start | bytes 983048 | tf_op jit(solution)/shard_map/while/body/ppermute | solution.py:260
  56.0 6.5 %body.70.refs_4_ = bf16[5136,1280]{1,0:T(8,128)(2,1)S(1)} custom-call(s32[4]{0:T(128)S(1)} %get-tuple-element.768, s32[9,512]{1,0:T(8,128)S(1)} %get-tuple-element.767, bf16[1280,128]{1,0:T(8,128)(2,1)S(1)} %body.68.refs_0_, bf16[1280,128]{1,0:T(8,128)(2,1)S(1)} %collective-permute-done.17.refs_1_, bf16[1280,128]{1,0:T(8,128)(2,1)S(1)} %collective-permute-done.8.refs_2_, ...), custom_call_target="tpu_custom_call" | custom-call | flops 1000000000 | tf_op jit(solution)/shard_map/while/body/pallas_call | solution.py:273
  64.7 2.8 %collective-permute-start.23 = (bf16[640,128]{1,0:T(8,128)(2,1)S(1)}, bf16[640,128]{1,0:T(8,128)(2,1)S(1)}, u32[]{:S(2)}, u32[]{:S(2)}) collective-permute-start(bf16[640,128]{1,0:T(8,128)(2,1)S(1)} %get-tuple-element.564), channel_id=1, source_target_pairs={{0,7},{1,0},{2,1},{3,2},{4,3},{5,4},{6,5},{7,6},{8,15},{9,8},{10,9... | collective-permute-start | bytes 491528 | tf_op jit(solution)/shard_map/while/body/ppermute | solution.py:260
  67.5 2.7 %body.72.refs_4_ = bf16[5136,1280]{1,0:T(8,128)(2,1)S(1)} custom-call(s32[4]{0:T(128)S(1)} %get-tuple-element.768, s32[9,512]{1,0:T(8,128)S(1)} %get-tuple-element.767, bf16[1280,128]{1,0:T(8,128)(2,1)S(1)} %collective-permute-done.15.down.refs_0_, bf16[1280,128]{1,0:T(8,128)(2,1)S(1)} %collective-permute-done.24.refs_1_, ...), custom_call_target="tpu_custom_call", output_to_operand_aliasing={{}: (6, {})} | custom-call | flops 1000000000 | tf_op jit(solution)/shard_map/while/body/pallas_call | solution.py:273
  74.0 5.0 %body.73 = (f32[80,1280]{1,0:T(8,128)S(1)}, bf16[80,1280]{1,0:T(8,128)(2,1)S(1)}, bf16[5136,1280]{1,0:T(8,128)(2,1)S(1)}) custom-call(s32[4]{0:T(128)S(1)} %get-tuple-element.768, s32[40,40]{1,0:T(8,128)S(1)} %copy-done.1, s32[9,512]{1,0:T(8,128)S(1)} %get-tuple-element.767, ...), custom_call_target="tpu_custom_call", output_to_operand_aliasing={{2}: (7, {})} | custom-call | flops 1000000000 | tf_op jit(solution)/shard_map/while/body/pallas_call | solution.py:273
  79.0 4.2 %collective-permute-start.28 = (bf16[80,1280]{1,0:T(8,128)(2,1)S(1)}, bf16[80,1280]{1,0:T(8,128)(2,1)S(1)}, u32[]{:S(2)}, u32[]{:S(2)}) collective-permute-start(bf16[80,1280]{1,0:T(8,128)(2,1)S(1)} %get-tuple-element.576.refs_0_), channel_id=1, source_target_pairs={{0,24},{8,0},{16,8},{24,16},{1,25},{9,1},{17,9},{25,17},{2,26},{10... | collective-permute-start | bytes 614408 | tf_op jit(solution)/shard_map/while/body/ppermute | solution.py:252
  83.9 7.9 %collective-permute-done.28.refs_1_ = bf16[80,1280]{1,0:T(8,128)(2,1)S(1)} collective-permute-done((bf16[80,1280]{1,0:T(8,128)(2,1)S(1)}, bf16[80,1280]{1,0:T(8,128)(2,1)S(1)}, u32[]{:S(2)}, u32[]{:S(2)}) %collective-permute-start.28) | collective-permute-done | bytes 204832 | tf_op jit(solution)/shard_map/while/body/ppermute | solution.py:252
  91.8 3.7 %collective-permute-done.30.refs_3_ = bf16[80,1280]{1,0:T(8,128)(2,1)S(1)} collective-permute-done((bf16[80,1280]{1,0:T(8,128)(2,1)S(1)}, bf16[80,1280]{1,0:T(8,128)(2,1)S(1)}, u32[]{:S(2)}, u32[]{:S(2)}) %collective-permute-start.30) | collective-permute-done | bytes 204832 | tf_op jit(solution)/shard_map/while/body/ppermute | solution.py:252
  95.5 4.2 %body.74 = (f32[80,1280]{1,0:T(8,128)}, bf16[80,1280]{1,0:T(8,128)(2,1)S(1)}) custom-call(s32[4]{0:T(128)S(1)} %get-tuple-element.768, s32[40,40]{1,0:T(8,128)S(1)} %copy-done.1, f32[80,1280]{1,0:T(8,128)S(1)} %get-tuple-element.574.square, bf16[5136,1280]{1,0:T(8,128)(2,1)S(1)} %get-tuple-element.575.panel, ...), custom_call_target="tpu_custom_call" | custom-call | flops 1000000000 | tf_op jit(solution)/shard_map/while/body/pallas_call | solution.py:273
  101.2 4.0 %body.67 = (s32[9,512]{1,0:T(8,128)S(1)}, s32[1]{0:T(128)}) custom-call(s32[4]{0:T(128)S(1)} %get-tuple-element.546.pos, s32[40,40]{1,0:T(8,128)} %get-tuple-element.690.pat), custom_call_target="tpu_custom_call" | custom-call | flops 1000000000 | tf_op jit(solution)/shard_map/while/body/pallas_call | solution.py:300
  107.2 5.8 %collective-permute-done.3.refs_3_ = bf16[80,1280]{1,0:T(8,128)(2,1)S(1)} collective-permute-done((bf16[80,1280]{1,0:T(8,128)(2,1)S(1)}, bf16[80,1280]{1,0:T(8,128)(2,1)S(1)}, u32[]{:S(2)}, u32[]{:S(2)}) %collective-permute-start.3) | collective-permute-done | bytes 204832 | tf_op jit(solution)/shard_map/while/body/ppermute | solution.py:256
  117.6 2.7 %collective-permute-start.10 = (bf16[1280,128]{1,0:T(8,128)(2,1)S(1)}, bf16[1280,128]{1,0:T(8,128)(2,1)S(1)}, u32[]{:S(2)}, u32[]{:S(2)}) collective-permute-start(bf16[1280,128]{1,0:T(8,128)(2,1)S(1)} %body.68.refs_0_), channel_id=1, source_target_pairs={{0,7},{1,0},{2,1},{3,2},{4,3},{5,4},{6,5},{7,6},{8,15},{9,8},{10,9... | collective-permute-start | bytes 983048 | tf_op jit(solution)/shard_map/while/body/ppermute | solution.py:260
  120.8 6.2 %collective-permute-done.10.refs_4_ = bf16[1280,128]{1,0:T(8,128)(2,1)S(1)} collective-permute-done((bf16[1280,128]{1,0:T(8,128)(2,1)S(1)}, bf16[1280,128]{1,0:T(8,128)(2,1)S(1)}, u32[]{:S(2)}, u32[]{:S(2)}) %collective-permute-start.10) | collective-permute-done | bytes 327712 | tf_op jit(solution)/shard_map/while/body/ppermute | solution.py:260
  127.0 3.4 %collective-permute-start.11 = (bf16[1280,128]{1,0:T(8,128)(2,1)S(1)}, bf16[1280,128]{1,0:T(8,128)(2,1)S(1)}, u32[]{:S(2)}, u32[]{:S(2)}) collective-permute-start(bf16[1280,128]{1,0:T(8,128)(2,1)S(1)} %collective-permute-done.10.refs_4_), channel_id=1, source_target_pairs={{0,7},{1,0},{2,1},{3,2},{4,3},{5,4},{6,5},{7,6},{8,15},{9,8},{10,9... | collective-permute-start | bytes 983048 | tf_op jit(solution)/shard_map/while/body/ppermute | solution.py:260
  132.0 7.4 %collective-permute-done.14.refs_8_ = bf16[80,1280]{1,0:T(8,128)(2,1)S(1)} collective-permute-done((bf16[80,1280]{1,0:T(8,128)(2,1)S(1)}, bf16[80,1280]{1,0:T(8,128)(2,1)S(1)}, u32[]{:S(2)}, u32[]{:S(2)}) %collective-permute-start.14) | collective-permute-done | bytes 204832 | tf_op jit(solution)/shard_map/while/body/ppermute | solution.py:252
  141.8 2.7 %collective-permute-start.16 = (bf16[1280,128]{1,0:T(8,128)(2,1)S(1)}, bf16[1280,128]{1,0:T(8,128)(2,1)S(1)}, u32[]{:S(2)}, u32[]{:S(2)}) collective-permute-start(bf16[1280,128]{1,0:T(8,128)(2,1)S(1)} %collective-permute-done.11.refs_8_), channel_id=1, source_target_pairs={{0,7},{1,0},{2,1},{3,2},{4,3},{5,4},{6,5},{7,6},{8,15},{9,8},{10,9... | collective-permute-start | bytes 983048 | tf_op jit(solution)/shard_map/while/body/ppermute | solution.py:260
  144.5 6.5 %body.70.refs_4_ = bf16[5136,1280]{1,0:T(8,128)(2,1)S(1)} custom-call(s32[4]{0:T(128)S(1)} %get-tuple-element.768, s32[9,512]{1,0:T(8,128)S(1)} %get-tuple-element.767, bf16[1280,128]{1,0:T(8,128)(2,1)S(1)} %body.68.refs_0_, bf16[1280,128]{1,0:T(8,128)(2,1)S(1)} %collective-permute-done.17.refs_1_, bf16[1280,128]{1,0:T(8,128)(2,1)S(1)} %collective-permute-done.8.refs_2_, ...), custom_call_target="tpu_custom_call" | custom-call | flops 1000000000 | tf_op jit(solution)/shard_map/while/body/pallas_call | solution.py:273
  153.3 2.7 %collective-permute-start.23 = (bf16[640,128]{1,0:T(8,128)(2,1)S(1)}, bf16[640,128]{1,0:T(8,128)(2,1)S(1)}, u32[]{:S(2)}, u32[]{:S(2)}) collective-permute-start(bf16[640,128]{1,0:T(8,128)(2,1)S(1)} %get-tuple-element.564), channel_id=1, source_target_pairs={{0,7},{1,0},{2,1},{3,2},{4,3},{5,4},{6,5},{7,6},{8,15},{9,8},{10,9... | collective-permute-start | bytes 491528 | tf_op jit(solution)/shard_map/while/body/ppermute | solution.py:260
  156.0 2.7 %body.72.refs_4_ = bf16[5136,1280]{1,0:T(8,128)(2,1)S(1)} custom-call(s32[4]{0:T(128)S(1)} %get-tuple-element.768, s32[9,512]{1,0:T(8,128)S(1)} %get-tuple-element.767, bf16[1280,128]{1,0:T(8,128)(2,1)S(1)} %collective-permute-done.15.down.refs_0_, bf16[1280,128]{1,0:T(8,128)(2,1)S(1)} %collective-permute-done.24.refs_1_, ...), custom_call_target="tpu_custom_call", output_to_operand_aliasing={{}: (6, {})} | custom-call | flops 1000000000 | tf_op jit(solution)/shard_map/while/body/pallas_call | solution.py:273
  162.5 5.0 %body.73 = (f32[80,1280]{1,0:T(8,128)S(1)}, bf16[80,1280]{1,0:T(8,128)(2,1)S(1)}, bf16[5136,1280]{1,0:T(8,128)(2,1)S(1)}) custom-call(s32[4]{0:T(128)S(1)} %get-tuple-element.768, s32[40,40]{1,0:T(8,128)S(1)} %copy-done.1, s32[9,512]{1,0:T(8,128)S(1)} %get-tuple-element.767, ...), custom_call_target="tpu_custom_call", output_to_operand_aliasing={{2}: (7, {})} | custom-call | flops 1000000000 | tf_op jit(solution)/shard_map/while/body/pallas_call | solution.py:273
  170.6 7.8 %collective-permute-done.28.refs_1_ = bf16[80,1280]{1,0:T(8,128)(2,1)S(1)} collective-permute-done((bf16[80,1280]{1,0:T(8,128)(2,1)S(1)}, bf16[80,1280]{1,0:T(8,128)(2,1)S(1)}, u32[]{:S(2)}, u32[]{:S(2)}) %collective-permute-start.28) | collective-permute-done | bytes 204832 | tf_op jit(solution)/shard_map/while/body/ppermute | solution.py:252
  178.4 3.9 %collective-permute-done.30.refs_3_ = bf16[80,1280]{1,0:T(8,128)(2,1)S(1)} collective-permute-done((bf16[80,1280]{1,0:T(8,128)(2,1)S(1)}, bf16[80,1280]{1,0:T(8,128)(2,1)S(1)}, u32[]{:S(2)}, u32[]{:S(2)}) %collective-permute-start.30) | collective-permute-done | bytes 204832 | tf_op jit(solution)/shard_map/while/body/ppermute | solution.py:252
  182.3 4.2 %body.74 = (f32[80,1280]{1,0:T(8,128)}, bf16[80,1280]{1,0:T(8,128)(2,1)S(1)}) custom-call(s32[4]{0:T(128)S(1)} %get-tuple-element.768, s32[40,40]{1,0:T(8,128)S(1)} %copy-done.1, f32[80,1280]{1,0:T(8,128)S(1)} %get-tuple-element.574.square, bf16[5136,1280]{1,0:T(8,128)(2,1)S(1)} %get-tuple-element.575.panel, ...), custom_call_target="tpu_custom_call" | custom-call | flops 1000000000 | tf_op jit(solution)/shard_map/while/body/pallas_call | solution.py:273
  (126 shorter events, 42.0 us)
Async XLA Ops:
  4.2 11.9 %collective-permute-start.1 = (bf16[80,1280]{1,0:T(8,128)(2,1)S(1)}, bf16[80,1280]{1,0:T(8,128)(2,1)S(1)}, u32[]{:S(2)}, u32[]{:S(2)}) collective-permute-start(bf16[80,1280]{1,0:T(8,128)(2,1)S(1)} %get-tuple-element.569.refs_0_.refs_5_), channel_id=1, source_target_pairs={{0,192},{32,224},{64,0},{96,32},{128,64},{160,96},{192,128},{224,1... | collective-permute-start | bytes 614408 | tf_op jit(solution)/shard_map/while/body/ppermute | solution.py:256
  7.9 8.3 %collective-permute-start.2 = (bf16[80,1280]{1,0:T(8,128)(2,1)S(1)}, bf16[80,1280]{1,0:T(8,128)(2,1)S(1)}, u32[]{:S(2)}, u32[]{:S(2)}) collective-permute-start(bf16[80,1280]{1,0:T(8,128)(2,1)S(1)} %get-tuple-element.569.refs_0_.refs_5_), channel_id=1, source_target_pairs={{0,128},{32,160},{64,192},{96,224},{128,0},{160,32},{192,64},{224,... | collective-permute-start | bytes 614408 | tf_op jit(solution)/shard_map/while/body/ppermute | solution.py:256
  8.2 12.5 %collective-permute-start.3 = (bf16[80,1280]{1,0:T(8,128)(2,1)S(1)}, bf16[80,1280]{1,0:T(8,128)(2,1)S(1)}, u32[]{:S(2)}, u32[]{:S(2)}) collective-permute-start(bf16[80,1280]{1,0:T(8,128)(2,1)S(1)} %get-tuple-element.569.refs_0_.refs_5_), channel_id=1, source_target_pairs={{0,64},{32,96},{64,128},{96,160},{128,192},{160,224},{192,0},{224,... | collective-permute-start | bytes 614408 | tf_op jit(solution)/shard_map/while/body/ppermute | solution.py:256
  25.4 12.4 %collective-permute-start.10 = (bf16[1280,128]{1,0:T(8,128)(2,1)S(1)}, bf16[1280,128]{1,0:T(8,128)(2,1)S(1)}, u32[]{:S(2)}, u32[]{:S(2)}) collective-permute-start(bf16[1280,128]{1,0:T(8,128)(2,1)S(1)} %body.68.refs_0_), channel_id=1, source_target_pairs={{0,7},{1,0},{2,1},{3,2},{4,3},{5,4},{6,5},{7,6},{8,15},{9,8},{10,9... | collective-permute-start | bytes 983048 | tf_op jit(solution)/shard_map/while/body/ppermute | solution.py:260
  31.1 10.2 %collective-permute-start.8 = (bf16[1280,128]{1,0:T(8,128)(2,1)S(1)}, bf16[1280,128]{1,0:T(8,128)(2,1)S(1)}, u32[]{:S(2)}, u32[]{:S(2)}) collective-permute-start(bf16[1280,128]{1,0:T(8,128)(2,1)S(1)} %body.68.refs_0_), channel_id=1, source_target_pairs={{0,1},{1,2},{2,3},{3,4},{4,5},{5,6},{6,7},{7,0},{8,9},{9,10},{10,1... | collective-permute-start | bytes 983048 | tf_op jit(solution)/shard_map/while/body/ppermute | solution.py:260
  31.1 11.6 %collective-permute-start.12 = (bf16[80,1280]{1,0:T(8,128)(2,1)S(1)}, bf16[80,1280]{1,0:T(8,128)(2,1)S(1)}, u32[]{:S(2)}, u32[]{:S(2)}) collective-permute-start(bf16[80,1280]{1,0:T(8,128)(2,1)S(1)} %get-tuple-element.753), channel_id=1, source_target_pairs={{0,24},{8,0},{16,8},{24,16},{1,25},{9,1},{17,9},{25,17},{2,26},{10... | collective-permute-start | bytes 614408 | tf_op jit(solution)/shard_map/while/body/ppermute | solution.py:252
  33.5 9.7 %collective-permute-start.13 = (bf16[80,1280]{1,0:T(8,128)(2,1)S(1)}, bf16[80,1280]{1,0:T(8,128)(2,1)S(1)}, u32[]{:S(2)}, u32[]{:S(2)}) collective-permute-start(bf16[80,1280]{1,0:T(8,128)(2,1)S(1)} %get-tuple-element.753), channel_id=1, source_target_pairs={{0,16},{8,24},{16,0},{24,8},{1,17},{9,25},{17,1},{25,9},{2,18},{10... | collective-permute-start | bytes 614408 | tf_op jit(solution)/shard_map/while/body/ppermute | solution.py:252
  37.8 14.8 %collective-permute-start.11 = (bf16[1280,128]{1,0:T(8,128)(2,1)S(1)}, bf16[1280,128]{1,0:T(8,128)(2,1)S(1)}, u32[]{:S(2)}, u32[]{:S(2)}) collective-permute-start(bf16[1280,128]{1,0:T(8,128)(2,1)S(1)} %collective-permute-done.10.refs_4_), channel_id=1, source_target_pairs={{0,7},{1,0},{2,1},{3,2},{4,3},{5,4},{6,5},{7,6},{8,15},{9,8},{10,9... | collective-permute-start | bytes 983048 | tf_op jit(solution)/shard_map/while/body/ppermute | solution.py:260
  41.2 11.4 %collective-permute-start.9 = (bf16[1280,128]{1,0:T(8,128)(2,1)S(1)}, bf16[1280,128]{1,0:T(8,128)(2,1)S(1)}, u32[]{:S(2)}, u32[]{:S(2)}) collective-permute-start(bf16[1280,128]{1,0:T(8,128)(2,1)S(1)} %collective-permute-done.8.refs_2_), channel_id=1, source_target_pairs={{0,1},{1,2},{2,3},{3,4},{4,5},{5,6},{6,7},{7,0},{8,9},{9,10},{10,1... | collective-permute-start | bytes 983048 | tf_op jit(solution)/shard_map/while/body/ppermute | solution.py:260
  41.2 11.9 %collective-permute-start.17 = (bf16[1280,128]{1,0:T(8,128)(2,1)S(1)}, bf16[1280,128]{1,0:T(8,128)(2,1)S(1)}, u32[]{:S(2)}, u32[]{:S(2)}) collective-permute-start(bf16[1280,128]{1,0:T(8,128)(2,1)S(1)} %body.68.refs_0_), channel_id=1, source_target_pairs={{0,32},{32,0},{64,96},{96,64},{128,160},{160,128},{192,224},{224,1... | collective-permute-start | bytes 983048 | tf_op jit(solution)/shard_map/while/body/ppermute | solution.py:264
  42.7 10.5 %collective-permute-start.18 = (bf16[1280,128]{1,0:T(8,128)(2,1)S(1)}, bf16[1280,128]{1,0:T(8,128)(2,1)S(1)}, u32[]{:S(2)}, u32[]{:S(2)}) collective-permute-start(bf16[1280,128]{1,0:T(8,128)(2,1)S(1)} %collective-permute-done.8.refs_2_), channel_id=1, source_target_pairs={{0,32},{32,0},{64,96},{96,64},{128,160},{160,128},{192,224},{224,1... | collective-permute-start | bytes 983048 | tf_op jit(solution)/shard_map/while/body/ppermute | solution.py:264
  43.2 8.8 %collective-permute-start.14 = (bf16[80,1280]{1,0:T(8,128)(2,1)S(1)}, bf16[80,1280]{1,0:T(8,128)(2,1)S(1)}, u32[]{:S(2)}, u32[]{:S(2)}) collective-permute-start(bf16[80,1280]{1,0:T(8,128)(2,1)S(1)} %get-tuple-element.753), channel_id=1, source_target_pairs={{0,8},{8,16},{16,24},{24,0},{1,9},{9,17},{17,25},{25,1},{2,10},{10... | collective-permute-start | bytes 614408 | tf_op jit(solution)/shard_map/while/body/ppermute | solution.py:252
  53.2 10.4 %collective-permute-start.15 = (bf16[1280,128]{1,0:T(8,128)(2,1)S(1)}, bf16[1280,128]{1,0:T(8,128)(2,1)S(1)}, u32[]{:S(2)}, u32[]{:S(2)}) collective-permute-start(bf16[1280,128]{1,0:T(8,128)(2,1)S(1)} %collective-permute-done.9.refs_6_), channel_id=1, source_target_pairs={{0,1},{1,2},{2,3},{3,4},{4,5},{5,6},{6,7},{7,0},{8,9},{9,10},{10,1... | collective-permute-start | bytes 983048 | tf_op jit(solution)/shard_map/while/body/ppermute | solution.py:260
  53.2 10.4 %collective-permute-start.16 = (bf16[1280,128]{1,0:T(8,128)(2,1)S(1)}, bf16[1280,128]{1,0:T(8,128)(2,1)S(1)}, u32[]{:S(2)}, u32[]{:S(2)}) collective-permute-start(bf16[1280,128]{1,0:T(8,128)(2,1)S(1)} %collective-permute-done.11.refs_8_), channel_id=1, source_target_pairs={{0,7},{1,0},{2,1},{3,2},{4,3},{5,4},{6,5},{7,6},{8,15},{9,8},{10,9... | collective-permute-start | bytes 983048 | tf_op jit(solution)/shard_map/while/body/ppermute | solution.py:260
  79.0 12.8 %collective-permute-start.28 = (bf16[80,1280]{1,0:T(8,128)(2,1)S(1)}, bf16[80,1280]{1,0:T(8,128)(2,1)S(1)}, u32[]{:S(2)}, u32[]{:S(2)}) collective-permute-start(bf16[80,1280]{1,0:T(8,128)(2,1)S(1)} %get-tuple-element.576.refs_0_), channel_id=1, source_target_pairs={{0,24},{8,0},{16,8},{24,16},{1,25},{9,1},{17,9},{25,17},{2,26},{10... | collective-permute-start | bytes 614408 | tf_op jit(solution)/shard_map/while/body/ppermute | solution.py:252
  83.2 8.6 %collective-permute-start.29 = (bf16[80,1280]{1,0:T(8,128)(2,1)S(1)}, bf16[80,1280]{1,0:T(8,128)(2,1)S(1)}, u32[]{:S(2)}, u32[]{:S(2)}) collective-permute-start(bf16[80,1280]{1,0:T(8,128)(2,1)S(1)} %get-tuple-element.576.refs_0_), channel_id=1, source_target_pairs={{0,16},{8,24},{16,0},{24,8},{1,17},{9,25},{17,1},{25,9},{2,18},{10... | collective-permute-start | bytes 614408 | tf_op jit(solution)/shard_map/while/body/ppermute | solution.py:252
  83.2 12.3 %collective-permute-start.30 = (bf16[80,1280]{1,0:T(8,128)(2,1)S(1)}, bf16[80,1280]{1,0:T(8,128)(2,1)S(1)}, u32[]{:S(2)}, u32[]{:S(2)}) collective-permute-start(bf16[80,1280]{1,0:T(8,128)(2,1)S(1)} %get-tuple-element.576.refs_0_), channel_id=1, source_target_pairs={{0,8},{8,16},{16,24},{24,0},{1,9},{9,17},{17,25},{25,1},{2,10},{10... | collective-permute-start | bytes 614408 | tf_op jit(solution)/shard_map/while/body/ppermute | solution.py:252
  100.4 12.5 %collective-permute-start.3 = (bf16[80,1280]{1,0:T(8,128)(2,1)S(1)}, bf16[80,1280]{1,0:T(8,128)(2,1)S(1)}, u32[]{:S(2)}, u32[]{:S(2)}) collective-permute-start(bf16[80,1280]{1,0:T(8,128)(2,1)S(1)} %get-tuple-element.569.refs_0_.refs_5_), channel_id=1, source_target_pairs={{0,64},{32,96},{64,128},{96,160},{128,192},{160,224},{192,0},{224,... | collective-permute-start | bytes 614408 | tf_op jit(solution)/shard_map/while/body/ppermute | solution.py:256
  117.6 9.4 %collective-permute-start.10 = (bf16[1280,128]{1,0:T(8,128)(2,1)S(1)}, bf16[1280,128]{1,0:T(8,128)(2,1)S(1)}, u32[]{:S(2)}, u32[]{:S(2)}) collective-permute-start(bf16[1280,128]{1,0:T(8,128)(2,1)S(1)} %body.68.refs_0_), channel_id=1, source_target_pairs={{0,7},{1,0},{2,1},{3,2},{4,3},{5,4},{6,5},{7,6},{8,15},{9,8},{10,9... | collective-permute-start | bytes 983048 | tf_op jit(solution)/shard_map/while/body/ppermute | solution.py:260
  120.2 10.2 %collective-permute-start.8 = (bf16[1280,128]{1,0:T(8,128)(2,1)S(1)}, bf16[1280,128]{1,0:T(8,128)(2,1)S(1)}, u32[]{:S(2)}, u32[]{:S(2)}) collective-permute-start(bf16[1280,128]{1,0:T(8,128)(2,1)S(1)} %body.68.refs_0_), channel_id=1, source_target_pairs={{0,1},{1,2},{2,3},{3,4},{4,5},{5,6},{6,7},{7,0},{8,9},{9,10},{10,1... | collective-permute-start | bytes 983048 | tf_op jit(solution)/shard_map/while/body/ppermute | solution.py:260
  120.2 11.6 %collective-permute-start.12 = (bf16[80,1280]{1,0:T(8,128)(2,1)S(1)}, bf16[80,1280]{1,0:T(8,128)(2,1)S(1)}, u32[]{:S(2)}, u32[]{:S(2)}) collective-permute-start(bf16[80,1280]{1,0:T(8,128)(2,1)S(1)} %get-tuple-element.753), channel_id=1, source_target_pairs={{0,24},{8,0},{16,8},{24,16},{1,25},{9,1},{17,9},{25,17},{2,26},{10... | collective-permute-start | bytes 614408 | tf_op jit(solution)/shard_map/while/body/ppermute | solution.py:252
  120.3 11.7 %collective-permute-start.13 = (bf16[80,1280]{1,0:T(8,128)(2,1)S(1)}, bf16[80,1280]{1,0:T(8,128)(2,1)S(1)}, u32[]{:S(2)}, u32[]{:S(2)}) collective-permute-start(bf16[80,1280]{1,0:T(8,128)(2,1)S(1)} %get-tuple-element.753), channel_id=1, source_target_pairs={{0,16},{8,24},{16,0},{24,8},{1,17},{9,25},{17,1},{25,9},{2,18},{10... | collective-permute-start | bytes 614408 | tf_op jit(solution)/shard_map/while/body/ppermute | solution.py:252
  127.0 13.7 %collective-permute-start.11 = (bf16[1280,128]{1,0:T(8,128)(2,1)S(1)}, bf16[1280,128]{1,0:T(8,128)(2,1)S(1)}, u32[]{:S(2)}, u32[]{:S(2)}) collective-permute-start(bf16[1280,128]{1,0:T(8,128)(2,1)S(1)} %collective-permute-done.10.refs_4_), channel_id=1, source_target_pairs={{0,7},{1,0},{2,1},{3,2},{4,3},{5,4},{6,5},{7,6},{8,15},{9,8},{10,9... | collective-permute-start | bytes 983048 | tf_op jit(solution)/shard_map/while/body/ppermute | solution.py:260
  130.4 10.3 %collective-permute-start.9 = (bf16[1280,128]{1,0:T(8,128)(2,1)S(1)}, bf16[1280,128]{1,0:T(8,128)(2,1)S(1)}, u32[]{:S(2)}, u32[]{:S(2)}) collective-permute-start(bf16[1280,128]{1,0:T(8,128)(2,1)S(1)} %collective-permute-done.8.refs_2_), channel_id=1, source_target_pairs={{0,1},{1,2},{2,3},{3,4},{4,5},{5,6},{6,7},{7,0},{8,9},{9,10},{10,1... | collective-permute-start | bytes 983048 | tf_op jit(solution)/shard_map/while/body/ppermute | solution.py:260
  130.4 11.3 %collective-permute-start.17 = (bf16[1280,128]{1,0:T(8,128)(2,1)S(1)}, bf16[1280,128]{1,0:T(8,128)(2,1)S(1)}, u32[]{:S(2)}, u32[]{:S(2)}) collective-permute-start(bf16[1280,128]{1,0:T(8,128)(2,1)S(1)} %body.68.refs_0_), channel_id=1, source_target_pairs={{0,32},{32,0},{64,96},{96,64},{128,160},{160,128},{192,224},{224,1... | collective-permute-start | bytes 983048 | tf_op jit(solution)/shard_map/while/body/ppermute | solution.py:264
  131.9 9.9 %collective-permute-start.18 = (bf16[1280,128]{1,0:T(8,128)(2,1)S(1)}, bf16[1280,128]{1,0:T(8,128)(2,1)S(1)}, u32[]{:S(2)}, u32[]{:S(2)}) collective-permute-start(bf16[1280,128]{1,0:T(8,128)(2,1)S(1)} %collective-permute-done.8.refs_2_), channel_id=1, source_target_pairs={{0,32},{32,0},{64,96},{96,64},{128,160},{160,128},{192,224},{224,1... | collective-permute-start | bytes 983048 | tf_op jit(solution)/shard_map/while/body/ppermute | solution.py:264
  132.0 7.4 %collective-permute-start.14 = (bf16[80,1280]{1,0:T(8,128)(2,1)S(1)}, bf16[80,1280]{1,0:T(8,128)(2,1)S(1)}, u32[]{:S(2)}, u32[]{:S(2)}) collective-permute-start(bf16[80,1280]{1,0:T(8,128)(2,1)S(1)} %get-tuple-element.753), channel_id=1, source_target_pairs={{0,8},{8,16},{16,24},{24,0},{1,9},{9,17},{17,25},{25,1},{2,10},{10... | collective-permute-start | bytes 614408 | tf_op jit(solution)/shard_map/while/body/ppermute | solution.py:252
  141.8 10.0 %collective-permute-start.15 = (bf16[1280,128]{1,0:T(8,128)(2,1)S(1)}, bf16[1280,128]{1,0:T(8,128)(2,1)S(1)}, u32[]{:S(2)}, u32[]{:S(2)}) collective-permute-start(bf16[1280,128]{1,0:T(8,128)(2,1)S(1)} %collective-permute-done.9.refs_6_), channel_id=1, source_target_pairs={{0,1},{1,2},{2,3},{3,4},{4,5},{5,6},{6,7},{7,0},{8,9},{9,10},{10,1... | collective-permute-start | bytes 983048 | tf_op jit(solution)/shard_map/while/body/ppermute | solution.py:260
  141.8 10.0 %collective-permute-start.16 = (bf16[1280,128]{1,0:T(8,128)(2,1)S(1)}, bf16[1280,128]{1,0:T(8,128)(2,1)S(1)}, u32[]{:S(2)}, u32[]{:S(2)}) collective-permute-start(bf16[1280,128]{1,0:T(8,128)(2,1)S(1)} %collective-permute-done.11.refs_8_), channel_id=1, source_target_pairs={{0,7},{1,0},{2,1},{3,2},{4,3},{5,4},{6,5},{7,6},{8,15},{9,8},{10,9... | collective-permute-start | bytes 983048 | tf_op jit(solution)/shard_map/while/body/ppermute | solution.py:260
  167.5 10.9 %collective-permute-start.28 = (bf16[80,1280]{1,0:T(8,128)(2,1)S(1)}, bf16[80,1280]{1,0:T(8,128)(2,1)S(1)}, u32[]{:S(2)}, u32[]{:S(2)}) collective-permute-start(bf16[80,1280]{1,0:T(8,128)(2,1)S(1)} %get-tuple-element.576.refs_0_), channel_id=1, source_target_pairs={{0,24},{8,0},{16,8},{24,16},{1,25},{9,1},{17,9},{25,17},{2,26},{10... | collective-permute-start | bytes 614408 | tf_op jit(solution)/shard_map/while/body/ppermute | solution.py:252
  170.0 8.4 %collective-permute-start.29 = (bf16[80,1280]{1,0:T(8,128)(2,1)S(1)}, bf16[80,1280]{1,0:T(8,128)(2,1)S(1)}, u32[]{:S(2)}, u32[]{:S(2)}) collective-permute-start(bf16[80,1280]{1,0:T(8,128)(2,1)S(1)} %get-tuple-element.576.refs_0_), channel_id=1, source_target_pairs={{0,16},{8,24},{16,0},{24,8},{1,17},{9,25},{17,1},{25,9},{2,18},{10... | collective-permute-start | bytes 614408 | tf_op jit(solution)/shard_map/while/body/ppermute | solution.py:252
  170.0 12.3 %collective-permute-start.30 = (bf16[80,1280]{1,0:T(8,128)(2,1)S(1)}, bf16[80,1280]{1,0:T(8,128)(2,1)S(1)}, u32[]{:S(2)}, u32[]{:S(2)}) collective-permute-start(bf16[80,1280]{1,0:T(8,128)(2,1)S(1)} %get-tuple-element.576.refs_0_), channel_id=1, source_target_pairs={{0,8},{8,16},{16,24},{24,0},{1,9},{9,17},{17,25},{25,1},{2,10},{10... | collective-permute-start | bytes 614408 | tf_op jit(solution)/shard_map/while/body/ppermute | solution.py:252
  (35 other events, 151.7 us)
